TPU v7x, 256 devices: a whole 4x4x8 slice. The times are simulated.
256 devices in a mesh: lat: 2 (over x_hi), lon: 2 (over x_lo), lev: 64 (over z, y, core).
Axes of the slice: x: 4 (x_hi: 2, x_lo: 2; x = x_hi * 2 + x_lo), y: 4, z: 8, core: 2. Of those that a mesh axis runs over, the one named last changes fastest.
Arguments:
- along_axis_flow: bfloat16 [640, 4, 32, 1440], P(('lat', 'lev'), None, None, 'lon'), may hold values from -6 to 6
- poleward_flow: bfloat16 [640, 4, 32, 1440], P(('lat', 'lev'), None, None, 'lon'), may hold values from -6 to 6
- warmth_departure: bfloat16 [640, 4, 32, 1440], P(('lat', 'lev'), None, None, 'lon'), may hold values from -6 to 6
- validity_indicator: int32 [640, 32, 1440], P(('lat', 'lev'), None, 'lon'), may hold values from 0 to 1
- layer_depth_span: float32 [32], replicated, may hold values from 0.3 to 3
- desired_circulation_norm: float32 [640, 4, 32], P(('lat', 'lev')), may hold values from -4 to 4
Outputs:
- psi_norm: float32 [640, 4, 32], P(('lat', 'lev'))
- heat_cospec: float32 [720, 640, 128], P('lon', ('lat', 'lev'))
- momentum_cospec: float32 [720, 640, 128], P('lon', ('lat', 'lev'))
- budget_penalty: float32 [], replicated
All inputs are finite; a program needn't handle non-finite values. Where the computation divides by a largest or mean magnitude, that divisor is 1e-20 or more.
Results may differ from a plain program's by a relative error of at most 0.0033.
Values may be sent and summed in bfloat16 or wider, within the bound.
No kernel may reach another device: no remote copies, remote signals or barrier semaphores. Data moves between devices by JAX's collectives and lax.ppermute only.
A program may use at most 64 MiB of HBM per device.

v0:
```python
import functools
import math

import jax
import jax.numpy as jnp
from jax import lax
from jax.sharding import Mesh
from jax.sharding import PartitionSpec as P

GRID_MERIDIANS = 1440
HARMONIC_ORDERS = 720
LAT_LEV = ("lat", "lev_0", "lev_1", "lev_2")


epsilon = 1e-06


def from_everyone(array, axis):
    copies = jnp.broadcast_to(array, (lax.axis_size(axis), *array.shape))
    return lax.all_to_all(copies, axis, split_axis=0, concat_axis=0, tiled=True)


def over_copies(array, axis):
    everything = from_everyone(array, axis)
    return jnp.sum(everything, axis=0)


def in_one(arrays, axis):
    flat, at, outs = (jnp.concatenate([a.reshape(-1) for a in arrays]), 0, [])
    so_far = over_copies(flat, axis)
    for a in arrays:
        outs.append(so_far[at : at + a.size].reshape(a.shape))
        at += a.size
    return tuple(outs)


def nothing_yet(array, identity):
    return jnp.broadcast_to(jnp.asarray(identity, array.dtype), array.shape)


def prefix_by_axis(array, axes, combine, identity):
    before = start = nothing_yet(array, identity)
    so_far = array
    for axis in reversed(axes):
        length, place = (lax.axis_size(axis), lax.axis_index(axis))
        pieces = lax.all_gather(so_far, axis)
        inside, so_far = (start, start)
        for k in range(length):
            passed = k < place
            so_far = combine(so_far, pieces[k])
            inside = jnp.where(passed, so_far, inside)
        before = combine(inside, before)
    return before


def one_axis_at_a_time(array, axes):
    return functools.reduce(lax.pmax, axes, array)


def over_axes(array, axes):
    for axis in axes:
        array = lax.psum(array, axis)
    return array


def build_waves(wave_rows, lon_index):
    wavenumber = wave_rows // 2 + 1
    component = wave_rows % 2
    turns = wavenumber[:, None] * lon_index[None, :] % GRID_MERIDIANS
    angle = turns.astype(jnp.float32) * (2.0 * math.pi / GRID_MERIDIANS)
    return jnp.where(component[:, None] == 0, jnp.cos(angle), jnp.sin(angle)).astype(jnp.bfloat16)


def add_arrays(earlier, later):
    return earlier + later


def cospectra(fourier_weights, norm_factor):
    heat_part = norm_factor * (
        fourier_weights[:, 0, 1] * fourier_weights[:, 0, 2]
        + fourier_weights[:, 1, 1] * fourier_weights[:, 1, 2]
    )
    moment_part = norm_factor * (
        fourier_weights[:, 0, 0] * fourier_weights[:, 0, 1]
        + fourier_weights[:, 1, 0] * fourier_weights[:, 1, 1]
    )
    return (heat_part, moment_part)


def per_device(
    along_axis_flow,
    poleward_flow,
    warmth_departure,
    validity_indicator,
    layer_depth_span,
    desired_circulation_norm,
):
    bands, batch, level_values, lon_count = poleward_flow.shape
    lon_ways = lax.axis_size("lon")
    retained_indicator = validity_indicator.astype(jnp.bfloat16)[:, None]
    screened_eastward_speed = along_axis_flow * retained_indicator
    screened_northward_speed = poleward_flow * retained_indicator
    screened_thermal_anomaly = warmth_departure * retained_indicator
    zonal_v = jnp.sum(screened_northward_speed, axis=3, dtype=jnp.float32)
    kept_count = jnp.sum(validity_indicator, axis=2).astype(jnp.float32)
    zonal_v, kept_count = in_one((zonal_v, kept_count), "lon")
    mean_v = zonal_v / jnp.maximum(kept_count, 1.0)[:, None, :]
    columns = batch * level_values
    joined_arrays = jnp.stack(
        [screened_eastward_speed, screened_northward_speed, screened_thermal_anomaly]
    ).reshape(3, bands, columns, lon_count)
    norm_factor = 2.0 / (GRID_MERIDIANS * GRID_MERIDIANS)
    wave_local = HARMONIC_ORDERS // lon_ways
    own_rows = lax.axis_index("lon") * (2 * wave_local) + jnp.arange(
        2 * wave_local, dtype=jnp.int32
    )
    waves_table = build_waves(own_rows, jnp.arange(GRID_MERIDIANS, dtype=jnp.int32))
    fourier_weights = lax.dot_general(
        waves_table,
        lax.all_gather(joined_arrays, "lon", axis=3, tiled=True),
        (((1,), (3,)), ((), ())),
        preferred_element_type=jnp.float32,
    )
    fourier_weights = fourier_weights.reshape(wave_local, 2, 3, bands, columns)
    heat_cospec, momentum_cospec = cospectra(fourier_weights, norm_factor)
    nlat = bands * lax.axis_size(LAT_LEV)
    band_index = lax.axis_index(LAT_LEV) * bands + jnp.arange(bands, dtype=jnp.int32)
    latitude = ((band_index.astype(jnp.float32) + 0.5) / nlat - 0.5) * math.pi
    cosine = jnp.cos(latitude)
    weighted = mean_v * cosine[:, None, None] * layer_depth_span[None, None, :]
    upward = jnp.cumsum(weighted, axis=2)
    southward = jnp.cumsum(upward, axis=0)
    band_sums = southward[-1]
    southern = prefix_by_axis(
        band_sums, LAT_LEV, add_arrays, jnp.zeros((batch, level_values), jnp.float32)
    )
    stream = southward + southern[None]
    local_peak = jnp.max(jnp.abs(stream))
    cell_count = batch * level_values * nlat
    weight_lat = cosine[:, None, None]
    peak_value = one_axis_at_a_time(local_peak, LAT_LEV)
    psi_norm = stream / (peak_value + epsilon)
    local_misfit = jnp.sum(weight_lat * (psi_norm - desired_circulation_norm) ** 2)
    budget_penalty = over_axes(local_misfit, LAT_LEV) / cell_count
    return (psi_norm, heat_cospec, momentum_cospec, budget_penalty)


def solution(mesh):
    torus = Mesh(
        mesh.devices.reshape(mesh.shape["lat"], mesh.shape["lon"], 8, 4, 2),
        ("lat", "lon", "lev_0", "lev_1", "lev_2"),
    )
    in_specs = (
        P(LAT_LEV, None, None, "lon"),
        P(LAT_LEV, None, None, "lon"),
        P(LAT_LEV, None, None, "lon"),
        P(LAT_LEV, None, "lon"),
        P(),
        P(LAT_LEV, None, None),
    )
    out_specs = (P(LAT_LEV, None, None), P("lon", LAT_LEV, None), P("lon", LAT_LEV, None), P())
    return jax.shard_map(
        per_device, mesh=torus, in_specs=in_specs, out_specs=out_specs, check_vma=False
    )
```

profile of v0, /device:TPU:1, one launch (start us, length us, event | category | flops | bytes accessed | tf_op | source)
XLA Modules:
  0.0 185.7 jit_solution(17721754598539388875)
XLA Ops:
  7.2 1.4 fusion.27
  8.6 1.5 convert_reduce_fusion
  11.0 1.6 broadcast_multiply_fusion.1
  12.6 1.3 copy.47
  14.8 3.0 %pad_maximum_fusion = bf16[3,5,128,720]{2,3,1,0:T(8,128)(2,1)} fusion(bf16[1,5,128,720]{2,3,1,0:T(8,128)(2,1)S(1)} %copy.49, bf16[1,5,128,720]{2,3,1,0:T(8,128)(2,1)S(1)} %copy.48, bf16[1,5,128,720]{2,3,1,0:T(8,128)(2,1)} %copy.47), kind=kLoop, calls=%fused_computation.8 | loop fusion | flops 2764800 | bytes 5529600 | tf_op jit(solution)/shard_map/stack | solution.py:109
  18.6 3.3 %all-to-all-start = ((f32[2,1,800]{2,1,0:T(1,128)}), f32[2,1,800]{2,1,0:T(1,128)S(1)}, u32[]{:S(2)}, u32[]{:S(2)}) async-start(f32[2,1,800]{2,1,0:T(1,128)} %broadcast_in_dim.9), calls=%async_computation | async-start | bytes 14336 | tf_op jit(solution)/shard_map/all_to_all | solution.py:20
  22.0 3.1 %all-to-all-done = f32[2,1,800]{2,1,0:T(1,128)S(1)} async-done(((f32[2,1,800]{2,1,0:T(1,128)}), f32[2,1,800]{2,1,0:T(1,128)S(1)}, u32[]{:S(2)}, u32[]{:S(2)}) %all-to-all-start) | async-done | bytes 6432 | tf_op jit(solution)/shard_map/all_to_all | solution.py:20
  25.3 1.0 reduce_window_sum.22
  26.3 5.3 %all_gather.18 = f32[2,4,32]{2,1,0:T(4,128)S(1)} all-gather(f32[1,4,32]{2,1,0:T(4,128)S(1)} %slice.110), channel_id=1, replica_groups=mesh['lat'=2,'lon'=2,'lev_0'=8,'lev_1'=4,'lev_2'=2] {'lev_2'}, dimensions={0}, use_global_device_ids=true | all-gather | bytes 1536 | tf_op jit(solution)/shard_map/all_gather | solution.py:46
  31.6 8.1 %all_gather.19 = f32[4,4,32]{2,1,0:T(4,128)S(1)} all-gather(f32[1,4,32]{2,1,0:T(4,128)S(1)} %slice_add_fusion.11), channel_id=1, replica_groups=mesh['lat'=2,'lon'=2,'lev_0'=8,'lev_1'=4,'lev_2'=2] {'lev_1'}, dimensions={0}, use_global_device_ids=true | all-gather | bytes 2560 | tf_op jit(solution)/shard_map/all_gather | solution.py:46
  39.7 20.2 %all_gather.20 = f32[8,4,32]{2,1,0:T(4,128)S(1)} all-gather(f32[1,4,32]{2,1,0:T(4,128)S(1)} %slice_add_fusion.8), channel_id=1, replica_groups=mesh['lat'=2,'lon'=2,'lev_0'=8,'lev_1'=4,'lev_2'=2] {'lev_0'}, dimensions={0}, use_global_device_ids=true | all-gather | bytes 4608 | tf_op jit(solution)/shard_map/all_gather | solution.py:46
  59.9 4.9 %all_gather.21 = f32[2,4,32]{2,1,0:T(4,128)S(1)} all-gather(f32[1,4,32]{2,1,0:T(4,128)S(1)} %get-tuple-element.6), channel_id=1, replica_groups=mesh['lat'=2,'lon'=2,'lev_0'=8,'lev_1'=4,'lev_2'=2] {'lat'}, dimensions={0}, use_global_device_ids=true | all-gather | bytes 1536 | tf_op jit(solution)/shard_map/all_gather | solution.py:46
  65.5 6.1 %pmax.28 = f32[]{:T(128)} all-reduce(f32[]{:T(128)} %abs_reduce_fusion), channel_id=1, replica_groups=mesh['lat'=2,'lon'=2,'lev_0'=8,'lev_1'=4,'lev_2'=2] {'lat'}, use_global_device_ids=true, to_apply=%region_6.7 | all-reduce | flops 1 | bytes 8 | tf_op jit(solution)/shard_map/pmax | solution.py:57
  71.6 12.4 %pmax.29 = f32[]{:T(128)} all-reduce(f32[]{:T(128)} %pmax.28), channel_id=1, replica_groups=mesh['lat'=2,'lon'=2,'lev_0'=8,'lev_1'=4,'lev_2'=2] {'lev_0'}, use_global_device_ids=true, to_apply=%region_7.8 | all-reduce | flops 1 | bytes 8 | tf_op jit(solution)/shard_map/pmax | solution.py:57
  83.9 8.3 %pmax.30 = f32[]{:T(128)} all-reduce(f32[]{:T(128)} %pmax.29), channel_id=1, replica_groups=mesh['lat'=2,'lon'=2,'lev_0'=8,'lev_1'=4,'lev_2'=2] {'lev_1'}, use_global_device_ids=true, to_apply=%region_8.9 | all-reduce | flops 1 | bytes 8 | tf_op jit(solution)/shard_map/pmax | solution.py:57
  92.2 17.9 %pmax.31 = f32[]{:T(128)} all-reduce(f32[]{:T(128)} %pmax.30), channel_id=1, replica_groups=mesh['lat'=2,'lon'=2,'lev_0'=8,'lev_1'=4,'lev_2'=2] {'lev_2'}, use_global_device_ids=true, to_apply=%region_9.10 | all-reduce | flops 1 | bytes 8 | tf_op jit(solution)/shard_map/pmax | solution.py:57
  110.7 1.2 multiply_reduce_fusion
  111.9 5.9 %psum.28 = f32[]{:T(128)} all-reduce(f32[]{:T(128)} %get-tuple-element.4), channel_id=1, replica_groups=mesh['lat'=2,'lon'=2,'lev_0'=8,'lev_1'=4,'lev_2'=2] {'lat'}, use_global_device_ids=true, to_apply=%region_11.12 | all-reduce | flops 1 | bytes 8 | tf_op jit(solution)/shard_map/psum | solution.py:62
  117.8 11.7 %psum.29 = f32[]{:T(128)} all-reduce(f32[]{:T(128)} %psum.28), channel_id=1, replica_groups=mesh['lat'=2,'lon'=2,'lev_0'=8,'lev_1'=4,'lev_2'=2] {'lev_0'}, use_global_device_ids=true, to_apply=%region_12.13 | all-reduce | flops 1 | bytes 8 | tf_op jit(solution)/shard_map/psum | solution.py:62
  129.6 6.6 %psum.30 = f32[]{:T(128)} all-reduce(f32[]{:T(128)} %psum.29), channel_id=1, replica_groups=mesh['lat'=2,'lon'=2,'lev_0'=8,'lev_1'=4,'lev_2'=2] {'lev_1'}, use_global_device_ids=true, to_apply=%region_13.14 | all-reduce | flops 1 | bytes 8 | tf_op jit(solution)/shard_map/psum | solution.py:62
  136.2 10.1 %psum.31 = f32[]{:T(128)} all-reduce(f32[]{:T(128)} %psum.30), channel_id=1, replica_groups=mesh['lat'=2,'lon'=2,'lev_0'=8,'lev_1'=4,'lev_2'=2] {'lev_2'}, use_global_device_ids=true, to_apply=%region_14.15 | all-reduce | flops 1 | bytes 8 | tf_op jit(solution)/shard_map/psum | solution.py:62
  147.0 25.1 %fusion.6 = f32[720,3,5,128]{3,0,2,1:T(8,128)S(1)} fusion(bf16[3,5,128,1440]{2,3,1,0:T(8,128)(2,1)} %all-gather.2.cloned.1.call-done, s32[720]{0:T(1024)S(1)} %fusion.14, pred[720]{0:T(1024)(128)(4,1)S(1)} %fusion.13), kind=kOutput, calls=%fused_computation.10 | convolution fusion | flops 3992716800 | bytes 11062800 | tf_op jit(solution)/shard_map/dot_general | solution.py:118
  172.1 3.9 %fusion.26 = (f32[360,1,1,5,128]{4,1,0,3,2:T(1,128)S(1)}, f32[360,1,1,5,128]{4,1,0,3,2:T(1,128)S(1)}, f32[360,1,1,5,128]{4,1,0,3,2:T(1,128)S(1)}, f32[360,1,1,5,...) fusion(f32[360,2,3,5,128]{4,1,0,3,2:T(2,128)S(1)} %bitcast.27), kind=kLoop, calls=%fused_computation.61 | loop fusion | bytes 11059200 | tf_op jit(solution)/shard_map/slice | solution.py:84
  176.0 1.7 multiply_bitcast_fusion
  (29 shorter events, 3.4 us)
Async XLA Ops:
  7.2 139.8 %all-gather.2.cloned.1.call-start = ((), (), s32[]{:S(2)}) async-start(), calls=%async_computation.1 | async-start | bytes 8294400 | tf_op jit(solution)/shard_map/all_gather | solution.py:120
  14.7 10.5 %copy-start.1 = (f32[32]{0:T(128)S(1)}, f32[32]{0:T(128)}, u32[]{:S(2)}) copy-start(f32[32]{0:T(128)} %param.10) | copy-start | bytes 388
  14.8 96.0 %copy-start = (f32[5,4,32]{2,1,0:T(4,128)S(1)}, f32[5,4,32]{2,1,0:T(4,128)}, u32[]{:S(2)}) copy-start(f32[5,4,32]{2,1,0:T(4,128)} %param.11) | copy-start | bytes 7684
  18.6 6.4 %all-to-all-start = ((f32[2,1,800]{2,1,0:T(1,128)}), f32[2,1,800]{2,1,0:T(1,128)S(1)}, u32[]{:S(2)}, u32[]{:S(2)}) async-start(f32[2,1,800]{2,1,0:T(1,128)} %broadcast_in_dim.9), calls=%async_computation | async-start | bytes 14336 | tf_op jit(solution)/shard_map/all_to_all | solution.py:20
Sparse Core Ops, SparseCore 0:
  17.9 80.5 all-gather.1
where the time goes:
time: 186 us
  blocking collectives  117 us (63%)
  matrix products  25.1 us (13%)
  between operations  16.6 us (9%)
  other arithmetic  12.4 us (7%)
  local copies, waits for them, and re-layouts  7.7 us (4%)
  starting transfers between devices  3.33 us (2%)
  waiting for transfers between devices  3.1 us (2%)
    pmax x4, blocking collectives, one_axis_at_a_time(): return functools.reduce(lax.pmax, axes, array)  44.6 us
    all_gather x4, blocking collectives, prefix_by_axis(): pieces = lax.all_gather(so_far, axis)  38.5 us
    psum x4, blocking collectives, over_axes(): array = lax.psum(array, axis)  34.3 us
    dot_general x1, matrix products, per_device(): lax.dot_general(waves_table, lax.all_gather(joined_arrays, 'lon', axis=3,...  25.1 us
    slice x1, local copies, waits for them, and re-layouts, cospectra(): fourier_weights[:, 0, 0] * fourier_weights[:, 0, 1]  3.85 us
  transfers between devices with their start and end apart: 2, of which 1 were waited for; matrix products, arithmetic and copies ran while one was open for 2% of the time, Pallas kernels for 0%

commit v1 on v0

v1 whole, which is shorter than its diff:
```python
import math

import jax
import jax.numpy as jnp
import numpy as np
from jax import lax
from jax.experimental import pallas as pl
from jax.experimental.pallas import tpu as pltpu
from jax.sharding import Mesh
from jax.sharding import PartitionSpec as P

MERIDIANS = 1440
ORDERS = 720
LAT_LEV = ("lat", "lev_0", "lev_1", "lev_2")
EPSILON = 1e-06
GROUPS = ((0,), (1, 2), (3, 4))
F32 = jnp.float32
BF16 = jnp.bfloat16
VMEM_LIMIT = 40 * 1024 * 1024


def half_table(lon):
    order = np.arange(1, ORDERS + 1, dtype=np.int64)
    turns = (order[:, None] * np.arange(lon, dtype=np.int64)[None, :]) % MERIDIANS
    angle = turns.astype(np.float32) * np.float32(2.0 * math.pi / MERIDIANS)
    both = np.stack([np.cos(angle), np.sin(angle)]).reshape(2, 2, ORDERS // 2, lon)
    return np.ascontiguousarray(both.transpose(1, 0, 2, 3)).reshape(2, ORDERS, lon)


def params(**kw):
    return pltpu.CompilerParams(vmem_limit_bytes=VMEM_LIMIT, **kw)


def masked(field_ref, keep):
    return (field_ref[0] * keep[None]).reshape(-1, keep.shape[-1])


def pack_kernel(half_ref, u_ref, v_ref, t_ref, m_ref, o_ref):
    keep = m_ref[0].astype(F32).astype(BF16)
    o_ref[0] = jnp.concatenate([masked(t_ref, keep), masked(u_ref, keep), masked(v_ref, keep)])


def pack(half, u, v, t, mask, rows):
    _, samples, levels, lon = u.shape
    part = samples // 2
    first = rows[0]
    field = pl.BlockSpec((1, part, levels, lon), lambda i, s: (i + first, s[0], 0, 0))
    return pl.pallas_call(
        pack_kernel,
        out_shape=jax.ShapeDtypeStruct((len(rows), 3 * part * levels, lon), BF16),
        grid_spec=pltpu.PrefetchScalarGridSpec(
            num_scalar_prefetch=1,
            grid=(len(rows),),
            in_specs=[
                field,
                field,
                field,
                pl.BlockSpec((1, levels, lon), lambda i, s: (i + first, 0, 0)),
            ],
            out_specs=pl.BlockSpec((1, 3 * part * levels, lon), lambda i, s: (i, 0, 0)),
        ),
        compiler_params=params(),
        name="pack",
    )(half, u, v, t, mask)


CONTRACT = (((1,), (1,)), ((), ()))


def zonal_kernel(v_ref, m_ref, d_ref, o_ref):
    rows, samples, levels, lon = v_ref.shape
    ones = jnp.ones((8, lon), BF16)
    for j in range(rows):
        keep = m_ref[j].astype(F32).astype(BF16)
        v = (v_ref[j] * keep[None]).reshape(samples * levels, lon)
        o_ref[j : j + 1, :] = lax.dot_general(ones, v, CONTRACT, preferred_element_type=F32)[0:1]
        full = jnp.broadcast_to(keep[None], (samples, levels, lon)).reshape(samples * levels, lon)
        o_ref[rows + j : rows + j + 1, :] = lax.dot_general(
            ones, full, CONTRACT, preferred_element_type=F32
        )[0:1]
    o_ref[2 * rows : 3 * rows, :] = d_ref[...]
    o_ref[3 * rows :, :] = jnp.zeros((1, o_ref.shape[1]), F32)


def zonal(v, mask, desired):
    rows, samples, levels, _ = v.shape
    return pl.pallas_call(
        zonal_kernel,
        out_shape=jax.ShapeDtypeStruct((3 * rows + 1, samples * levels), F32),
        compiler_params=params(),
        name="zonal",
    )(v, mask, desired)


def wave_kernel(half_ref, table_ref, own_ref, got_ref, o_ref):
    def lay(ref):
        x = ref[0]
        return jnp.concatenate([x, x[2 * x.shape[0] // 3 :]])

    table = table_ref[0]
    near = lax.dot_general(table, lay(own_ref), CONTRACT, preferred_element_type=F32)
    far = lax.dot_general(table, lay(got_ref), CONTRACT, preferred_element_type=F32)
    n = near.shape[0] // 2
    odd = lax.broadcasted_iota(jnp.int32, (n, 1), 0) % 2 == 0
    sign = jnp.where(odd, -1.0, 1.0).astype(F32)
    cos = near[:n] + sign * far[:n]
    sin = near[n:] + sign * far[n:]
    w = cos.shape[1] // 2
    scale = 2.0 / (MERIDIANS * MERIDIANS)
    o_ref[0] = (scale * (cos[:, :w] * cos[:, w:] + sin[:, :w] * sin[:, w:])).astype(o_ref.dtype)


def waves(half, table, own, got, dtype):
    rows, cols, lon = own.shape
    n = table.shape[1] // 2
    unit = pl.BlockSpec((1, cols, lon), lambda i, s: (i, 0, 0))
    return pl.pallas_call(
        wave_kernel,
        out_shape=jax.ShapeDtypeStruct((rows, n, 2 * cols // 3), dtype),
        grid_spec=pltpu.PrefetchScalarGridSpec(
            num_scalar_prefetch=1,
            grid=(rows,),
            in_specs=[pl.BlockSpec((1, 2 * n, lon), lambda i, s: (s[0], 0, 0)), unit, unit],
            out_specs=pl.BlockSpec((1, n, 2 * cols // 3), lambda i, s: (i, 0, 0)),
        ),
        compiler_params=params(),
        name="waves",
    )(half, table, own, got)


def join_kernel(half_ref, own_ref, got_ref, heat_in, mom_in, heat_ref, mom_ref):
    own = own_ref[0]
    got = got_ref[0].astype(F32)
    first = half_ref[0] == 0
    a = jnp.where(first, own, got)
    b = jnp.where(first, got, own)
    w = own.shape[1] // 2
    low = lax.broadcasted_iota(jnp.int32, own.shape, 1) < w
    heat_ref[0] = jnp.where(low, a, pltpu.roll(b, w, 1))
    mom_ref[0] = jnp.where(low, pltpu.roll(a, w, 1), b)


def join(half, own, got, outs, rows, total):
    first = rows[0]
    n, width = own.shape[1:]
    unit = pl.BlockSpec((1, n, width), lambda i, s: (i, 0, 0))
    plane = pl.BlockSpec((1, n, width), lambda i, s: (i + first, 0, 0))
    shape = jax.ShapeDtypeStruct((total, n, width), F32)
    body = join_kernel
    extra = {}
    args = (half, own, got)
    specs = [unit, unit]
    if outs is None:
        body = lambda h, a, b, x, y: join_kernel(h, a, b, None, None, x, y)
    else:
        args += outs
        specs += [pl.BlockSpec(memory_space=pl.ANY)] * 2
        extra = {"input_output_aliases": {3: 0, 4: 1}}
    return pl.pallas_call(
        body,
        out_shape=(shape, shape),
        grid_spec=pltpu.PrefetchScalarGridSpec(
            num_scalar_prefetch=1, grid=(len(rows),), in_specs=specs, out_specs=(plane, plane)
        ),
        compiler_params=params(),
        name="join",
        **extra,
    )(*args)


def cosines(first, rows, total):
    index = lax.broadcasted_iota(jnp.int32, (rows, 1), 0) + first
    return jnp.cos(((index.astype(F32) + 0.5) / total - 0.5) * math.pi)


def weigh_kernel(total, place_ref, own_ref, lon_ref, lat_ref, diag_ref, depth_ref, o_ref):
    rows = (own_ref.shape[0] - 1) // 3
    north = place_ref[0] == 1
    depth = depth_ref[0:1, :]

    def both(near, far, first):
        mean = (near[0:rows] + far[0:rows]) / jnp.maximum(
            near[rows : 2 * rows] + far[rows : 2 * rows], 1.0
        )
        return mean * cosines(first, rows, total) * depth, near[2 * rows : 3 * rows]

    mine = both(own_ref, lon_ref, place_ref[1])
    other = both(lat_ref, diag_ref, place_ref[2])
    for i in range(2):
        o_ref[0, i] = jnp.where(north, other[i], mine[i])
        o_ref[1, i] = jnp.where(north, mine[i], other[i])


def band_kernel(total, place_ref, g_ref, l_ref, s_ref, w_ref):
    peers, _, _, rows, width = g_ref.shape
    span = peers * rows
    lane = lax.broadcasted_iota(jnp.int32, (1, width), 1) % 32
    for half in range(2):
        so_far = jnp.zeros((1, width), F32)
        for p in range(peers):
            for r in range(rows):
                so_far = so_far + g_ref[p, half, 0, r : r + 1, :]
                w_ref[p * rows + r : p * rows + r + 1, :] = so_far
        run = w_ref[0:span, :]
        for step in (1, 2, 4, 8, 16):
            run = run + jnp.where(lane >= step, pltpu.roll(run, step, 1), 0.0)
        l_ref[half] = run
        want = jnp.concatenate([g_ref[p, half, 1] for p in range(peers)])
        cosine = cosines(place_ref[half], span, total)
        stats = (
            run[span - 1 : span],
            jnp.max(run, axis=0, keepdims=True),
            jnp.min(run, axis=0, keepdims=True),
            jnp.sum(cosine * run, axis=0, keepdims=True),
            jnp.sum(cosine * run * run, axis=0, keepdims=True),
            jnp.sum(cosine * want, axis=0, keepdims=True),
            jnp.sum(cosine * run * want, axis=0, keepdims=True),
            jnp.sum(cosine * want * want, axis=0, keepdims=True),
        )
        for i, stat in enumerate(stats):
            s_ref[8 * half + i : 8 * half + i + 1, :] = stat


def finish_kernel(total, span, place_ref, own_ref, s_ref, psi_ref, loss_ref):
    blocks, _, width = s_ref.shape
    offset = jnp.zeros((1, width), F32)
    mine = offset
    peak = offset
    square = offset
    cross = offset
    want = offset
    for half in range(2):
        for z in range(blocks):
            at = 8 * half
            s, hi, lo, run1, run2, want1, cross1, want2 = (
                s_ref[z, at + i : at + i + 1, :] for i in range(8)
            )
            here = half * blocks + z
            first = here * span
            weight = float(
                np.sum(np.cos(((np.arange(first, first + span) + 0.5) / total - 0.5) * math.pi))
            )
            mine = jnp.where(place_ref[0] == here, offset, mine)
            peak = jnp.maximum(peak, jnp.maximum(jnp.abs(offset + hi), jnp.abs(offset + lo)))
            square = square + (run2 + 2.0 * offset * run1 + offset * offset * weight)
            cross = cross + (cross1 + offset * want1)
            want = want + want2
            offset = offset + s
    scale = jnp.max(peak, axis=1, keepdims=True) + EPSILON
    psi_ref[...] = (own_ref[...] + mine) / scale
    a = jnp.sum(square, axis=1, keepdims=True)
    b = jnp.sum(cross, axis=1, keepdims=True)
    c = jnp.sum(want, axis=1, keepdims=True)
    loss = (a / scale / scale - 2.0 * (b / scale) + c) / (width * total)
    loss_ref[...] = jnp.broadcast_to(loss, loss_ref.shape)


def all_of(x, axes):
    return lax.all_to_all(
        jnp.broadcast_to(x, (lax.axis_size(axes), *x.shape)), axes, split_axis=0, concat_axis=0, tiled=True
    )


def per_device(u, v, t, mask, depth, desired):
    bands, samples, levels, lon = v.shape
    width = samples * levels
    half = lax.axis_index("lon")
    near = half[None].astype(jnp.int32)
    far = 1 - near
    total = bands * lax.axis_size(LAT_LEV)
    smem = pl.BlockSpec(memory_space=pltpu.SMEM)
    vmem = pl.BlockSpec(memory_space=pltpu.VMEM)

    across = [(0, 1), (1, 0)]
    with jax.named_scope("send"):
        sent = [lax.ppermute(pack(far, u, v, t, mask, rows), "lon", across) for rows in GROUPS]
    own = [pack(near, u, v, t, mask, rows) for rows in GROUPS]

    with jax.named_scope("small"):
        sums = zonal(v, mask, desired.reshape(bands, width))
        by_lon = lax.ppermute(sums, "lon", across)
        by_lat = lax.ppermute(sums, "lat", across)
        by_both = lax.ppermute(sums, ("lat", "lon"), [(i, 3 - i) for i in range(4)])
    per_half = bands * lax.axis_size(("lev_0", "lev_1", "lev_2"))
    lat = lax.axis_index("lat")
    band = lax.axis_index(("lev_0", "lev_1", "lev_2"))
    inner = lax.axis_index(("lev_1", "lev_2"))
    outer = lax.axis_index("lev_0")
    span = bands * lax.axis_size(("lev_1", "lev_2"))
    place = jnp.stack(
        [lat, lat * per_half + band * bands, (1 - lat) * per_half + band * bands]
    ).astype(jnp.int32)
    spread = jnp.tile(depth, samples)[None]
    rows4 = pl.pallas_call(
        lambda *refs: weigh_kernel(total, *refs),
        out_shape=jax.ShapeDtypeStruct((2, 2, bands, width), F32),
        in_specs=[smem] + [vmem] * 5,
        out_specs=vmem,
        name="weigh",
    )(place, sums, by_lon, by_lat, by_both, spread)
    near_bands = all_of(rows4, ("lev_1", "lev_2"))
    place = jnp.stack([outer * span, per_half + outer * span]).astype(jnp.int32)
    runs, stats = pl.pallas_call(
        lambda *refs: band_kernel(total, *refs),
        out_shape=(
            jax.ShapeDtypeStruct((2, span, width), F32),
            jax.ShapeDtypeStruct((16, width), F32),
        ),
        in_specs=[smem, vmem],
        out_specs=(vmem, vmem),
        scratch_shapes=[pltpu.VMEM((span, width), F32)],
        name="bands",
    )(place, near_bands)
    all_stats = all_of(stats, "lev_0")
    mine = lax.dynamic_slice(runs, (lat, inner * bands, 0), (1, bands, width))[0]
    place = (lat * lax.axis_size("lev_0") + outer)[None].astype(jnp.int32)
    psi, loss = pl.pallas_call(
        lambda *refs: finish_kernel(total, span, *refs),
        out_shape=(
            jax.ShapeDtypeStruct((bands, width), F32),
            jax.ShapeDtypeStruct((1, width), F32),
        ),
        in_specs=[smem, vmem, vmem],
        out_specs=(vmem, vmem),
        name="finish",
    )(place, mine, all_stats)

    table = jnp.asarray(half_table(lon), BF16)
    outs = None
    back = []
    kept = []
    for mine, got in zip(own, sent):
        with jax.named_scope("back"):
            back.append(lax.ppermute(waves(far, table, mine, got, BF16), "lon", across))
        kept.append(waves(near, table, mine, got, F32))
    for rows, mine, got in zip(GROUPS, kept, back):
        outs = join(near, mine, got, outs, rows, bands)
    heat, momentum = (jnp.transpose(x, (1, 0, 2)) for x in outs)
    return psi.reshape(bands, samples, levels), heat, momentum, loss[0, 0]


def solution(mesh):
    torus = Mesh(
        mesh.devices.reshape(mesh.shape["lat"], mesh.shape["lon"], 8, 4, 2),
        ("lat", "lon", "lev_0", "lev_1", "lev_2"),
    )
    in_specs = (
        P(LAT_LEV, None, None, "lon"),
        P(LAT_LEV, None, None, "lon"),
        P(LAT_LEV, None, None, "lon"),
        P(LAT_LEV, None, "lon"),
        P(),
        P(LAT_LEV, None, None),
    )
    out_specs = (P(LAT_LEV, None, None), P("lon", LAT_LEV, None), P("lon", LAT_LEV, None), P())
    return jax.shard_map(
        per_device, mesh=torus, in_specs=in_specs, out_specs=out_specs, check_vma=False
    )
```

time: 186 us -> 105 us (0.56)
  blocking collectives: 117 us -> 0 us
  Pallas kernels: 0 us -> 27.9 us
  matrix products: 25.1 us -> 0 us
  starting transfers between devices: 3.33 us -> 26.4 us
  waiting for transfers between devices: 3.1 us -> 23.9 us
  between operations: 16.6 us -> 0.86 us
  local copies, waits for them, and re-layouts: 7.7 us -> 22.7 us
  other arithmetic: 12.4 us -> 1.15 us
    pmax x4 -> x0, blocking collectives: 44.6 us -> none  [one_axis_at_a_time(): return functools.reduce(lax.pmax, axes, array)]
    all_gather x4 -> x0, blocking collectives: 38.5 us -> none  [prefix_by_axis(): pieces = lax.all_gather(so_far, axis)]
    psum x4 -> x0, blocking collectives: 34.3 us -> none  [over_axes(): array = lax.psum(array, axis)]
    pallas_call x0 -> x19, Pallas kernels: none -> 27.9 us  [the longest x6 14.9 us: waves(): pl.pallas_call(wave_kernel, out_shape=jax.ShapeDtypeStruct((rows, n, 2 *...]
    dot_general x1 -> x0, matrix products: 25.1 us -> none  [per_device(): lax.dot_general(waves_table, lax.all_gather(joined_arrays, 'lon', axis=3,...]
    ppermute x0 -> x9, waiting for transfers between devices: none -> 23.3 us  [the longest x1 23.3 us: per_device(): by_lon = lax.ppermute(sums, 'lon', across)]
    unnamed x4 -> x56, local copies, waits for them, and re-layouts: 0.01 us -> 15.9 us
    ppermute x0 -> x9, starting transfers between devices: none -> 11.9 us  [the longest x1 3.79 us: per_device(): by_both = lax.ppermute(sums, ('lat', 'lon'), [(i, 3 - i) for i in range(4)])]
  transfers between devices with their start and end apart: 2 -> 11, of which waited for: 1 -> 2; matrix products, arithmetic and copies ran while one was open for 2% -> 8% of each run, Pallas kernels for 0% -> 24%
where the time goes in v1:
time: 105 us; the launch traced here: 103 us
  Pallas kernels  27.9 us (27%)
  starting transfers between devices  26.4 us (25%)
  waiting for transfers between devices  23.9 us (23%)
  local copies, waits for them, and re-layouts  22.7 us (22%)
  other arithmetic  1.15 us (1%)
    ppermute x1, waiting for transfers between devices, per_device(): by_lon = lax.ppermute(sums, 'lon', across)  23.3 us
    unnamed x56, local copies, waits for them, and re-layouts  15.9 us
    pallas_call x6, Pallas kernels, waves(): pl.pallas_call(wave_kernel, out_shape=jax.ShapeDtypeStruct((rows, n, 2 *...  14.9 us
    all_to_all x2, starting transfers between devices, all_of(): lax.all_to_all(jnp.broadcast_to(x, (lax.axis_size(axes), *x.shape)), axes...  14.5 us
    pallas_call x3, Pallas kernels, join(): pl.pallas_call(body, out_shape=(shape, shape), grid_spec=pltpu.PrefetchSc...  4.79 us
    ppermute x1, starting transfers between devices, per_device(): by_both = lax.ppermute(sums, ('lat', 'lon'), [(i, 3 - i) for i in range(4)])  3.79 us
    ppermute x3, starting transfers between devices, per_device(): lax.ppermute(pack(far, u, v, t, mask, rows), 'lon', across)  3.57 us
    ppermute x1, starting transfers between devices, per_device(): by_lat = lax.ppermute(sums, 'lat', across)  2.98 us
  transfers between devices with their start and end apart: 11, of which 2 were waited for; matrix products, arithmetic and copies ran while one was open for 8% of the time, Pallas kernels for 24%

profile of v1, /device:TPU:1, one launch (start us, length us, event | category | flops | bytes accessed | tf_op | source)
XLA Modules:
  0.0 102.9 jit_solution(17778811683492231368)
XLA Ops:
  1.8 1.2 %copy-done.3 = bf16[5,4,32,720]{3,2,1,0:T(8,128)(2,1)S(1)} copy-done((bf16[5,4,32,720]{3,2,1,0:T(8,128)(2,1)S(1)}, bf16[5,4,32,720]{3,2,1,0:T(8,128)(2,1)}, u32[]{:S(2)}) %copy-start.3) | copy-done | bytes 921624
  6.1 2.0 %collective-permute-start.5 = (bf16[2,192,720]{2,1,0:T(8,128)(2,1)}, bf16[2,192,720]{2,1,0:T(8,128)(2,1)}, u32[]{:S(2)}, u32[]{:S(2)}) collective-permute-start(bf16[2,192,720]{2,1,0:T(8,128)(2,1)} %pack.9), channel_id=1, source_target_pairs={{0,64},{64,0},{1,65},{65,1},{2,66},{66,2},{3,67},{67,3},{4,68},{68... | collective-permute-start | bytes 1658888 | tf_op jit(solution)/shard_map/send/ppermute | solution.py:276
  9.8 1.4 %collective-permute-start.7 = (bf16[1,192,720]{2,1,0:T(8,128)(2,1)}, bf16[1,192,720]{2,1,0:T(8,128)(2,1)}, u32[]{:S(2)}, u32[]{:S(2)}) collective-permute-start(bf16[1,192,720]{2,1,0:T(8,128)(2,1)} %pack.11), channel_id=1, source_target_pairs={{0,64},{64,0},{1,65},{65,1},{2,66},{66,2},{3,67},{67,3},{4,68},{68... | collective-permute-start | bytes 829448 | tf_op jit(solution)/shard_map/send/ppermute | solution.py:276
  13.0 3.0 %collective-permute-start.1 = (f32[16,128]{1,0:T(8,128)S(1)}, f32[16,128]{1,0:T(8,128)S(1)}, u32[]{:S(2)}, u32[]{:S(2)}) collective-permute-start(f32[16,128]{1,0:T(8,128)S(1)} %zonal.1.refs_1_), channel_id=1, source_target_pairs={{0,128},{128,0},{1,129},{129,1},{2,130},{130,2},{3,131},{131,3},{4... | collective-permute-start | bytes 24584 | tf_op jit(solution)/shard_map/small/ppermute | solution.py:282
  16.0 23.3 %collective-permute-done.refs_2_ = f32[16,128]{1,0:T(8,128)S(1)} collective-permute-done((f32[16,128]{1,0:T(8,128)S(1)}, f32[16,128]{1,0:T(8,128)S(1)}, u32[]{:S(2)}, u32[]{:S(2)}) %collective-permute-start) | collective-permute-done | bytes 8224 | tf_op jit(solution)/shard_map/small/ppermute | solution.py:281
  39.3 3.8 %collective-permute-start.2 = (f32[16,128]{1,0:T(8,128)S(1)}, f32[16,128]{1,0:T(8,128)S(1)}, u32[]{:S(2)}, u32[]{:S(2)}) collective-permute-start(f32[16,128]{1,0:T(8,128)S(1)} %zonal.1.refs_1_), channel_id=1, source_target_pairs={{0,192},{64,128},{128,64},{192,0},{1,193},{65,129},{129,65},{193,1... | collective-permute-start | bytes 24584 | tf_op jit(solution)/shard_map/small/ppermute | solution.py:283
  45.6 1.2 %copy-done.5 = bf16[5,4,32,720]{3,2,1,0:T(8,128)(2,1)S(1)} copy-done((bf16[5,4,32,720]{3,2,1,0:T(8,128)(2,1)S(1)}, bf16[5,4,32,720]{3,2,1,0:T(8,128)(2,1)}, u32[]{:S(2)}) %copy-start.5) | copy-done | bytes 921624
  49.5 1.5 %weigh.1 = f32[2,2,5,128]{3,2,1,0:T(8,128)} custom-call(s32[3]{0:T(128)} %pad_add_fusion.1.refs_0_, f32[16,128]{1,0:T(8,128)} %copy-done.21, f32[16,128]{1,0:T(8,128)} %copy-done.24, f32[16,128]{1,0:T(8,128)} %copy-done.25, f32[16,128]{1,0:T(8,128)} %copy-done.26, f32[1,128]{1,0:T(1,128)} %broadcast_in_dim_tile.3.refs_5_), custom_call_target="tpu_custom_call" | custom-call | tf_op jit(solution)/shard_map/weigh/pallas_call | solution.py:294
  52.4 6.3 %all-to-all-start = ((f32[8,2,2,5,128]{4,2,3,1,0:T(2,128)}), f32[8,2,2,5,128]{4,2,3,1,0:T(2,128)S(1)}, u32[]{:S(2)}, u32[]{:S(2)}) async-start(f32[8,2,2,5,128]{4,2,3,1,0:T(2,128)} %broadcast_in_dim.13), calls=%async_computation | async-start | bytes 163840 | tf_op jit(solution)/shard_map/all_to_all | solution.py:259
  59.8 3.2 %waves.9 = bf16[2,360,128]{2,1,0:T(8,128)(2,1)} custom-call(s32[1]{0:T(128)S(6)} %sub.7.half_ref, bf16[2,720,720]{2,1,0:T(8,128)(2,1)S(1)} %copy-done, bf16[2,192,720]{2,1,0:T(8,128)(2,1)S(1)} %copy-done.19, bf16[2,192,720]{2,1,0:T(8,128)(2,1)} %collective-permute-done.5.got_ref), custom_call_target="tpu_custom_call" | custom-call | tf_op jit(solution)/shard_map/back/waves/pallas_call | solution.py:117
  63.0 3.2 %waves.7 = bf16[2,360,128]{2,1,0:T(8,128)(2,1)} custom-call(s32[1]{0:T(128)S(6)} %sub.7.half_ref, bf16[2,720,720]{2,1,0:T(8,128)(2,1)S(1)} %copy-done, bf16[2,192,720]{2,1,0:T(8,128)(2,1)S(1)} %copy-done.16, bf16[2,192,720]{2,1,0:T(8,128)(2,1)} %collective-permute-done.3.got_ref), custom_call_target="tpu_custom_call" | custom-call | tf_op jit(solution)/shard_map/back/waves/pallas_call | solution.py:117
  66.1 1.4 %collective-permute-start.4 = (bf16[2,360,128]{2,1,0:T(8,128)(2,1)}, bf16[2,360,128]{2,1,0:T(8,128)(2,1)}, u32[]{:S(2)}, u32[]{:S(2)}) collective-permute-start(bf16[2,360,128]{2,1,0:T(8,128)(2,1)} %waves.7), channel_id=1, source_target_pairs={{0,64},{64,0},{1,65},{65,1},{2,66},{66,2},{3,67},{67,3},{4,68},{68... | collective-permute-start | bytes 552968 | tf_op jit(solution)/shard_map/back/ppermute | solution.py:334
  68.8 2.0 %bands.1 = (f32[2,40,128]{2,1,0:T(8,128)}, f32[16,128]{1,0:T(8,128)}) custom-call(s32[2]{0:T(128)} %pad_add_fusion.refs_0_, f32[8,2,2,5,128]{4,3,2,1,0:T(8,128)} %copy.16.refs_1_), custom_call_target="tpu_custom_call" | custom-call | tf_op jit(solution)/shard_map/bands/pallas_call | solution.py:303
  70.8 1.3 %broadcast_in_dim.14 = f32[8,16,128]{2,1,0:T(8,128)} broadcast(f32[16,128]{1,0:T(8,128)} %get-tuple-element.15), dimensions={1,2} | broadcast | bytes 73728 | tf_op jit(solution)/shard_map/broadcast_in_dim | solution.py:260
  72.1 8.2 %all-to-all-start.1 = ((f32[8,16,128]{2,1,0:T(8,128)}), f32[8,16,128]{2,1,0:T(8,128)S(1)}, u32[]{:S(2)}, u32[]{:S(2)}) async-start(f32[8,16,128]{2,1,0:T(8,128)} %broadcast_in_dim.14), calls=%async_computation.1 | async-start | bytes 131072 | tf_op jit(solution)/shard_map/all_to_all | solution.py:259
  83.8 1.7 %waves.11 = bf16[1,360,128]{2,1,0:T(8,128)(2,1)S(1)} custom-call(s32[1]{0:T(128)S(6)} %sub.7.half_ref, bf16[2,720,720]{2,1,0:T(8,128)(2,1)S(1)} %copy-done, bf16[1,192,720]{2,1,0:T(8,128)(2,1)S(1)} %pack.10.own_ref, bf16[1,192,720]{2,1,0:T(8,128)(2,1)} %collective-permute-done.7.got_ref), custom_call_target="tpu_custom_call" | custom-call | tf_op jit(solution)/shard_map/back/waves/pallas_call | solution.py:117
  85.7 1.4 %dynamic-slice_bitcast_fusion.refs_1_ = f32[5,128]{1,0:T(8,128)} fusion(f32[2,40,128]{2,1,0:T(8,128)} %get-tuple-element.14, s32[]{:T(128)S(6)} %select_n.6, s32[]{:T(128)S(6)} %select_n.7), kind=kLoop, calls=%fused_computation | loop fusion | bytes 5128 | tf_op jit(solution)/shard_map/squeeze | solution.py:315
  88.3 1.6 %finish.1 = (f32[5,128]{1,0:T(8,128)}, f32[1,128]{1,0:T(1,128)}) custom-call(s32[1]{0:T(128)} %bitcast.refs_0_, f32[5,128]{1,0:T(8,128)} %dynamic-slice_bitcast_fusion.refs_1_, f32[8,16,128]{2,1,0:T(8,128)} %copy-done.22), custom_call_target="tpu_custom_call" | custom-call | tf_op jit(solution)/shard_map/finish/pallas_call | solution.py:317
  89.8 1.4 %reshape.16 = f32[5,4,32]{2,1,0:T(4,128)} reshape(f32[5,128]{1,0:T(8,128)} %get-tuple-element.16) | data formatting | bytes 5120 | tf_op jit(solution)/shard_map/reshape | solution.py:339
  91.2 1.7 %waves.10.a = f32[1,360,128]{2,1,0:T(8,128)S(1)} custom-call(s32[1]{0:T(128)} %bitcast.7.half_ref.h, bf16[2,720,720]{2,1,0:T(8,128)(2,1)S(1)} %copy-done, bf16[1,192,720]{2,1,0:T(8,128)(2,1)S(1)} %pack.10.own_ref, bf16[1,192,720]{2,1,0:T(8,128)(2,1)} %collective-permute-done.7.got_ref), custom_call_target="tpu_custom_call" | custom-call | tf_op jit(solution)/shard_map/waves/pallas_call | solution.py:117
  93.8 2.5 %waves.8.own_ref = f32[2,360,128]{2,1,0:T(8,128)S(1)} custom-call(s32[1]{0:T(128)} %bitcast.7.half_ref.h, bf16[2,720,720]{2,1,0:T(8,128)(2,1)S(1)} %copy-done, bf16[2,192,720]{2,1,0:T(8,128)(2,1)S(1)} %copy-done.20, bf16[2,192,720]{2,1,0:T(8,128)(2,1)} %collective-permute-done.5.got_ref), custom_call_target="tpu_custom_call" | custom-call | tf_op jit(solution)/shard_map/waves/pallas_call | solution.py:117
  96.4 2.5 %waves.6.own_ref = f32[2,360,128]{2,1,0:T(8,128)S(1)} custom-call(s32[1]{0:T(128)} %bitcast.7.half_ref.h, bf16[2,720,720]{2,1,0:T(8,128)(2,1)S(1)} %copy-done, bf16[2,192,720]{2,1,0:T(8,128)(2,1)S(1)} %copy-done.17, bf16[2,192,720]{2,1,0:T(8,128)(2,1)} %collective-permute-done.3.got_ref), custom_call_target="tpu_custom_call" | custom-call | tf_op jit(solution)/shard_map/waves/pallas_call | solution.py:117
  98.9 2.0 %join.4 = (f32[5,360,128]{2,1,0:T(8,128)}, f32[5,360,128]{2,1,0:T(8,128)}) custom-call(s32[1]{0:T(128)} %bitcast.7.half_ref.h, f32[2,360,128]{2,1,0:T(8,128)S(1)} %waves.8.own_ref, bf16[2,360,128]{2,1,0:T(8,128)(2,1)} %collective-permute-done.6.got_ref, f32[5,360,128]{2,1,0:T(8,128)} %get-tuple-element.17.heat_in, ...), custom_call_target="tpu_custom_call", output_to_operand_aliasing={{0}: (3, {}), {1}: (4, {})} | custom-call | tf_op jit(solution)/shard_map/join/pallas_call | solution.py:159
  100.9 2.0 %join.5 = (f32[5,360,128]{2,1,0:T(8,128)}, f32[5,360,128]{2,1,0:T(8,128)}) custom-call(s32[1]{0:T(128)} %bitcast.7.half_ref.h, f32[2,360,128]{2,1,0:T(8,128)S(1)} %waves.6.own_ref, bf16[2,360,128]{2,1,0:T(8,128)(2,1)} %collective-permute-done.4.got_ref, f32[5,360,128]{2,1,0:T(8,128)} %get-tuple-element.19.heat_in, ...), custom_call_target="tpu_custom_call", output_to_operand_aliasing={{0}: (3, {}), {1}: (4, {})} | custom-call | tf_op jit(solution)/shard_map/join/pallas_call | solution.py:159
  (84 shorter events, 22.4 us)
Async XLA Ops:
  0.6 1.2 %copy-start.1 = (bf16[5,4,32,720]{3,2,1,0:T(8,128)(2,1)S(1)}, bf16[5,4,32,720]{3,2,1,0:T(8,128)(2,1)}, u32[]{:S(2)}) copy-start(bf16[5,4,32,720]{3,2,1,0:T(8,128)(2,1)} %v_ref.13) | copy-start | bytes 2764804
  6.1 52.5 %collective-permute-start.5 = (bf16[2,192,720]{2,1,0:T(8,128)(2,1)}, bf16[2,192,720]{2,1,0:T(8,128)(2,1)}, u32[]{:S(2)}, u32[]{:S(2)}) collective-permute-start(bf16[2,192,720]{2,1,0:T(8,128)(2,1)} %pack.9), channel_id=1, source_target_pairs={{0,64},{64,0},{1,65},{65,1},{2,66},{66,2},{3,67},{67,3},{4,68},{68... | collective-permute-start | bytes 1658888 | tf_op jit(solution)/shard_map/send/ppermute | solution.py:276
  9.0 2.3 %copy-start.23 = (f32[5,4,32]{2,1,0:T(4,128)S(1)}, f32[5,4,32]{2,1,0:T(4,128)}, u32[]{:S(2)}) copy-start(f32[5,4,32]{2,1,0:T(4,128)} %param.12) | copy-start | bytes 7684
  9.0 2.4 %copy-start.2 = (bf16[5,4,32,720]{3,2,1,0:T(8,128)(2,1)S(1)}, bf16[5,4,32,720]{3,2,1,0:T(8,128)(2,1)}, u32[]{:S(2)}) copy-start(bf16[5,4,32,720]{3,2,1,0:T(8,128)(2,1)} %v_ref.13) | copy-start | bytes 2764804
  9.0 34.6 %copy-start.4 = (bf16[5,4,32,720]{3,2,1,0:T(8,128)(2,1)S(1)}, bf16[5,4,32,720]{3,2,1,0:T(8,128)(2,1)}, u32[]{:S(2)}) copy-start(bf16[5,4,32,720]{3,2,1,0:T(8,128)(2,1)} %u_ref.11) | copy-start | bytes 2764804
  9.0 34.6 %copy-start.8 = (bf16[5,4,32,720]{3,2,1,0:T(8,128)(2,1)S(1)}, bf16[5,4,32,720]{3,2,1,0:T(8,128)(2,1)}, u32[]{:S(2)}) copy-start(bf16[5,4,32,720]{3,2,1,0:T(8,128)(2,1)} %t_ref.11) | copy-start | bytes 2764804
  9.0 54.0 %collective-permute-start.3 = (bf16[2,192,720]{2,1,0:T(8,128)(2,1)}, bf16[2,192,720]{2,1,0:T(8,128)(2,1)}, u32[]{:S(2)}, u32[]{:S(2)}) collective-permute-start(bf16[2,192,720]{2,1,0:T(8,128)(2,1)} %pack.7), channel_id=1, source_target_pairs={{0,64},{64,0},{1,65},{65,1},{2,66},{66,2},{3,67},{67,3},{4,68},{68... | collective-permute-start | bytes 1658888 | tf_op jit(solution)/shard_map/send/ppermute | solution.py:276
  9.8 74.0 %collective-permute-start.7 = (bf16[1,192,720]{2,1,0:T(8,128)(2,1)}, bf16[1,192,720]{2,1,0:T(8,128)(2,1)}, u32[]{:S(2)}, u32[]{:S(2)}) collective-permute-start(bf16[1,192,720]{2,1,0:T(8,128)(2,1)} %pack.11), channel_id=1, source_target_pairs={{0,64},{64,0},{1,65},{65,1},{2,66},{66,2},{3,67},{67,3},{4,68},{68... | collective-permute-start | bytes 829448 | tf_op jit(solution)/shard_map/send/ppermute | solution.py:276
  13.0 33.9 %copy-start.21 = (f32[16,128]{1,0:T(8,128)}, f32[16,128]{1,0:T(8,128)S(1)}, u32[]{:S(2)}) copy-start(f32[16,128]{1,0:T(8,128)S(1)} %zonal.1.refs_1_) | copy-start | bytes 24580
  13.0 26.3 %collective-permute-start = (f32[16,128]{1,0:T(8,128)S(1)}, f32[16,128]{1,0:T(8,128)S(1)}, u32[]{:S(2)}, u32[]{:S(2)}) collective-permute-start(f32[16,128]{1,0:T(8,128)S(1)} %zonal.1.refs_1_), channel_id=1, source_target_pairs={{0,64},{64,0},{1,65},{65,1},{2,66},{66,2},{3,67},{67,3},{4,68},{68... | collective-permute-start | bytes 24584 | tf_op jit(solution)/shard_map/small/ppermute | solution.py:281
  13.0 35.3 %collective-permute-start.1 = (f32[16,128]{1,0:T(8,128)S(1)}, f32[16,128]{1,0:T(8,128)S(1)}, u32[]{:S(2)}, u32[]{:S(2)}) collective-permute-start(f32[16,128]{1,0:T(8,128)S(1)} %zonal.1.refs_1_), channel_id=1, source_target_pairs={{0,128},{128,0},{1,129},{129,1},{2,130},{130,2},{3,131},{131,3},{4... | collective-permute-start | bytes 24584 | tf_op jit(solution)/shard_map/small/ppermute | solution.py:282
  16.0 29.6 %copy-start.9 = (bf16[5,4,32,720]{3,2,1,0:T(8,128)(2,1)S(1)}, bf16[5,4,32,720]{3,2,1,0:T(8,128)(2,1)}, u32[]{:S(2)}) copy-start(bf16[5,4,32,720]{3,2,1,0:T(8,128)(2,1)} %t_ref.11) | copy-start | bytes 2764804
  39.3 7.6 %copy-start.24 = (f32[16,128]{1,0:T(8,128)}, f32[16,128]{1,0:T(8,128)S(1)}, u32[]{:S(2)}) copy-start(f32[16,128]{1,0:T(8,128)S(1)} %collective-permute-done.refs_2_) | copy-start | bytes 24580
  39.3 9.0 %collective-permute-start.2 = (f32[16,128]{1,0:T(8,128)S(1)}, f32[16,128]{1,0:T(8,128)S(1)}, u32[]{:S(2)}, u32[]{:S(2)}) collective-permute-start(f32[16,128]{1,0:T(8,128)S(1)} %zonal.1.refs_1_), channel_id=1, source_target_pairs={{0,192},{64,128},{128,64},{192,0},{1,193},{65,129},{129,65},{193,1... | collective-permute-start | bytes 24584 | tf_op jit(solution)/shard_map/small/ppermute | solution.py:283
  45.6 1.2 %copy-start.5 = (bf16[5,4,32,720]{3,2,1,0:T(8,128)(2,1)S(1)}, bf16[5,4,32,720]{3,2,1,0:T(8,128)(2,1)}, u32[]{:S(2)}) copy-start(bf16[5,4,32,720]{3,2,1,0:T(8,128)(2,1)} %u_ref.11) | copy-start | bytes 2764804
  46.8 11.9 %copy-start = (bf16[2,720,720]{2,1,0:T(8,128)(2,1)S(1)}, bf16[2,720,720]{2,1,0:T(8,128)(2,1)}, u32[]{:S(2)}) copy-start(bf16[2,720,720]{2,1,0:T(8,128)(2,1)} %constant.37.clone.table_ref) | copy-start | bytes 6220804
  52.4 15.8 %all-to-all-start = ((f32[8,2,2,5,128]{4,2,3,1,0:T(2,128)}), f32[8,2,2,5,128]{4,2,3,1,0:T(2,128)S(1)}, u32[]{:S(2)}, u32[]{:S(2)}) async-start(f32[8,2,2,5,128]{4,2,3,1,0:T(2,128)} %broadcast_in_dim.13), calls=%async_computation | async-start | bytes 163840 | tf_op jit(solution)/shard_map/all_to_all | solution.py:259
  58.6 4.3 %copy-start.16 = (bf16[2,192,720]{2,1,0:T(8,128)(2,1)S(1)}, bf16[2,192,720]{2,1,0:T(8,128)(2,1)}, u32[]{:S(2)}) copy-start(bf16[2,192,720]{2,1,0:T(8,128)(2,1)} %copy-done.15) | copy-start | bytes 1658884
  62.9 36.0 %collective-permute-start.6 = (bf16[2,360,128]{2,1,0:T(8,128)(2,1)}, bf16[2,360,128]{2,1,0:T(8,128)(2,1)}, u32[]{:S(2)}, u32[]{:S(2)}) collective-permute-start(bf16[2,360,128]{2,1,0:T(8,128)(2,1)} %waves.9), channel_id=1, source_target_pairs={{0,64},{64,0},{1,65},{65,1},{2,66},{66,2},{3,67},{67,3},{4,68},{68... | collective-permute-start | bytes 552968 | tf_op jit(solution)/shard_map/back/ppermute | solution.py:334
  66.1 34.8 %collective-permute-start.4 = (bf16[2,360,128]{2,1,0:T(8,128)(2,1)}, bf16[2,360,128]{2,1,0:T(8,128)(2,1)}, u32[]{:S(2)}, u32[]{:S(2)}) collective-permute-start(bf16[2,360,128]{2,1,0:T(8,128)(2,1)} %waves.7), channel_id=1, source_target_pairs={{0,64},{64,0},{1,65},{65,1},{2,66},{66,2},{3,67},{67,3},{4,68},{68... | collective-permute-start | bytes 552968 | tf_op jit(solution)/shard_map/back/ppermute | solution.py:334
  72.1 15.5 %all-to-all-start.1 = ((f32[8,16,128]{2,1,0:T(8,128)}), f32[8,16,128]{2,1,0:T(8,128)S(1)}, u32[]{:S(2)}, u32[]{:S(2)}) async-start(f32[8,16,128]{2,1,0:T(8,128)} %broadcast_in_dim.14), calls=%async_computation.1 | async-start | bytes 131072 | tf_op jit(solution)/shard_map/all_to_all | solution.py:259
  85.6 8.3 %copy-start.20 = (bf16[2,192,720]{2,1,0:T(8,128)(2,1)S(1)}, bf16[2,192,720]{2,1,0:T(8,128)(2,1)}, u32[]{:S(2)}) copy-start(bf16[2,192,720]{2,1,0:T(8,128)(2,1)} %copy-done.18) | copy-start | bytes 1658884
  85.6 7.4 %collective-permute-start.8 = (bf16[1,360,128]{2,1,0:T(8,128)(2,1)S(1)}, bf16[1,360,128]{2,1,0:T(8,128)(2,1)S(1)}, u32[]{:S(2)}, u32[]{:S(2)}) collective-permute-start(bf16[1,360,128]{2,1,0:T(8,128)(2,1)S(1)} %waves.11), channel_id=1, source_target_pairs={{0,64},{64,0},{1,65},{65,1},{2,66},{66,2},{3,67},{67,3},{4,68},{68... | collective-permute-start | bytes 276488 | tf_op jit(solution)/shard_map/back/ppermute | solution.py:334
  92.9 3.4 %copy-start.17 = (bf16[2,192,720]{2,1,0:T(8,128)(2,1)S(1)}, bf16[2,192,720]{2,1,0:T(8,128)(2,1)}, u32[]{:S(2)}) copy-start(bf16[2,192,720]{2,1,0:T(8,128)(2,1)} %copy-done.15) | copy-start | bytes 1658884
  (15 other events, 14.4 us)

commit v2 on v0

v2 whole, which is shorter than its diff:
```python
import math

import jax
import jax.numpy as jnp
import numpy as np
from jax import lax
from jax.experimental import pallas as pl
from jax.experimental.pallas import tpu as pltpu
from jax.sharding import Mesh
from jax.sharding import PartitionSpec as P


MERIDIANS = 1440
ORDERS = 720
LAT_LEV = ("lat", "lev_0", "lev_1", "lev_2")
INNER = ("lev_1", "lev_2")
EPSILON = 1e-06
GROUPS = ((0,), (1, 2), (3, 4))
F32 = jnp.float32
BF16 = jnp.bfloat16
MIB = 1024 * 1024
CONTRACT = (((1,), (1,)), ((), ()))
SMEM = pl.BlockSpec(memory_space=pltpu.SMEM)
VMEM = pl.BlockSpec(memory_space=pltpu.VMEM)
HBM = pl.BlockSpec(memory_space=pltpu.HBM)
ANY = pl.BlockSpec(memory_space=pl.ANY)


def half_table(lon):
    order = np.arange(1, ORDERS + 1, dtype=np.int64)
    turns = (order[:, None] * np.arange(lon, dtype=np.int64)[None, :]) % MERIDIANS
    angle = turns.astype(np.float32) * np.float32(2.0 * math.pi / MERIDIANS)
    both = np.stack([np.cos(angle), np.sin(angle)]).reshape(2, 2, ORDERS // 2, lon)
    return np.ascontiguousarray(both.transpose(1, 0, 2, 3)).reshape(2, ORDERS, lon)


def params(mib):
    return pltpu.CompilerParams(vmem_limit_bytes=mib * MIB)


def keep_of(mask):
    return mask.astype(F32).astype(BF16)


def pack_kernel(rows, flip, half_ref, u_ref, v_ref, t_ref, m_ref, o_ref, fields, masks, sems):
    part = fields.shape[2]
    half = 1 - half_ref[0] if flip else half_ref[0]
    copies = []
    for i, row in enumerate(rows):
        group = [pltpu.make_async_copy(m_ref.at[row], masks.at[i], sems.at[i, 3])]
        for f, ref in enumerate((t_ref, u_ref, v_ref)):
            group.append(
                pltpu.make_async_copy(
                    ref.at[row, pl.ds(half * part, part)], fields.at[i, f], sems.at[i, f]
                )
            )
        for c in group:
            c.start()
        copies.append(group)
    size = part * fields.shape[3]
    for i, group in enumerate(copies):
        for c in group:
            c.wait()
        keep = keep_of(masks[i])[None]
        for f in range(3):
            o_ref[i, f * size : (f + 1) * size, :] = (fields[i, f] * keep).reshape(size, -1)


def pack(half, u, v, t, mask, rows, flip):
    _, samples, levels, lon = u.shape
    part = samples // 2
    n = len(rows)
    return pl.pallas_call(
        lambda *refs: pack_kernel(rows, flip, *refs),
        out_shape=jax.ShapeDtypeStruct((n, 3 * part * levels, lon), BF16),
        in_specs=[SMEM, HBM, HBM, HBM, HBM],
        out_specs=VMEM,
        scratch_shapes=[
            pltpu.VMEM((n, 3, part, levels, lon), BF16),
            pltpu.VMEM((n, levels, lon), jnp.int32),
            pltpu.SemaphoreType.DMA((n, 4)),
        ],
        compiler_params=params(60),
        name="pack",
    )(half, u, v, t, mask)


def send_kernel(groups, half_ref, u_ref, v_ref, t_ref, m_ref, _, *rest):
    outs, (sums_ref, us, vs, ts, masks, sems) = rest[: len(groups)], rest[len(groups) :]
    rows, samples, levels, lon = vs.shape
    part = samples // 2
    size = part * levels
    far = 1 - half_ref[0]
    wanted = [row for group in groups for row in group]
    copies = {}
    for j in range(rows):
        group = [
            pltpu.make_async_copy(m_ref.at[j], masks.at[j], sems.at[j, 0]),
            pltpu.make_async_copy(v_ref.at[j], vs.at[j], sems.at[j, 1]),
        ]
        if j in wanted:
            at = pl.ds(far * part, part)
            group.append(pltpu.make_async_copy(u_ref.at[j, at], us.at[j], sems.at[j, 2]))
            group.append(pltpu.make_async_copy(t_ref.at[j, at], ts.at[j], sems.at[j, 3]))
        for c in group:
            c.start()
        copies[j] = group
    ones = jnp.ones((8, lon), BF16)
    for j in range(rows):
        for c in copies[j]:
            c.wait()
        keep = keep_of(masks[j])
        v = (vs[j] * keep[None]).reshape(samples * levels, lon)
        sums_ref[j : j + 1, :] = lax.dot_general(ones, v, CONTRACT, preferred_element_type=F32)[0:1]
        full = jnp.broadcast_to(keep[None], (samples, levels, lon)).reshape(samples * levels, lon)
        sums_ref[rows + j : rows + j + 1, :] = lax.dot_general(
            ones, full, CONTRACT, preferred_element_type=F32
        )[0:1]
        for g, group in enumerate(groups):
            if j in group:
                i = group.index(j)
                outs[g][i, 0:size, :] = (ts[j] * keep[None]).reshape(size, lon)
                outs[g][i, size : 2 * size, :] = (us[j] * keep[None]).reshape(size, lon)
                mine = vs[j, pl.ds(far * part, part)] * keep[None]
                outs[g][i, 2 * size :, :] = mine.reshape(size, lon)


def send(half, u, v, t, mask, after, groups):
    rows, samples, levels, lon = v.shape
    part = samples // 2
    return pl.pallas_call(
        lambda *refs: send_kernel(groups, *refs),
        out_shape=(
            *(jax.ShapeDtypeStruct((len(g), 3 * part * levels, lon), BF16) for g in groups),
            jax.ShapeDtypeStruct((2 * rows, samples * levels), F32),
        ),
        in_specs=[SMEM, HBM, HBM, HBM, HBM, ANY],
        out_specs=(VMEM,) * (len(groups) + 1),
        scratch_shapes=[
            pltpu.VMEM((rows, part, levels, lon), BF16),
            pltpu.VMEM((rows, samples, levels, lon), BF16),
            pltpu.VMEM((rows, part, levels, lon), BF16),
            pltpu.VMEM((rows, levels, lon), jnp.int32),
            pltpu.SemaphoreType.DMA((rows, 4)),
        ],
        compiler_params=params(60),
        name="send",
    )(half, u, v, t, mask, after)


def wave_kernel(flip, half_ref, table_ref, own_ref, got_ref, _, o_ref):
    def lay(x):
        return jnp.concatenate([x, x[2 * x.shape[0] // 3 :]])

    table = table_ref[1 - half_ref[0] if flip else half_ref[0]]
    n = table.shape[0] // 2
    odd = lax.broadcasted_iota(jnp.int32, (n, 1), 0) % 2 == 0
    sign = jnp.where(odd, -1.0, 1.0).astype(F32)
    scale = 2.0 / (MERIDIANS * MERIDIANS)
    for i in range(got_ref.shape[0]):
        near = lax.dot_general(table, lay(own_ref[i]), CONTRACT, preferred_element_type=F32)
        far = lax.dot_general(table, lay(got_ref[i]), CONTRACT, preferred_element_type=F32)
        cos = near[:n] + sign * far[:n]
        sin = near[n:] + sign * far[n:]
        w = cos.shape[1] // 2
        both = cos[:, :w] * cos[:, w:] + sin[:, :w] * sin[:, w:]
        o_ref[i] = (scale * both).astype(o_ref.dtype)


def waves(half, table, own, got, after, flip, dtype):
    rows, cols, _ = got.shape
    return pl.pallas_call(
        lambda *refs: wave_kernel(flip, *refs),
        out_shape=jax.ShapeDtypeStruct((rows, table.shape[1] // 2, 2 * cols // 3), dtype),
        in_specs=[SMEM, VMEM, VMEM, VMEM, ANY],
        out_specs=VMEM,
        compiler_params=params(16),
        name="waves",
    )(half, table, own, got, after)


def join_kernel(first, half_ref, own_ref, got_ref, heat_in, mom_in, heat_ref, mom_ref, heat, mom, sems):
    copies = []
    for i in range(own_ref.shape[0]):
        own = own_ref[i]
        got = got_ref[i].astype(F32)
        zero = half_ref[0] == 0
        a = jnp.where(zero, own, got)
        b = jnp.where(zero, got, own)
        w = own.shape[1] // 2
        low = lax.broadcasted_iota(jnp.int32, own.shape, 1) < w
        heat[i] = jnp.where(low, a, pltpu.roll(b, w, 1))
        mom[i] = jnp.where(low, pltpu.roll(a, w, 1), b)
        for k, (x, ref) in enumerate(((heat, heat_ref), (mom, mom_ref))):
            c = pltpu.make_async_copy(x.at[i], ref.at[first + i], sems.at[i, k])
            c.start()
            copies.append(c)
    for c in copies:
        c.wait()


def join(half, own, got, outs, rows, total):
    n, width = own.shape[1:]
    shape = jax.ShapeDtypeStruct((total, n, width), F32)
    args = (half, own, got)
    specs = [SMEM, VMEM, VMEM]
    extra = {}
    first = rows[0]
    if outs is None:
        body = lambda h, a, b, *refs: join_kernel(first, h, a, b, None, None, *refs)
    else:
        body = lambda *refs: join_kernel(first, *refs)
        args += outs
        specs += [HBM, HBM]
        extra = {"input_output_aliases": {3: 0, 4: 1}}
    return pl.pallas_call(
        body,
        out_shape=(shape, shape),
        in_specs=specs,
        out_specs=(HBM, HBM),
        scratch_shapes=[
            pltpu.VMEM((len(rows), n, width), F32),
            pltpu.VMEM((len(rows), n, width), F32),
            pltpu.SemaphoreType.DMA((len(rows), 2)),
        ],
        compiler_params=params(8),
        name="join",
        **extra,
    )(*args)


def cosines(first, rows, total):
    index = lax.broadcasted_iota(jnp.int32, (rows, 1), 0) + first
    return jnp.cos(((index.astype(F32) + 0.5) / total - 0.5) * math.pi)


def weight_of(first, rows, total):
    latitude = ((np.arange(first, first + rows) + 0.5) / total - 0.5) * math.pi
    return float(np.sum(np.cos(latitude)))


def weigh_kernel(total, place_ref, own_ref, lon_ref, depth_ref, d_ref, o_ref):
    rows, samples, levels = d_ref.shape
    band = place_ref[0] // 128 * 64 + place_ref[0] % 64
    depth = depth_ref[...]
    spread = jnp.concatenate([depth] * samples, axis=1)
    kept = own_ref[rows : 2 * rows] + lon_ref[rows : 2 * rows]
    mean = (own_ref[0:rows] + lon_ref[0:rows]) / jnp.maximum(kept, 1.0)
    weighted = mean * cosines(band * rows, rows, total) * spread
    for p in range(o_ref.shape[0]):
        o_ref[p, 0:rows, :] = weighted
        for b in range(samples):
            o_ref[p, 8 : 8 + rows, b * levels : (b + 1) * levels] = d_ref[:, b, :]


def band_kernel(total, rows, levels, place_ref, g_ref, mine_ref, s_ref, w_ref):
    peers, _, width = g_ref.shape
    span = peers * rows
    lane = lax.broadcasted_iota(jnp.int32, (1, width), 1) % levels
    so_far = jnp.zeros((1, width), F32)
    for p in range(peers):
        for r in range(rows):
            so_far = so_far + g_ref[p, r : r + 1, :]
            w_ref[p * rows + r : p * rows + r + 1, :] = so_far
            w_ref[span + p * rows + r : span + p * rows + r + 1, :] = g_ref[p, 8 + r : 9 + r, :]
    run = w_ref[0:span, :]
    step = 1
    while step < levels:
        run = run + jnp.where(lane >= step, pltpu.roll(run, step, 1), 0.0)
        step *= 2
    want = w_ref[span:, :]
    block = place_ref[0] // 128 * 8 + place_ref[0] % 64 // 8
    cosine = cosines(block * span, span, total)
    stats = (
        run[span - 1 : span],
        jnp.max(run, axis=0, keepdims=True),
        jnp.min(run, axis=0, keepdims=True),
        jnp.sum(cosine * run, axis=0, keepdims=True),
        jnp.sum(cosine * run * run, axis=0, keepdims=True),
        jnp.sum(cosine * want, axis=0, keepdims=True),
        jnp.sum(cosine * run * want, axis=0, keepdims=True),
        jnp.sum(cosine * want * want, axis=0, keepdims=True),
    )
    for p in range(s_ref.shape[0]):
        for i, stat in enumerate(stats):
            s_ref[p, i : i + 1, :] = stat
    w_ref[0:span, :] = run
    for p in range(peers):

        @pl.when(place_ref[0] % 8 == p)
        def _():
            mine_ref[...] = w_ref[p * rows : (p + 1) * rows, :]


def add_block(so_far, block, weight):
    s, hi, lo, run1, run2, want1, cross, want2 = block
    if so_far is None:
        return block
    off = so_far[0]
    return (
        off + s,
        jnp.maximum(so_far[1], off + hi),
        jnp.minimum(so_far[2], off + lo),
        so_far[3] + (run1 + off * weight),
        so_far[4] + (run2 + 2.0 * off * run1 + off * off * weight),
        so_far[5] + want1,
        so_far[6] + (cross + off * want1),
        so_far[7] + want2,
    )


def half_kernel(total, span, place_ref, mine_ref, s_ref, own_ref, half_ref):
    blocks = s_ref.shape[0]
    here = place_ref[0] % 64 // 8
    north = place_ref[0] // 128 == 1
    stats = None
    offset = jnp.zeros((1, s_ref.shape[2]), F32)
    for z in range(blocks):
        if z:
            offset = jnp.where(here == z, stats[0], offset)
        weights = [weight_of((h * blocks + z) * span, span, total) for h in range(2)]
        weight = jnp.where(north, weights[1], weights[0])
        stats = add_block(stats, [s_ref[z, i : i + 1, :] for i in range(8)], weight)
    own_ref[...] = mine_ref[...] + offset
    for i, stat in enumerate(stats):
        half_ref[i : i + 1, :] = stat


def finish_kernel(total, place_ref, own_ref, near_ref, far_ref, psi_ref, loss_ref):
    _, samples, levels = psi_ref.shape
    north = place_ref[0] // 128 == 1
    near = near_ref[...]
    far = far_ref[...]
    south_half = jnp.where(north, far, near)
    north_half = jnp.where(north, near, far)
    weight = weight_of(total // 2, total // 2, total)
    stats = add_block(
        [south_half[i : i + 1] for i in range(8)], [north_half[i : i + 1] for i in range(8)], weight
    )
    peak = jnp.max(jnp.maximum(jnp.abs(stats[1]), jnp.abs(stats[2])), axis=1, keepdims=True)
    scale = peak + EPSILON
    psi = (own_ref[...] + jnp.where(north, far[0:1], 0.0)) / scale
    for b in range(samples):
        psi_ref[:, b, :] = psi[:, b * levels : (b + 1) * levels]
    a, b, c = (jnp.sum(stats[i], axis=1, keepdims=True) for i in (4, 6, 7))
    loss = (a / scale / scale - 2.0 * (b / scale) + c) / (samples * levels * total)
    loss_ref[...] = jnp.broadcast_to(loss, loss_ref.shape)


def small(body, out_shape, *args, scratch=(), after=None):
    many = isinstance(out_shape, tuple)
    specs = [SMEM] + [VMEM] * (len(args) - 1)
    if after is not None:
        plain, count = body, len(args)
        body = lambda *refs: plain(*refs[:count], *refs[count + 1 :])
        args += (after,)
        specs.append(ANY)
    return pl.pallas_call(
        body,
        out_shape=out_shape,
        in_specs=specs,
        out_specs=(VMEM,) * len(out_shape) if many else VMEM,
        scratch_shapes=scratch,
        compiler_params=params(2),
    )(*args)


def all_of(x, axes):
    return lax.all_to_all(x, axes, split_axis=0, concat_axis=0, tiled=True)


def floats(*shape):
    return jax.ShapeDtypeStruct(shape, F32)


def per_device(u, v, t, mask, depth, desired):
    bands, samples, levels, lon = v.shape
    width = samples * levels
    total = bands * lax.axis_size(LAT_LEV)
    half = lax.axis_index("lon")[None].astype(jnp.int32)
    place = lax.axis_index(("lat", "lon", "lev_0", "lev_1", "lev_2"))[None].astype(jnp.int32)
    across = [(0, 1), (1, 0)]
    table = jnp.asarray(half_table(lon), BF16)

    def swap(x):
        return lax.ppermute(x, "lon", across)

    sent = [pack(half, u, v, t, mask, GROUPS[0], True)]
    *rest, sums = send(half, u, v, t, mask, sent[0], GROUPS[1:])
    sent += rest
    got = [swap(sent[0])]
    by_lon = swap(sums)
    got += [swap(x) for x in rest]
    own = [pack(half, u, v, t, mask, group, False) for group in GROUPS]

    def both(g, after):
        far = waves(half, table, own[g], got[g], after, True, BF16)
        return far, waves(half, table, own[g], got[g], far, False, F32)

    peers = lax.axis_size(INNER)
    outer = lax.axis_size("lev_0")
    rows = small(
        lambda *refs: weigh_kernel(total, *refs),
        floats(peers, 16, width),
        place,
        sums,
        by_lon,
        depth[None],
        desired,
        after=own[0],
    )
    near_bands = all_of(rows, INNER)
    far0, near0 = both(0, rows)
    span = bands * peers
    mine, stats = small(
        lambda *refs: band_kernel(total, bands, levels, *refs),
        (floats(bands, width), floats(outer, 8, width)),
        place,
        near_bands,
        scratch=[pltpu.VMEM((2 * span, width), F32)],
        after=near0,
    )
    all_stats = all_of(stats, "lev_0")
    far1, near1 = both(1, stats)
    mine, near_half = small(
        lambda *refs: half_kernel(total, span, *refs),
        (floats(bands, width), floats(8, width)),
        place,
        mine,
        all_stats,
        after=far1,
    )
    far_half = lax.ppermute(near_half, "lat", across)
    far2, near2 = both(2, near_half)
    psi, loss = small(
        lambda *refs: finish_kernel(total, *refs),
        (floats(bands, samples, levels), floats(1, width)),
        place,
        mine,
        near_half,
        far_half,
        after=near2,
    )

    back = [swap(x) for x in (far0, far1, far2)]
    kept = [near0, near1, near2]
    outs = None
    for group, mine, far in zip(GROUPS, kept, back):
        outs = join(half, mine, far, outs, group, bands)
    heat, momentum = (jnp.transpose(x, (1, 0, 2)) for x in outs)
    return psi, heat, momentum, loss[0, 0]


def solution(mesh):
    torus = Mesh(
        mesh.devices.reshape(mesh.shape["lat"], mesh.shape["lon"], 8, 4, 2),
        ("lat", "lon", "lev_0", "lev_1", "lev_2"),
    )
    in_specs = (
        P(LAT_LEV, None, None, "lon"),
        P(LAT_LEV, None, None, "lon"),
        P(LAT_LEV, None, None, "lon"),
        P(LAT_LEV, None, "lon"),
        P(),
        P(LAT_LEV, None, None),
    )
    out_specs = (P(LAT_LEV, None, None), P("lon", LAT_LEV, None), P("lon", LAT_LEV, None), P())

    return jax.shard_map(
        per_device, mesh=torus, in_specs=in_specs, out_specs=out_specs, check_vma=False
    )
```

time: 186 us -> 90.9 us (0.49)
  blocking collectives: 117 us -> 0 us
  waiting for transfers between devices: 3.1 us -> 33.6 us
  Pallas kernels: 0 us -> 27.2 us
  matrix products: 25.1 us -> 0 us
  starting transfers between devices: 3.33 us -> 24.3 us
  between operations: 16.6 us -> 0.88 us
  other arithmetic: 12.4 us -> 0 us
  local copies, waits for them, and re-layouts: 7.7 us -> 3.84 us
    pmax x4 -> x0, blocking collectives: 44.6 us -> none  [one_axis_at_a_time(): return functools.reduce(lax.pmax, axes, array)]
    all_gather x4 -> x0, blocking collectives: 38.5 us -> none  [prefix_by_axis(): pieces = lax.all_gather(so_far, axis)]
    psum x4 -> x0, blocking collectives: 34.3 us -> none  [over_axes(): array = lax.psum(array, axis)]
    ppermute x0 -> x8, waiting for transfers between devices: none -> 31.3 us  [the longest x7 31.3 us: swap(): return lax.ppermute(x, 'lon', across)]
    pallas_call x0 -> x18, Pallas kernels: none -> 27.2 us  [the longest x6 9.8 us: waves(): pl.pallas_call(lambda *refs: wave_kernel(flip, *refs), out_shape=jax.Shap...]
    dot_general x1 -> x0, matrix products: 25.1 us -> none  [per_device(): lax.dot_general(waves_table, lax.all_gather(joined_arrays, 'lon', axis=3,...]
    all_to_all x1 -> x2, starting transfers between devices: 3.3 us -> 15.4 us  [all_of(): return lax.all_to_all(x, axes, split_axis=0, concat_axis=0, tiled=True)]
    ppermute x0 -> x8, starting transfers between devices: none -> 8.89 us  [the longest x7 6.44 us: swap(): return lax.ppermute(x, 'lon', across)]
  transfers between devices with their start and end apart: 2 -> 10, of which waited for: 1 -> 3; matrix products, arithmetic and copies ran while one was open for 2% -> 0% of each run, Pallas kernels for 0% -> 24%
where the time goes in v2:
time: 90.9 us; the launch traced here: 89.9 us
  waiting for transfers between devices  33.6 us (37%)
  Pallas kernels  27.2 us (30%)
  starting transfers between devices  24.3 us (27%)
  local copies, waits for them, and re-layouts  3.84 us (4%)
    ppermute x7, waiting for transfers between devices, swap(): return lax.ppermute(x, 'lon', across)  31.3 us
    all_to_all x2, starting transfers between devices, all_of(): return lax.all_to_all(x, axes, split_axis=0, concat_axis=0, tiled=True)  15.4 us
    pallas_call x6, Pallas kernels, waves(): pl.pallas_call(lambda *refs: wave_kernel(flip, *refs), out_shape=jax.Shap...  9.8 us
    pallas_call x4, Pallas kernels, pack(): pl.pallas_call(lambda *refs: pack_kernel(rows, flip, *refs), out_shape=ja...  7.86 us
    ppermute x7, starting transfers between devices, swap(): return lax.ppermute(x, 'lon', across)  6.44 us
    unnamed x26, local copies, waits for them, and re-layouts  3.84 us
    pallas_call x3, Pallas kernels, join(): pl.pallas_call(body, out_shape=(shape, shape), in_specs=specs, out_specs=...  3.83 us
    pallas_call x1, Pallas kernels, send(): pl.pallas_call(lambda *refs: send_kernel(groups, *refs), out_shape=(*(jax...  3.09 us
  transfers between devices with their start and end apart: 10, of which 3 were waited for; matrix products, arithmetic and copies ran while one was open for 0% of the time, Pallas kernels for 24%

profile of v2, /device:TPU:1, one launch (start us, length us, event | category | flops | bytes accessed | tf_op | source)
XLA Modules:
  0.0 89.9 jit_solution(3136394558849994510)
XLA Ops:
  0.6 1.8 %pack.4.refs_5_ = bf16[1,192,720]{2,1,0:T(8,128)(2,1)} custom-call(s32[1]{0:T(128)} %bitcast.1.refs_0_.h, bf16[5,4,32,720]{3,2,1,0:T(8,128)(2,1)} %refs_1_.15, bf16[5,4,32,720]{3,2,1,0:T(8,128)(2,1)} %refs_2_.9, bf16[5,4,32,720]{3,2,1,0:T(8,128)(2,1)} %refs_3_.9, s32[5,32,720]{2,1,0:T(8,128)} %refs_4_.11), custom_call_target="tpu_custom_call" | custom-call | tf_op jit(solution)/shard_map/pack/pallas_call | solution.py:73
  2.4 3.1 %send.1 = (bf16[2,192,720]{2,1,0:T(8,128)(2,1)}, bf16[2,192,720]{2,1,0:T(8,128)(2,1)}, f32[10,128]{1,0:T(8,128)}) custom-call(s32[1]{0:T(128)} %bitcast.1.refs_0_.h, bf16[5,4,32,720]{3,2,1,0:T(8,128)(2,1)} %refs_1_.15, bf16[5,4,32,720]{3,2,1,0:T(8,128)(2,1)} %refs_2_.9, bf16[5,4,32,720]{3,2,1,0:T(8,128)(2,1)} %refs_3_.9, s32[5,32,720]{2,1,0:T(8,128)} %refs_4_.11, ...), custom_call_target="tpu_custom_call" | custom-call | tf_op jit(solution)/shard_map/send/pallas_call | solution.py:131
  5.6 2.1 %collective-permute-start.2 = (bf16[2,192,720]{2,1,0:T(8,128)(2,1)}, bf16[2,192,720]{2,1,0:T(8,128)(2,1)S(1)}, u32[]{:S(2)}, u32[]{:S(2)}) collective-permute-start(bf16[2,192,720]{2,1,0:T(8,128)(2,1)} %get-tuple-element.22), channel_id=1, source_target_pairs={{0,64},{64,0},{1,65},{65,1},{2,66},{66,2},{3,67},{67,3},{4,68},{68... | collective-permute-start | bytes 1658888 | tf_op jit(solution)/shard_map/ppermute | solution.py:386
  7.8 1.4 %collective-permute-start.1 = (bf16[1,192,720]{2,1,0:T(8,128)(2,1)}, bf16[1,192,720]{2,1,0:T(8,128)(2,1)S(1)}, u32[]{:S(2)}, u32[]{:S(2)}) collective-permute-start(bf16[1,192,720]{2,1,0:T(8,128)(2,1)} %pack.4.refs_5_), channel_id=1, source_target_pairs={{0,64},{64,0},{1,65},{65,1},{2,66},{66,2},{3,67},{67,3},{4,68},{68... | collective-permute-start | bytes 829448 | tf_op jit(solution)/shard_map/ppermute | solution.py:386
  9.3 1.8 %pack.5.refs_5_.refs_2_ = bf16[1,192,720]{2,1,0:T(8,128)(2,1)} custom-call(s32[1]{0:T(128)} %bitcast.1.refs_0_.h, bf16[5,4,32,720]{3,2,1,0:T(8,128)(2,1)} %refs_1_.15, bf16[5,4,32,720]{3,2,1,0:T(8,128)(2,1)} %refs_2_.9, bf16[5,4,32,720]{3,2,1,0:T(8,128)(2,1)} %refs_3_.9, s32[5,32,720]{2,1,0:T(8,128)} %refs_4_.11), custom_call_target="tpu_custom_call" | custom-call | tf_op jit(solution)/shard_map/pack/pallas_call | solution.py:73
  11.1 27.7 %collective-permute-done.refs_2_ = f32[10,128]{1,0:T(8,128)S(1)} collective-permute-done((f32[10,128]{1,0:T(8,128)}, f32[10,128]{1,0:T(8,128)S(1)}, u32[]{:S(2)}, u32[]{:S(2)}) %collective-permute-start) | collective-permute-done | bytes 5152 | tf_op jit(solution)/shard_map/ppermute | solution.py:386
  38.8 1.0 %copy-done.4 = bf16[1,192,720]{2,1,0:T(8,128)(2,1)S(1)} copy-done((bf16[1,192,720]{2,1,0:T(8,128)(2,1)S(1)}, bf16[1,192,720]{2,1,0:T(8,128)(2,1)}, u32[]{:S(2)}) %copy-start.4) | copy-done | bytes 276504
  40.5 7.2 %all-to-all-start = ((f32[8,16,128]{2,1,0:T(8,128)}), f32[8,16,128]{2,1,0:T(8,128)S(1)}, u32[]{:S(2)}, u32[]{:S(2)}) async-start(f32[8,16,128]{2,1,0:T(8,128)} %shard_map.102.refs_4_), calls=%async_computation | async-start | bytes 131072 | tf_op jit(solution)/shard_map/all_to_all | solution.py:369
  50.3 2.3 %all-to-all-done.refs_1_ = f32[8,16,128]{2,1,0:T(8,128)S(1)} async-done(((f32[8,16,128]{2,1,0:T(8,128)}), f32[8,16,128]{2,1,0:T(8,128)S(1)}, u32[]{:S(2)}, u32[]{:S(2)}) %all-to-all-start) | async-done | bytes 65568 | tf_op jit(solution)/shard_map/all_to_all | solution.py:369
  52.6 1.1 %shard_map.103 = (f32[5,128]{1,0:T(8,128)S(1)}, f32[8,8,128]{2,1,0:T(8,128)}) custom-call(s32[1]{0:T(128)} %bitcast.refs_0_, f32[8,16,128]{2,1,0:T(8,128)S(1)} %all-to-all-done.refs_1_, f32[1,360,128]{2,1,0:T(8,128)S(1)} %waves.7.refs_2_.a), custom_call_target="tpu_custom_call" | custom-call | tf_op jit(solution)/shard_map/pallas_call | solution.py:358
  53.7 8.2 %all-to-all-start.1 = ((f32[8,8,128]{2,1,0:T(8,128)}), f32[8,8,128]{2,1,0:T(8,128)S(1)}, u32[]{:S(2)}, u32[]{:S(2)}) async-start(f32[8,8,128]{2,1,0:T(8,128)} %get-tuple-element.21.refs_4_), calls=%async_computation.1 | async-start | bytes 65536 | tf_op jit(solution)/shard_map/all_to_all | solution.py:369
  61.9 2.1 %pack.7.refs_2_ = bf16[2,192,720]{2,1,0:T(8,128)(2,1)} custom-call(s32[1]{0:T(128)} %bitcast.1.refs_0_.h, bf16[5,4,32,720]{3,2,1,0:T(8,128)(2,1)} %refs_1_.15, bf16[5,4,32,720]{3,2,1,0:T(8,128)(2,1)} %refs_2_.9, bf16[5,4,32,720]{3,2,1,0:T(8,128)(2,1)} %refs_3_.9, s32[5,32,720]{2,1,0:T(8,128)} %refs_4_.11), custom_call_target="tpu_custom_call" | custom-call | tf_op jit(solution)/shard_map/pack/pallas_call | solution.py:73
  64.0 2.1 %pack.6.refs_2_ = bf16[2,192,720]{2,1,0:T(8,128)(2,1)} custom-call(s32[1]{0:T(128)} %bitcast.1.refs_0_.h, bf16[5,4,32,720]{3,2,1,0:T(8,128)(2,1)} %refs_1_.15, bf16[5,4,32,720]{3,2,1,0:T(8,128)(2,1)} %refs_2_.9, bf16[5,4,32,720]{3,2,1,0:T(8,128)(2,1)} %refs_3_.9, s32[5,32,720]{2,1,0:T(8,128)} %refs_4_.11), custom_call_target="tpu_custom_call" | custom-call | tf_op jit(solution)/shard_map/pack/pallas_call | solution.py:73
  66.2 1.1 %copy-done.1 = bf16[2,192,720]{2,1,0:T(8,128)(2,1)S(1)} copy-done((bf16[2,192,720]{2,1,0:T(8,128)(2,1)S(1)}, bf16[2,192,720]{2,1,0:T(8,128)(2,1)}, u32[]{:S(2)}) %copy-start.1) | copy-done | bytes 552984
  67.2 2.0 %waves.8.refs_3_.refs_4_ = bf16[2,360,128]{2,1,0:T(8,128)(2,1)} custom-call(s32[1]{0:T(128)} %bitcast.1.refs_0_.h, bf16[2,720,720]{2,1,0:T(8,128)(2,1)S(1)} %copy-done, bf16[2,192,720]{2,1,0:T(8,128)(2,1)S(1)} %copy-done.1, bf16[2,192,720]{2,1,0:T(8,128)(2,1)S(1)} %collective-permute-done.2.refs_3_, f32[8,8,128]{2,1,0:T(8,128)} %get-tuple-element.21.refs_4_), custom_call_target="tpu_custom_call" | custom-call | tf_op jit(solution)/shard_map/waves/pallas_call | solution.py:172
  70.1 1.2 %collective-permute-start.6 = (bf16[2,360,128]{2,1,0:T(8,128)(2,1)}, bf16[2,360,128]{2,1,0:T(8,128)(2,1)}, u32[]{:S(2)}, u32[]{:S(2)}) collective-permute-start(bf16[2,360,128]{2,1,0:T(8,128)(2,1)} %waves.8.refs_3_.refs_4_), channel_id=1, source_target_pairs={{0,64},{64,0},{1,65},{65,1},{2,66},{66,2},{3,67},{67,3},{4,68},{68... | collective-permute-start | bytes 552968 | tf_op jit(solution)/shard_map/ppermute | solution.py:386
  71.4 2.5 %waves.9.refs_4_ = bf16[2,360,128]{2,1,0:T(8,128)(2,1)S(1)} custom-call(s32[1]{0:T(128)} %bitcast.1.refs_0_.h, bf16[2,720,720]{2,1,0:T(8,128)(2,1)S(1)} %copy-done, bf16[2,192,720]{2,1,0:T(8,128)(2,1)S(1)} %copy-done.3, bf16[2,192,720]{2,1,0:T(8,128)(2,1)} %collective-permute-done.4.refs_3_, f32[8,128]{1,0:T(8,128)S(1)} %get-tuple-element.24.refs_4_.refs_2_), custom_call_target="tpu_custom_call" | custom-call | tf_op jit(solution)/shard_map/waves/pallas_call | solution.py:172
  74.2 1.2 %collective-permute-start.7 = (bf16[1,360,128]{2,1,0:T(8,128)(2,1)S(1)}, bf16[1,360,128]{2,1,0:T(8,128)(2,1)S(1)}, u32[]{:S(2)}, u32[]{:S(2)}) collective-permute-start(bf16[1,360,128]{2,1,0:T(8,128)(2,1)S(1)} %waves.6.refs_4_), channel_id=1, source_target_pairs={{0,64},{64,0},{1,65},{65,1},{2,66},{66,2},{3,67},{67,3},{4,68},{68... | collective-permute-start | bytes 276488 | tf_op jit(solution)/shard_map/ppermute | solution.py:386
  75.4 2.5 %collective-permute-start.3 = (f32[8,128]{1,0:T(8,128)S(1)}, f32[8,128]{1,0:T(8,128)S(1)}, u32[]{:S(2)}, u32[]{:S(2)}) collective-permute-start(f32[8,128]{1,0:T(8,128)S(1)} %get-tuple-element.24.refs_4_.refs_2_), channel_id=1, source_target_pairs={{0,128},{128,0},{1,129},{129,1},{2,130},{130,2},{3,131},{131,3},{4... | collective-permute-start | bytes 12296 | tf_op jit(solution)/shard_map/ppermute | solution.py:433
  77.8 3.6 %collective-permute-done.7.b = bf16[1,360,128]{2,1,0:T(8,128)(2,1)S(1)} collective-permute-done((bf16[1,360,128]{2,1,0:T(8,128)(2,1)S(1)}, bf16[1,360,128]{2,1,0:T(8,128)(2,1)S(1)}, u32[]{:S(2)}, u32[]{:S(2)}) %collective-permute-start.7) | collective-permute-done | bytes 92192 | tf_op jit(solution)/shard_map/ppermute | solution.py:386
  82.3 1.3 %waves.11.refs_1_ = f32[2,360,128]{2,1,0:T(8,128)S(1)} custom-call(s32[1]{0:T(128)} %bitcast.1.refs_0_.h, bf16[2,720,720]{2,1,0:T(8,128)(2,1)S(1)} %copy-done, bf16[2,192,720]{2,1,0:T(8,128)(2,1)S(1)} %copy-done.2, bf16[2,192,720]{2,1,0:T(8,128)(2,1)S(1)} %copy-done.7, bf16[2,360,128]{2,1,0:T(8,128)(2,1)} %waves.8.refs_3_.refs_4_), custom_call_target="tpu_custom_call" | custom-call | tf_op jit(solution)/shard_map/waves/pallas_call | solution.py:172
  83.7 2.4 %waves.10.refs_4_.refs_1_ = f32[2,360,128]{2,1,0:T(8,128)S(1)} custom-call(s32[1]{0:T(128)} %bitcast.1.refs_0_.h, bf16[2,720,720]{2,1,0:T(8,128)(2,1)S(1)} %copy-done, bf16[2,192,720]{2,1,0:T(8,128)(2,1)S(1)} %copy-done.3, bf16[2,192,720]{2,1,0:T(8,128)(2,1)} %collective-permute-done.4.refs_3_, bf16[2,360,128]{2,1,0:T(8,128)(2,1)S(1)} %waves.9.refs_4_), custom_call_target="tpu_custom_call" | custom-call | tf_op jit(solution)/shard_map/waves/pallas_call | solution.py:172
  86.9 1.9 %join.4 = (f32[5,360,128]{2,1,0:T(8,128)}, f32[5,360,128]{2,1,0:T(8,128)}) custom-call(s32[1]{0:T(128)} %bitcast.1.refs_0_.h, f32[2,360,128]{2,1,0:T(8,128)S(1)} %waves.11.refs_1_, bf16[2,360,128]{2,1,0:T(8,128)(2,1)} %collective-permute-done.6.refs_2_, f32[5,360,128]{2,1,0:T(8,128)} %get-tuple-element.27.refs_3_, ...), custom_call_target="tpu_custom_call", output_to_operand_aliasing={{0}: (3, {}), {1}: (4, {})} | custom-call | tf_op jit(solution)/shard_map/join/pallas_call | solution.py:216
  88.8 1.0 %join.5 = (f32[5,360,128]{2,1,0:T(8,128)}, f32[5,360,128]{2,1,0:T(8,128)}) custom-call(s32[1]{0:T(128)} %bitcast.1.refs_0_.h, f32[2,360,128]{2,1,0:T(8,128)S(1)} %waves.10.refs_4_.refs_1_, bf16[2,360,128]{2,1,0:T(8,128)(2,1)S(1)} %collective-permute-done.5.refs_2_, ...), custom_call_target="tpu_custom_call", output_to_operand_aliasing={{0}: (3, {}), {1}: (4, {})} | custom-call | tf_op jit(solution)/shard_map/join/pallas_call | solution.py:216
  (40 shorter events, 6.3 us)
Async XLA Ops:
  5.5 33.3 %copy-start.10 = (f32[5,4,32]{2,1,0:T(4,128)S(1)}, f32[5,4,32]{2,1,0:T(4,128)}, u32[]{:S(2)}) copy-start(f32[5,4,32]{2,1,0:T(4,128)} %refs_4_.9) | copy-start | bytes 7684
  5.5 33.3 %copy-start.11 = (f32[10,128]{1,0:T(8,128)S(1)}, f32[10,128]{1,0:T(8,128)}, u32[]{:S(2)}) copy-start(f32[10,128]{1,0:T(8,128)} %get-tuple-element.19.refs_1_) | copy-start | bytes 15364
  5.6 33.3 %copy-start.12 = (f32[32]{0:T(128)S(1)}, f32[32]{0:T(128)}, u32[]{:S(2)}) copy-start(f32[32]{0:T(128)} %param.11) | copy-start | bytes 388
  5.6 42.2 %copy-start = (bf16[2,720,720]{2,1,0:T(8,128)(2,1)S(1)}, bf16[2,720,720]{2,1,0:T(8,128)(2,1)}, u32[]{:S(2)}) copy-start(bf16[2,720,720]{2,1,0:T(8,128)(2,1)} %constant.29.clone.refs_1_) | copy-start | bytes 6220804
  5.6 60.6 %collective-permute-start.2 = (bf16[2,192,720]{2,1,0:T(8,128)(2,1)}, bf16[2,192,720]{2,1,0:T(8,128)(2,1)S(1)}, u32[]{:S(2)}, u32[]{:S(2)}) collective-permute-start(bf16[2,192,720]{2,1,0:T(8,128)(2,1)} %get-tuple-element.22), channel_id=1, source_target_pairs={{0,64},{64,0},{1,65},{65,1},{2,66},{66,2},{3,67},{67,3},{4,68},{68... | collective-permute-start | bytes 1658888 | tf_op jit(solution)/shard_map/ppermute | solution.py:386
  7.7 63.6 %collective-permute-start.4 = (bf16[2,192,720]{2,1,0:T(8,128)(2,1)}, bf16[2,192,720]{2,1,0:T(8,128)(2,1)}, u32[]{:S(2)}, u32[]{:S(2)}) collective-permute-start(bf16[2,192,720]{2,1,0:T(8,128)(2,1)} %get-tuple-element.25), channel_id=1, source_target_pairs={{0,64},{64,0},{1,65},{65,1},{2,66},{66,2},{3,67},{67,3},{4,68},{68... | collective-permute-start | bytes 1658888 | tf_op jit(solution)/shard_map/ppermute | solution.py:386
  7.8 39.9 %collective-permute-start.1 = (bf16[1,192,720]{2,1,0:T(8,128)(2,1)}, bf16[1,192,720]{2,1,0:T(8,128)(2,1)S(1)}, u32[]{:S(2)}, u32[]{:S(2)}) collective-permute-start(bf16[1,192,720]{2,1,0:T(8,128)(2,1)} %pack.4.refs_5_), channel_id=1, source_target_pairs={{0,64},{64,0},{1,65},{65,1},{2,66},{66,2},{3,67},{67,3},{4,68},{68... | collective-permute-start | bytes 829448 | tf_op jit(solution)/shard_map/ppermute | solution.py:386
  9.2 29.7 %collective-permute-start = (f32[10,128]{1,0:T(8,128)}, f32[10,128]{1,0:T(8,128)S(1)}, u32[]{:S(2)}, u32[]{:S(2)}) collective-permute-start(f32[10,128]{1,0:T(8,128)} %get-tuple-element.19.refs_1_), channel_id=1, source_target_pairs={{0,64},{64,0},{1,65},{65,1},{2,66},{66,2},{3,67},{67,3},{4,68},{68... | collective-permute-start | bytes 15368 | tf_op jit(solution)/shard_map/ppermute | solution.py:386
  38.8 1.0 %copy-start.4 = (bf16[1,192,720]{2,1,0:T(8,128)(2,1)S(1)}, bf16[1,192,720]{2,1,0:T(8,128)(2,1)}, u32[]{:S(2)}) copy-start(bf16[1,192,720]{2,1,0:T(8,128)(2,1)} %pack.5.refs_5_.refs_2_) | copy-start | bytes 829444
  40.5 12.1 %all-to-all-start = ((f32[8,16,128]{2,1,0:T(8,128)}), f32[8,16,128]{2,1,0:T(8,128)S(1)}, u32[]{:S(2)}, u32[]{:S(2)}) async-start(f32[8,16,128]{2,1,0:T(8,128)} %shard_map.102.refs_4_), calls=%async_computation | async-start | bytes 131072 | tf_op jit(solution)/shard_map/all_to_all | solution.py:369
  47.7 1.0 %copy-start.5 = (bf16[1,192,720]{2,1,0:T(8,128)(2,1)S(1)}, bf16[1,192,720]{2,1,0:T(8,128)(2,1)}, u32[]{:S(2)}) copy-start(bf16[1,192,720]{2,1,0:T(8,128)(2,1)} %pack.5.refs_5_.refs_2_) | copy-start | bytes 829444
  50.3 15.9 %copy-start.8 = (f32[1,360,128]{2,1,0:T(8,128)}, f32[1,360,128]{2,1,0:T(8,128)S(1)}, u32[]{:S(2)}) copy-start(f32[1,360,128]{2,1,0:T(8,128)S(1)} %waves.7.refs_2_.a) | copy-start | bytes 552964
  53.7 17.6 %all-to-all-start.1 = ((f32[8,8,128]{2,1,0:T(8,128)}), f32[8,8,128]{2,1,0:T(8,128)S(1)}, u32[]{:S(2)}, u32[]{:S(2)}) async-start(f32[8,8,128]{2,1,0:T(8,128)} %get-tuple-element.21.refs_4_), calls=%async_computation.1 | async-start | bytes 65536 | tf_op jit(solution)/shard_map/all_to_all | solution.py:369
  66.2 1.1 %copy-start.1 = (bf16[2,192,720]{2,1,0:T(8,128)(2,1)S(1)}, bf16[2,192,720]{2,1,0:T(8,128)(2,1)}, u32[]{:S(2)}) copy-start(bf16[2,192,720]{2,1,0:T(8,128)(2,1)} %pack.6.refs_2_) | copy-start | bytes 1658884
  67.2 4.1 %copy-start.3 = (bf16[2,192,720]{2,1,0:T(8,128)(2,1)S(1)}, bf16[2,192,720]{2,1,0:T(8,128)(2,1)}, u32[]{:S(2)}) copy-start(bf16[2,192,720]{2,1,0:T(8,128)(2,1)} %pack.7.refs_2_) | copy-start | bytes 1658884
  69.3 0.8 copy-start.6
  70.1 12.2 %copy-start.2 = (bf16[2,192,720]{2,1,0:T(8,128)(2,1)S(1)}, bf16[2,192,720]{2,1,0:T(8,128)(2,1)}, u32[]{:S(2)}) copy-start(bf16[2,192,720]{2,1,0:T(8,128)(2,1)} %pack.6.refs_2_) | copy-start | bytes 1658884
  70.1 16.8 %collective-permute-start.6 = (bf16[2,360,128]{2,1,0:T(8,128)(2,1)}, bf16[2,360,128]{2,1,0:T(8,128)(2,1)}, u32[]{:S(2)}, u32[]{:S(2)}) collective-permute-start(bf16[2,360,128]{2,1,0:T(8,128)(2,1)} %waves.8.refs_3_.refs_4_), channel_id=1, source_target_pairs={{0,64},{64,0},{1,65},{65,1},{2,66},{66,2},{3,67},{67,3},{4,68},{68... | collective-permute-start | bytes 552968 | tf_op jit(solution)/shard_map/ppermute | solution.py:386
  71.3 10.1 %copy-start.9 = (f32[1,360,128]{2,1,0:T(8,128)S(1)}, f32[1,360,128]{2,1,0:T(8,128)}, u32[]{:S(2)}) copy-start(f32[1,360,128]{2,1,0:T(8,128)} %copy-done.8) | copy-start | bytes 552964
  71.3 11.0 %copy-start.7 = (bf16[2,192,720]{2,1,0:T(8,128)(2,1)S(1)}, bf16[2,192,720]{2,1,0:T(8,128)(2,1)}, u32[]{:S(2)}) copy-start(bf16[2,192,720]{2,1,0:T(8,128)(2,1)} %copy-done.6) | copy-start | bytes 1658884
  73.8 15.0 %collective-permute-start.5 = (bf16[2,360,128]{2,1,0:T(8,128)(2,1)S(1)}, bf16[2,360,128]{2,1,0:T(8,128)(2,1)S(1)}, u32[]{:S(2)}, u32[]{:S(2)}) collective-permute-start(bf16[2,360,128]{2,1,0:T(8,128)(2,1)S(1)} %waves.9.refs_4_), channel_id=1, source_target_pairs={{0,64},{64,0},{1,65},{65,1},{2,66},{66,2},{3,67},{67,3},{4,68},{68... | collective-permute-start | bytes 552968 | tf_op jit(solution)/shard_map/ppermute | solution.py:386
  74.2 7.2 %collective-permute-start.7 = (bf16[1,360,128]{2,1,0:T(8,128)(2,1)S(1)}, bf16[1,360,128]{2,1,0:T(8,128)(2,1)S(1)}, u32[]{:S(2)}, u32[]{:S(2)}) collective-permute-start(bf16[1,360,128]{2,1,0:T(8,128)(2,1)S(1)} %waves.6.refs_4_), channel_id=1, source_target_pairs={{0,64},{64,0},{1,65},{65,1},{2,66},{66,2},{3,67},{67,3},{4,68},{68... | collective-permute-start | bytes 276488 | tf_op jit(solution)/shard_map/ppermute | solution.py:386
  75.4 10.7 %collective-permute-start.3 = (f32[8,128]{1,0:T(8,128)S(1)}, f32[8,128]{1,0:T(8,128)S(1)}, u32[]{:S(2)}, u32[]{:S(2)}) collective-permute-start(f32[8,128]{1,0:T(8,128)S(1)} %get-tuple-element.24.refs_4_.refs_2_), channel_id=1, source_target_pairs={{0,128},{128,0},{1,129},{129,1},{2,130},{130,2},{3,131},{131,3},{4... | collective-permute-start | bytes 12296 | tf_op jit(solution)/shard_map/ppermute | solution.py:433

commit v3 on v2

--- a/solution.py
+++ b/solution.py
@@ -86,62 +86,78 @@
 
 
 def send_kernel(groups, half_ref, u_ref, v_ref, t_ref, m_ref, _, *rest):
-    outs, (sums_ref, us, vs, ts, masks, sems) = rest[: len(groups)], rest[len(groups) :]
+    n = len(groups)
+    far_refs, near_refs, sums_ref = rest[: n - 1], rest[n - 1 : 2 * n - 1], rest[2 * n - 1]
+    us, vs, ts, masks, fars, nears, sems, out_sems = rest[2 * n :]
     rows, samples, levels, lon = vs.shape
     part = samples // 2
     size = part * levels
-    far = 1 - half_ref[0]
-    wanted = [row for group in groups for row in group]
-    copies = {}
+    near = half_ref[0]
+    far = 1 - near
+    copies = []
     for j in range(rows):
         group = [
             pltpu.make_async_copy(m_ref.at[j], masks.at[j], sems.at[j, 0]),
             pltpu.make_async_copy(v_ref.at[j], vs.at[j], sems.at[j, 1]),
+            pltpu.make_async_copy(u_ref.at[j], us.at[j], sems.at[j, 2]),
+            pltpu.make_async_copy(t_ref.at[j], ts.at[j], sems.at[j, 3]),
         ]
-        if j in wanted:
-            at = pl.ds(far * part, part)
-            group.append(pltpu.make_async_copy(u_ref.at[j, at], us.at[j], sems.at[j, 2]))
-            group.append(pltpu.make_async_copy(t_ref.at[j, at], ts.at[j], sems.at[j, 3]))
         for c in group:
             c.start()
-        copies[j] = group
+        copies.append(group)
     ones = jnp.ones((8, lon), BF16)
-    for j in range(rows):
-        for c in copies[j]:
-            c.wait()
-        keep = keep_of(masks[j])
-        v = (vs[j] * keep[None]).reshape(samples * levels, lon)
-        sums_ref[j : j + 1, :] = lax.dot_general(ones, v, CONTRACT, preferred_element_type=F32)[0:1]
-        full = jnp.broadcast_to(keep[None], (samples, levels, lon)).reshape(samples * levels, lon)
-        sums_ref[rows + j : rows + j + 1, :] = lax.dot_general(
-            ones, full, CONTRACT, preferred_element_type=F32
-        )[0:1]
-        for g, group in enumerate(groups):
-            if j in group:
-                i = group.index(j)
-                outs[g][i, 0:size, :] = (ts[j] * keep[None]).reshape(size, lon)
-                outs[g][i, size : 2 * size, :] = (us[j] * keep[None]).reshape(size, lon)
-                mine = vs[j, pl.ds(far * part, part)] * keep[None]
-                outs[g][i, 2 * size :, :] = mine.reshape(size, lon)
+    done = []
+    for g, group in enumerate(groups):
+        for i, j in enumerate(group):
+            for c in copies[j]:
+                c.wait()
+            keep = keep_of(masks[j])
+            v = (vs[j] * keep[None]).reshape(samples * levels, lon)
+            sums_ref[j : j + 1, :] = lax.dot_general(
+                ones, v, CONTRACT, preferred_element_type=F32
+            )[0:1]
+            full = jnp.broadcast_to(keep[None], (samples, levels, lon)).reshape(-1, lon)
+            sums_ref[rows + j : rows + j + 1, :] = lax.dot_general(
+                ones, full, CONTRACT, preferred_element_type=F32
+            )[0:1]
+            for k, (where, box) in enumerate(((far, fars), (near, nears))):
+                if k == 0 and g == 0:
+                    continue
+                ref = far_refs[g - 1] if k == 0 else near_refs[g]
+                for f, field in enumerate((ts, us, vs)):
+                    mine = field[j, pl.ds(where * part, part)] * keep[None]
+                    box[j, f * size : (f + 1) * size, :] = mine.reshape(size, lon)
+                c = pltpu.make_async_copy(box.at[j], ref.at[i], out_sems.at[j, k])
+                c.start()
+                done.append(c)
+    for c in done:
+        c.wait()
 
 
 def send(half, u, v, t, mask, after, groups):
     rows, samples, levels, lon = v.shape
     part = samples // 2
+    unit = 3 * part * levels
+    n = len(groups)
+    packed = [jax.ShapeDtypeStruct((len(g), unit, lon), BF16) for g in groups]
     return pl.pallas_call(
         lambda *refs: send_kernel(groups, *refs),
         out_shape=(
-            *(jax.ShapeDtypeStruct((len(g), 3 * part * levels, lon), BF16) for g in groups),
+            *packed[1:],
+            *packed,
             jax.ShapeDtypeStruct((2 * rows, samples * levels), F32),
         ),
         in_specs=[SMEM, HBM, HBM, HBM, HBM, ANY],
-        out_specs=(VMEM,) * (len(groups) + 1),
+        out_specs=(HBM,) * (2 * n - 1) + (VMEM,),
         scratch_shapes=[
-            pltpu.VMEM((rows, part, levels, lon), BF16),
             pltpu.VMEM((rows, samples, levels, lon), BF16),
-            pltpu.VMEM((rows, part, levels, lon), BF16),
+            pltpu.VMEM((rows, samples, levels, lon), BF16),
+            pltpu.VMEM((rows, samples, levels, lon), BF16),
             pltpu.VMEM((rows, levels, lon), jnp.int32),
+            pltpu.VMEM((rows, unit, lon), BF16),
+            pltpu.VMEM((rows, unit, lon), BF16),
             pltpu.SemaphoreType.DMA((rows, 4)),
+            pltpu.SemaphoreType.DMA((rows, 2)),
         ],
         compiler_params=params(60),
         name="send",
@@ -179,42 +195,44 @@
     )(half, table, own, got, after)
 
 
-def join_kernel(first, half_ref, own_ref, got_ref, heat_in, mom_in, heat_ref, mom_ref, heat, mom, sems):
+def join_kernel(first, parts, half_ref, *refs):
+    own_refs, got_refs = refs[:parts], refs[parts : 2 * parts]
+    heat_ref, mom_ref, heat, mom, sems = refs[-5:]
     copies = []
-    for i in range(own_ref.shape[0]):
-        own = own_ref[i]
-        got = got_ref[i].astype(F32)
-        zero = half_ref[0] == 0
-        a = jnp.where(zero, own, got)
-        b = jnp.where(zero, got, own)
-        w = own.shape[1] // 2
-        low = lax.broadcasted_iota(jnp.int32, own.shape, 1) < w
-        heat[i] = jnp.where(low, a, pltpu.roll(b, w, 1))
-        mom[i] = jnp.where(low, pltpu.roll(a, w, 1), b)
-        for k, (x, ref) in enumerate(((heat, heat_ref), (mom, mom_ref))):
-            c = pltpu.make_async_copy(x.at[i], ref.at[first + i], sems.at[i, k])
-            c.start()
-            copies.append(c)
+    at = 0
+    for own_ref, got_ref in zip(own_refs, got_refs):
+        for i in range(own_ref.shape[0]):
+            own = own_ref[i]
+            got = got_ref[i].astype(F32)
+            zero = half_ref[0] == 0
+            a = jnp.where(zero, own, got)
+            b = jnp.where(zero, got, own)
+            w = own.shape[1] // 2
+            low = lax.broadcasted_iota(jnp.int32, own.shape, 1) < w
+            heat[at] = jnp.where(low, a, pltpu.roll(b, w, 1))
+            mom[at] = jnp.where(low, pltpu.roll(a, w, 1), b)
+            for k, (x, ref) in enumerate(((heat, heat_ref), (mom, mom_ref))):
+                c = pltpu.make_async_copy(x.at[at], ref.at[first + at], sems.at[at, k])
+                c.start()
+                copies.append(c)
+            at += 1
     for c in copies:
         c.wait()
 
 
 def join(half, own, got, outs, rows, total):
-    n, width = own.shape[1:]
+    n, width = own[0].shape[1:]
     shape = jax.ShapeDtypeStruct((total, n, width), F32)
-    args = (half, own, got)
-    specs = [SMEM, VMEM, VMEM]
+    parts = len(own)
+    args = (half, *own, *got)
+    specs = [SMEM] + [VMEM] * (2 * parts)
     extra = {}
-    first = rows[0]
-    if outs is None:
-        body = lambda h, a, b, *refs: join_kernel(first, h, a, b, None, None, *refs)
-    else:
-        body = lambda *refs: join_kernel(first, *refs)
+    if outs is not None:
+        extra = {"input_output_aliases": {len(args): 0, len(args) + 1: 1}}
         args += outs
         specs += [HBM, HBM]
-        extra = {"input_output_aliases": {3: 0, 4: 1}}
     return pl.pallas_call(
-        body,
+        lambda *refs: join_kernel(rows[0], parts, *refs),
         out_shape=(shape, shape),
         in_specs=specs,
         out_specs=(HBM, HBM),
@@ -385,13 +403,12 @@
     def swap(x):
         return lax.ppermute(x, "lon", across)
 
-    sent = [pack(half, u, v, t, mask, GROUPS[0], True)]
-    *rest, sums = send(half, u, v, t, mask, sent[0], GROUPS[1:])
-    sent += rest
-    got = [swap(sent[0])]
+    first = pack(half, u, v, t, mask, GROUPS[0], True)
+    *packed, sums = send(half, u, v, t, mask, first, GROUPS)
+    rest, own = packed[: len(GROUPS) - 1], packed[len(GROUPS) - 1 :]
+    got = [swap(first)]
     by_lon = swap(sums)
     got += [swap(x) for x in rest]
-    own = [pack(half, u, v, t, mask, group, False) for group in GROUPS]
 
     def both(g, after):
         far = waves(half, table, own[g], got[g], after, True, BF16)
@@ -407,7 +424,6 @@
         by_lon,
         depth[None],
         desired,
-        after=own[0],
     )
     near_bands = all_of(rows, INNER)
     far0, near0 = both(0, rows)
@@ -428,7 +444,7 @@
         place,
         mine,
         all_stats,
-        after=far1,
+        after=near1,
     )
     far_half = lax.ppermute(near_half, "lat", across)
     far2, near2 = both(2, near_half)
@@ -444,9 +460,8 @@
 
     back = [swap(x) for x in (far0, far1, far2)]
     kept = [near0, near1, near2]
-    outs = None
-    for group, mine, far in zip(GROUPS, kept, back):
-        outs = join(half, mine, far, outs, group, bands)
+    outs = join(half, kept[:2], back[:2], None, GROUPS[0] + GROUPS[1], bands)
+    outs = join(half, kept[2:], back[2:], outs, GROUPS[2], bands)
     heat, momentum = (jnp.transpose(x, (1, 0, 2)) for x in outs)
     return psi, heat, momentum, loss[0, 0]
 

time: 90.9 us -> 87.3 us (0.960)
  Pallas kernels: 27.2 us -> 23.5 us
    pallas_call x4 -> x1, Pallas kernels: 7.86 us -> 1.83 us  [pack(): pl.pallas_call(lambda *refs: pack_kernel(rows, flip, *refs), out_shape=ja...]
    ppermute x7, waiting for transfers between devices: 31.3 us -> 29.6 us  [swap(): return lax.ppermute(x, 'lon', across)]
    pallas_call x6, Pallas kernels: 9.8 us -> 11.2 us  [waves(): pl.pallas_call(lambda *refs: wave_kernel(flip, *refs), out_shape=jax.Shap...]
    ppermute x1, waiting for transfers between devices: 0.01 us -> 1.32 us  [per_device(): far_half = lax.ppermute(near_half, 'lat', across)]
    unnamed x26 -> x20, local copies, waits for them, and re-layouts: 3.84 us -> 3.39 us
    pallas_call x4 -> x3, Pallas kernels: 6.91 us -> 7.1 us  [the longest x1 4.01 us: send(): pl.pallas_call(lambda *refs: send_kernel(groups, *refs), out_shape=(*pack...]
  transfers between devices with their start and end apart: 10 -> 10, of which waited for: 3 -> 4; matrix products, arithmetic and copies ran while one was open for 0% -> 0% of each run, Pallas kernels for 24% -> 19%
where the time goes in v3:
time: 87.3 us; the launch traced here: 85.8 us
  waiting for transfers between devices  33.4 us (38%)
  starting transfers between devices  24.7 us (28%)
  Pallas kernels  23.5 us (27%)
  local copies, waits for them, and re-layouts  3.39 us (4%)
    ppermute x7, waiting for transfers between devices, swap(): return lax.ppermute(x, 'lon', across)  29.6 us
    all_to_all x2, starting transfers between devices, all_of(): return lax.all_to_all(x, axes, split_axis=0, concat_axis=0, tiled=True)  15.4 us
    pallas_call x6, Pallas kernels, waves(): pl.pallas_call(lambda *refs: wave_kernel(flip, *refs), out_shape=jax.Shap...  11.2 us
    ppermute x7, starting transfers between devices, swap(): return lax.ppermute(x, 'lon', across)  6.53 us
    pallas_call x1, Pallas kernels, send(): pl.pallas_call(lambda *refs: send_kernel(groups, *refs), out_shape=(*pack...  4.01 us
    pallas_call x4, Pallas kernels, small(): pl.pallas_call(body, out_shape=out_shape, in_specs=specs, out_specs=(VMEM...  3.39 us
    unnamed x20, local copies, waits for them, and re-layouts  3.39 us
    pallas_call x2, Pallas kernels, join(): pl.pallas_call(lambda *refs: join_kernel(rows[0], parts, *refs), out_shap...  3.09 us
  transfers between devices with their start and end apart: 10, of which 4 were waited for; matrix products, arithmetic and copies ran while one was open for 0% of the time, Pallas kernels for 19%

profile of v3, /device:TPU:1, one launch (start us, length us, event | category | flops | bytes accessed | tf_op | source)
XLA Modules:
  0.0 85.8 jit_solution(3317640114424416109)
XLA Ops:
  0.6 1.8 %pack.1.refs_5_ = bf16[1,192,720]{2,1,0:T(8,128)(2,1)} custom-call(s32[1]{0:T(128)} %bitcast.1.refs_0_, bf16[5,4,32,720]{3,2,1,0:T(8,128)(2,1)} %refs_1_.9, bf16[5,4,32,720]{3,2,1,0:T(8,128)(2,1)} %refs_2_.3, bf16[5,4,32,720]{3,2,1,0:T(8,128)(2,1)} %refs_3_.3, s32[5,32,720]{2,1,0:T(8,128)} %refs_4_.4), custom_call_target="tpu_custom_call" | custom-call | tf_op jit(solution)/shard_map/pack/pallas_call | solution.py:73
  2.5 4.0 %send.1 = (bf16[2,192,720]{2,1,0:T(8,128)(2,1)}, bf16[2,192,720]{2,1,0:T(8,128)(2,1)}, bf16[1,192,720]{2,1,0:T(8,128)(2,1)}, bf16[2,192,720]{2,1,0:T(8,128)(2,1)...) custom-call(s32[1]{0:T(128)} %bitcast.1.refs_0_, bf16[5,4,32,720]{3,2,1,0:T(8,128)(2,1)} %refs_1_.9, ...), custom_call_target="tpu_custom_call" | custom-call | tf_op jit(solution)/shard_map/send/pallas_call | solution.py:143
  6.5 2.1 %collective-permute-start.2 = (bf16[2,192,720]{2,1,0:T(8,128)(2,1)}, bf16[2,192,720]{2,1,0:T(8,128)(2,1)}, u32[]{:S(2)}, u32[]{:S(2)}) collective-permute-start(bf16[2,192,720]{2,1,0:T(8,128)(2,1)} %get-tuple-element.25), channel_id=1, source_target_pairs={{0,64},{64,0},{1,65},{65,1},{2,66},{66,2},{3,67},{67,3},{4,68},{68... | collective-permute-start | bytes 1658888 | tf_op jit(solution)/shard_map/ppermute | solution.py:404
  8.8 1.4 %collective-permute-start.1 = (bf16[1,192,720]{2,1,0:T(8,128)(2,1)S(1)}, bf16[1,192,720]{2,1,0:T(8,128)(2,1)S(1)}, u32[]{:S(2)}, u32[]{:S(2)}) collective-permute-start(bf16[1,192,720]{2,1,0:T(8,128)(2,1)S(1)} %copy-done.9), channel_id=1, source_target_pairs={{0,64},{64,0},{1,65},{65,1},{2,66},{66,2},{3,67},{67,3},{4,68},{68... | collective-permute-start | bytes 829448 | tf_op jit(solution)/shard_map/ppermute | solution.py:404
  10.2 29.6 %collective-permute-done.refs_2_ = f32[10,128]{1,0:T(8,128)S(1)} collective-permute-done((f32[10,128]{1,0:T(8,128)}, f32[10,128]{1,0:T(8,128)S(1)}, u32[]{:S(2)}, u32[]{:S(2)}) %collective-permute-start) | collective-permute-done | bytes 5152 | tf_op jit(solution)/shard_map/ppermute | solution.py:404
  41.2 7.2 %all-to-all-start = ((f32[8,16,128]{2,1,0:T(8,128)}), f32[8,16,128]{2,1,0:T(8,128)S(1)}, u32[]{:S(2)}, u32[]{:S(2)}) async-start(f32[8,16,128]{2,1,0:T(8,128)} %shard_map.102.refs_4_), calls=%async_computation | async-start | bytes 131072 | tf_op jit(solution)/shard_map/all_to_all | solution.py:387
  48.4 1.0 %copy-done.3 = bf16[1,192,720]{2,1,0:T(8,128)(2,1)S(1)} copy-done((bf16[1,192,720]{2,1,0:T(8,128)(2,1)S(1)}, bf16[1,192,720]{2,1,0:T(8,128)(2,1)}, u32[]{:S(2)}) %copy-start.3) | copy-done | bytes 276504
  51.6 1.7 %all-to-all-done.refs_1_ = f32[8,16,128]{2,1,0:T(8,128)S(1)} async-done(((f32[8,16,128]{2,1,0:T(8,128)}), f32[8,16,128]{2,1,0:T(8,128)S(1)}, u32[]{:S(2)}, u32[]{:S(2)}) %all-to-all-start) | async-done | bytes 65568 | tf_op jit(solution)/shard_map/all_to_all | solution.py:387
  53.3 1.1 %shard_map.103 = (f32[5,128]{1,0:T(8,128)S(1)}, f32[8,8,128]{2,1,0:T(8,128)}) custom-call(s32[1]{0:T(128)} %bitcast.refs_0_, f32[8,16,128]{2,1,0:T(8,128)S(1)} %all-to-all-done.refs_1_, f32[1,360,128]{2,1,0:T(8,128)S(1)} %waves.7.refs_2_.refs_1_), custom_call_target="tpu_custom_call" | custom-call | tf_op jit(solution)/shard_map/pallas_call | solution.py:376
  54.4 8.2 %all-to-all-start.1 = ((f32[8,8,128]{2,1,0:T(8,128)}), f32[8,8,128]{2,1,0:T(8,128)}, u32[]{:S(2)}, u32[]{:S(2)}) async-start(f32[8,8,128]{2,1,0:T(8,128)} %get-tuple-element.23.refs_4_), calls=%async_computation.1 | async-start | bytes 65536 | tf_op jit(solution)/shard_map/all_to_all | solution.py:387
  62.6 2.4 %waves.8.refs_4_ = bf16[2,360,128]{2,1,0:T(8,128)(2,1)S(1)} custom-call(s32[1]{0:T(128)} %bitcast.1.refs_0_, bf16[2,720,720]{2,1,0:T(8,128)(2,1)S(1)} %copy-done, bf16[2,192,720]{2,1,0:T(8,128)(2,1)S(1)} %copy-done.1, bf16[2,192,720]{2,1,0:T(8,128)(2,1)} %collective-permute-done.2.refs_3_, f32[8,8,128]{2,1,0:T(8,128)} %get-tuple-element.23.refs_4_), custom_call_target="tpu_custom_call" | custom-call | tf_op jit(solution)/shard_map/waves/pallas_call | solution.py:188
  65.0 1.3 %collective-permute-start.7 = (bf16[2,360,128]{2,1,0:T(8,128)(2,1)S(1)}, bf16[2,360,128]{2,1,0:T(8,128)(2,1)}, u32[]{:S(2)}, u32[]{:S(2)}) collective-permute-start(bf16[2,360,128]{2,1,0:T(8,128)(2,1)S(1)} %waves.8.refs_4_), channel_id=1, source_target_pairs={{0,64},{64,0},{1,65},{65,1},{2,66},{66,2},{3,67},{67,3},{4,68},{68... | collective-permute-start | bytes 552968 | tf_op jit(solution)/shard_map/ppermute | solution.py:404
  66.3 2.4 %waves.9.refs_3_.refs_2_ = f32[2,360,128]{2,1,0:T(8,128)S(1)} custom-call(s32[1]{0:T(128)} %bitcast.1.refs_0_, bf16[2,720,720]{2,1,0:T(8,128)(2,1)S(1)} %copy-done, bf16[2,192,720]{2,1,0:T(8,128)(2,1)S(1)} %copy-done.1, bf16[2,192,720]{2,1,0:T(8,128)(2,1)} %collective-permute-done.2.refs_3_, bf16[2,360,128]{2,1,0:T(8,128)(2,1)S(1)} %waves.8.refs_4_), custom_call_target="tpu_custom_call" | custom-call | tf_op jit(solution)/shard_map/waves/pallas_call | solution.py:188
  68.7 0.8 all-to-all-done.1.refs_2_
  69.5 0.8 shard_map.104
  70.3 1.1 %copy-done.2 = bf16[2,192,720]{2,1,0:T(8,128)(2,1)S(1)} copy-done((bf16[2,192,720]{2,1,0:T(8,128)(2,1)S(1)}, bf16[2,192,720]{2,1,0:T(8,128)(2,1)}, u32[]{:S(2)}) %copy-start.2) | copy-done | bytes 552984
  71.4 2.4 %waves.10.refs_4_ = bf16[2,360,128]{2,1,0:T(8,128)(2,1)S(1)} custom-call(s32[1]{0:T(128)} %bitcast.1.refs_0_, bf16[2,720,720]{2,1,0:T(8,128)(2,1)S(1)} %copy-done, bf16[2,192,720]{2,1,0:T(8,128)(2,1)S(1)} %copy-done.2, bf16[2,192,720]{2,1,0:T(8,128)(2,1)} %collective-permute-done.4.refs_3_, f32[8,128]{1,0:T(8,128)S(1)} %get-tuple-element.27.refs_4_.refs_2_), custom_call_target="tpu_custom_call" | custom-call | tf_op jit(solution)/shard_map/waves/pallas_call | solution.py:188
  73.8 1.3 %collective-permute-start.5 = (bf16[2,360,128]{2,1,0:T(8,128)(2,1)S(1)}, bf16[2,360,128]{2,1,0:T(8,128)(2,1)S(1)}, u32[]{:S(2)}, u32[]{:S(2)}) collective-permute-start(bf16[2,360,128]{2,1,0:T(8,128)(2,1)S(1)} %waves.10.refs_4_), channel_id=1, source_target_pairs={{0,64},{64,0},{1,65},{65,1},{2,66},{66,2},{3,67},{67,3},{4,68},{68... | collective-permute-start | bytes 552968 | tf_op jit(solution)/shard_map/ppermute | solution.py:404
  75.4 2.7 %collective-permute-start.3 = (f32[8,128]{1,0:T(8,128)S(1)}, f32[8,128]{1,0:T(8,128)S(1)}, u32[]{:S(2)}, u32[]{:S(2)}) collective-permute-start(f32[8,128]{1,0:T(8,128)S(1)} %get-tuple-element.27.refs_4_.refs_2_), channel_id=1, source_target_pairs={{0,128},{128,0},{1,129},{129,1},{2,130},{130,2},{3,131},{131,3},{4... | collective-permute-start | bytes 12296 | tf_op jit(solution)/shard_map/ppermute | solution.py:449
  78.1 2.4 %waves.11.refs_4_.refs_1_ = f32[2,360,128]{2,1,0:T(8,128)S(1)} custom-call(s32[1]{0:T(128)} %bitcast.1.refs_0_, bf16[2,720,720]{2,1,0:T(8,128)(2,1)S(1)} %copy-done, bf16[2,192,720]{2,1,0:T(8,128)(2,1)S(1)} %copy-done.2, bf16[2,192,720]{2,1,0:T(8,128)(2,1)} %collective-permute-done.4.refs_3_, bf16[2,360,128]{2,1,0:T(8,128)(2,1)S(1)} %waves.10.refs_4_), custom_call_target="tpu_custom_call" | custom-call | tf_op jit(solution)/shard_map/waves/pallas_call | solution.py:188
  80.5 1.3 %collective-permute-done.3.refs_3_ = f32[8,128]{1,0:T(8,128)S(1)} collective-permute-done((f32[8,128]{1,0:T(8,128)S(1)}, f32[8,128]{1,0:T(8,128)S(1)}, u32[]{:S(2)}, u32[]{:S(2)}) %collective-permute-start.3) | collective-permute-done | bytes 4128 | tf_op jit(solution)/shard_map/ppermute | solution.py:449
  81.9 0.8 shard_map.105
  82.7 2.1 %join.2 = (f32[5,360,128]{2,1,0:T(8,128)}, f32[5,360,128]{2,1,0:T(8,128)}) custom-call(s32[1]{0:T(128)} %bitcast.1.refs_0_, f32[1,360,128]{2,1,0:T(8,128)S(1)} %waves.7.refs_2_.refs_1_, f32[2,360,128]{2,1,0:T(8,128)S(1)} %waves.9.refs_3_.refs_2_, bf16[1,360,128]{2,1,0:T(8,128)(2,1)S(1)} %collective-permute-done.6.refs_3_, ...), custom_call_target="tpu_custom_call" | custom-call | tf_op jit(solution)/shard_map/join/pallas_call | solution.py:234
  84.7 1.0 %join.3 = (f32[5,360,128]{2,1,0:T(8,128)}, f32[5,360,128]{2,1,0:T(8,128)}) custom-call(s32[1]{0:T(128)} %bitcast.1.refs_0_, f32[2,360,128]{2,1,0:T(8,128)S(1)} %waves.11.refs_4_.refs_1_, bf16[2,360,128]{2,1,0:T(8,128)(2,1)S(1)} %collective-permute-done.5.refs_2_, ...), custom_call_target="tpu_custom_call", output_to_operand_aliasing={{0}: (3, {}), {1}: (4, {})} | custom-call | tf_op jit(solution)/shard_map/join/pallas_call | solution.py:234
  (30 shorter events, 4.1 us)
Async XLA Ops:
  2.5 6.3 %copy-start.9 = (bf16[1,192,720]{2,1,0:T(8,128)(2,1)S(1)}, bf16[1,192,720]{2,1,0:T(8,128)(2,1)}, u32[]{:S(2)}) copy-start(bf16[1,192,720]{2,1,0:T(8,128)(2,1)} %pack.1.refs_5_) | copy-start | bytes 829444
  2.5 37.3 %copy-start.6 = (f32[5,4,32]{2,1,0:T(4,128)S(1)}, f32[5,4,32]{2,1,0:T(4,128)}, u32[]{:S(2)}) copy-start(f32[5,4,32]{2,1,0:T(4,128)} %refs_4_.5) | copy-start | bytes 7684
  2.5 37.3 %copy-start.8 = (f32[32]{0:T(128)S(1)}, f32[32]{0:T(128)}, u32[]{:S(2)}) copy-start(f32[32]{0:T(128)} %param.11) | copy-start | bytes 388
  2.5 45.9 %copy-start = (bf16[2,720,720]{2,1,0:T(8,128)(2,1)S(1)}, bf16[2,720,720]{2,1,0:T(8,128)(2,1)}, u32[]{:S(2)}) copy-start(bf16[2,720,720]{2,1,0:T(8,128)(2,1)} %constant.29.clone.refs_1_) | copy-start | bytes 6220804
  6.5 56.0 %collective-permute-start.2 = (bf16[2,192,720]{2,1,0:T(8,128)(2,1)}, bf16[2,192,720]{2,1,0:T(8,128)(2,1)}, u32[]{:S(2)}, u32[]{:S(2)}) collective-permute-start(bf16[2,192,720]{2,1,0:T(8,128)(2,1)} %get-tuple-element.25), channel_id=1, source_target_pairs={{0,64},{64,0},{1,65},{65,1},{2,66},{66,2},{3,67},{67,3},{4,68},{68... | collective-permute-start | bytes 1658888 | tf_op jit(solution)/shard_map/ppermute | solution.py:404
  8.7 61.7 %collective-permute-start.4 = (bf16[2,192,720]{2,1,0:T(8,128)(2,1)}, bf16[2,192,720]{2,1,0:T(8,128)(2,1)}, u32[]{:S(2)}, u32[]{:S(2)}) collective-permute-start(bf16[2,192,720]{2,1,0:T(8,128)(2,1)} %get-tuple-element.29), channel_id=1, source_target_pairs={{0,64},{64,0},{1,65},{65,1},{2,66},{66,2},{3,67},{67,3},{4,68},{68... | collective-permute-start | bytes 1658888 | tf_op jit(solution)/shard_map/ppermute | solution.py:404
  8.8 39.7 %collective-permute-start.1 = (bf16[1,192,720]{2,1,0:T(8,128)(2,1)S(1)}, bf16[1,192,720]{2,1,0:T(8,128)(2,1)S(1)}, u32[]{:S(2)}, u32[]{:S(2)}) collective-permute-start(bf16[1,192,720]{2,1,0:T(8,128)(2,1)S(1)} %copy-done.9), channel_id=1, source_target_pairs={{0,64},{64,0},{1,65},{65,1},{2,66},{66,2},{3,67},{67,3},{4,68},{68... | collective-permute-start | bytes 829448 | tf_op jit(solution)/shard_map/ppermute | solution.py:404
  10.1 29.7 %collective-permute-start = (f32[10,128]{1,0:T(8,128)}, f32[10,128]{1,0:T(8,128)S(1)}, u32[]{:S(2)}, u32[]{:S(2)}) collective-permute-start(f32[10,128]{1,0:T(8,128)} %get-tuple-element.20.refs_1_), channel_id=1, source_target_pairs={{0,64},{64,0},{1,65},{65,1},{2,66},{66,2},{3,67},{67,3},{4,68},{68... | collective-permute-start | bytes 15368 | tf_op jit(solution)/shard_map/ppermute | solution.py:404
  39.8 0.7 copy-start.7
  41.2 12.1 %all-to-all-start = ((f32[8,16,128]{2,1,0:T(8,128)}), f32[8,16,128]{2,1,0:T(8,128)S(1)}, u32[]{:S(2)}, u32[]{:S(2)}) async-start(f32[8,16,128]{2,1,0:T(8,128)} %shard_map.102.refs_4_), calls=%async_computation | async-start | bytes 131072 | tf_op jit(solution)/shard_map/all_to_all | solution.py:387
  48.4 1.0 %copy-start.3 = (bf16[1,192,720]{2,1,0:T(8,128)(2,1)S(1)}, bf16[1,192,720]{2,1,0:T(8,128)(2,1)}, u32[]{:S(2)}) copy-start(bf16[1,192,720]{2,1,0:T(8,128)(2,1)} %get-tuple-element.21.refs_2_) | copy-start | bytes 829444
  50.2 12.4 %copy-start.1 = (bf16[2,192,720]{2,1,0:T(8,128)(2,1)S(1)}, bf16[2,192,720]{2,1,0:T(8,128)(2,1)}, u32[]{:S(2)}) copy-start(bf16[2,192,720]{2,1,0:T(8,128)(2,1)} %get-tuple-element.24.refs_2_) | copy-start | bytes 1658884
  51.0 0.7 copy-start.4
  54.4 15.2 %all-to-all-start.1 = ((f32[8,8,128]{2,1,0:T(8,128)}), f32[8,8,128]{2,1,0:T(8,128)}, u32[]{:S(2)}, u32[]{:S(2)}) async-start(f32[8,8,128]{2,1,0:T(8,128)} %get-tuple-element.23.refs_4_), calls=%async_computation.1 | async-start | bytes 65536 | tf_op jit(solution)/shard_map/all_to_all | solution.py:387
  65.0 17.7 %collective-permute-start.7 = (bf16[2,360,128]{2,1,0:T(8,128)(2,1)S(1)}, bf16[2,360,128]{2,1,0:T(8,128)(2,1)}, u32[]{:S(2)}, u32[]{:S(2)}) collective-permute-start(bf16[2,360,128]{2,1,0:T(8,128)(2,1)S(1)} %waves.8.refs_4_), channel_id=1, source_target_pairs={{0,64},{64,0},{1,65},{65,1},{2,66},{66,2},{3,67},{67,3},{4,68},{68... | collective-permute-start | bytes 552968 | tf_op jit(solution)/shard_map/ppermute | solution.py:404
  68.7 6.4 %copy-start.5 = (bf16[1,360,128]{2,1,0:T(8,128)(2,1)S(1)}, bf16[1,360,128]{2,1,0:T(8,128)(2,1)}, u32[]{:S(2)}) copy-start(bf16[1,360,128]{2,1,0:T(8,128)(2,1)} %copy-done.4) | copy-start | bytes 276484
  70.3 1.1 %copy-start.2 = (bf16[2,192,720]{2,1,0:T(8,128)(2,1)S(1)}, bf16[2,192,720]{2,1,0:T(8,128)(2,1)}, u32[]{:S(2)}) copy-start(bf16[2,192,720]{2,1,0:T(8,128)(2,1)} %get-tuple-element.28.refs_2_) | copy-start | bytes 1658884
  73.8 10.9 %collective-permute-start.5 = (bf16[2,360,128]{2,1,0:T(8,128)(2,1)S(1)}, bf16[2,360,128]{2,1,0:T(8,128)(2,1)S(1)}, u32[]{:S(2)}, u32[]{:S(2)}) collective-permute-start(bf16[2,360,128]{2,1,0:T(8,128)(2,1)S(1)} %waves.10.refs_4_), channel_id=1, source_target_pairs={{0,64},{64,0},{1,65},{65,1},{2,66},{66,2},{3,67},{67,3},{4,68},{68... | collective-permute-start | bytes 552968 | tf_op jit(solution)/shard_map/ppermute | solution.py:404
  75.1 7.5 %collective-permute-start.6 = (bf16[1,360,128]{2,1,0:T(8,128)(2,1)S(1)}, bf16[1,360,128]{2,1,0:T(8,128)(2,1)S(1)}, u32[]{:S(2)}, u32[]{:S(2)}) collective-permute-start(bf16[1,360,128]{2,1,0:T(8,128)(2,1)S(1)} %copy-done.5), channel_id=1, source_target_pairs={{0,64},{64,0},{1,65},{65,1},{2,66},{66,2},{3,67},{67,3},{4,68},{68... | collective-permute-start | bytes 276488 | tf_op jit(solution)/shard_map/ppermute | solution.py:404
  75.4 6.5 %collective-permute-start.3 = (f32[8,128]{1,0:T(8,128)S(1)}, f32[8,128]{1,0:T(8,128)S(1)}, u32[]{:S(2)}, u32[]{:S(2)}) collective-permute-start(f32[8,128]{1,0:T(8,128)S(1)} %get-tuple-element.27.refs_4_.refs_2_), channel_id=1, source_target_pairs={{0,128},{128,0},{1,129},{129,1},{2,130},{130,2},{3,131},{131,3},{4... | collective-permute-start | bytes 12296 | tf_op jit(solution)/shard_map/ppermute | solution.py:449

commit v4 on v3

--- a/solution.py
+++ b/solution.py
@@ -1,3 +1,4 @@
+import functools
 import math
 
 import jax
@@ -14,6 +15,7 @@
 ORDERS = 720
 LAT_LEV = ("lat", "lev_0", "lev_1", "lev_2")
 INNER = ("lev_1", "lev_2")
+OUTER = ("lat", "lev_0")
 EPSILON = 1e-06
 GROUPS = ((0,), (1, 2), (3, 4))
 F32 = jnp.float32
@@ -164,32 +166,34 @@
     )(half, u, v, t, mask, after)
 
 
-def wave_kernel(flip, half_ref, table_ref, own_ref, got_ref, _, o_ref):
+def wave_kernel(half_ref, table_ref, own_ref, got_ref, _, *o_refs, flips):
     def lay(x):
         return jnp.concatenate([x, x[2 * x.shape[0] // 3 :]])
 
-    table = table_ref[1 - half_ref[0] if flip else half_ref[0]]
-    n = table.shape[0] // 2
+    n = table_ref.shape[1] // 2
     odd = lax.broadcasted_iota(jnp.int32, (n, 1), 0) % 2 == 0
     sign = jnp.where(odd, -1.0, 1.0).astype(F32)
     scale = 2.0 / (MERIDIANS * MERIDIANS)
-    for i in range(got_ref.shape[0]):
-        near = lax.dot_general(table, lay(own_ref[i]), CONTRACT, preferred_element_type=F32)
-        far = lax.dot_general(table, lay(got_ref[i]), CONTRACT, preferred_element_type=F32)
-        cos = near[:n] + sign * far[:n]
-        sin = near[n:] + sign * far[n:]
-        w = cos.shape[1] // 2
-        both = cos[:, :w] * cos[:, w:] + sin[:, :w] * sin[:, w:]
-        o_ref[i] = (scale * both).astype(o_ref.dtype)
-
-
-def waves(half, table, own, got, after, flip, dtype):
+    for flip, o_ref in zip(flips, o_refs):
+        table = table_ref[1 - half_ref[0] if flip else half_ref[0]]
+        for i in range(got_ref.shape[0]):
+            near = lax.dot_general(table, lay(own_ref[i]), CONTRACT, preferred_element_type=F32)
+            far = lax.dot_general(table, lay(got_ref[i]), CONTRACT, preferred_element_type=F32)
+            cos = near[:n] + sign * far[:n]
+            sin = near[n:] + sign * far[n:]
+            w = cos.shape[1] // 2
+            both = cos[:, :w] * cos[:, w:] + sin[:, :w] * sin[:, w:]
+            o_ref[i] = (scale * both).astype(o_ref.dtype)
+
+
+def waves(half, table, own, got, after, *flips):
     rows, cols, _ = got.shape
+    shape = (rows, table.shape[1] // 2, 2 * cols // 3)
     return pl.pallas_call(
-        lambda *refs: wave_kernel(flip, *refs),
-        out_shape=jax.ShapeDtypeStruct((rows, table.shape[1] // 2, 2 * cols // 3), dtype),
+        functools.partial(wave_kernel, flips=flips),
+        out_shape=tuple(jax.ShapeDtypeStruct(shape, BF16 if f else F32) for f in flips),
         in_specs=[SMEM, VMEM, VMEM, VMEM, ANY],
-        out_specs=VMEM,
+        out_specs=(VMEM,) * len(flips),
         compiler_params=params(16),
         name="waves",
     )(half, table, own, got, after)
@@ -327,37 +331,21 @@
     )
 
 
-def half_kernel(total, span, place_ref, mine_ref, s_ref, own_ref, half_ref):
+def finish_kernel(total, span, place_ref, mine_ref, s_ref, psi_ref, loss_ref):
+    _, samples, levels = psi_ref.shape
     blocks = s_ref.shape[0]
-    here = place_ref[0] % 64 // 8
-    north = place_ref[0] // 128 == 1
+    here = place_ref[0] // 128 * (blocks // 2) + place_ref[0] % 64 // 8
     stats = None
     offset = jnp.zeros((1, s_ref.shape[2]), F32)
     for z in range(blocks):
         if z:
             offset = jnp.where(here == z, stats[0], offset)
-        weights = [weight_of((h * blocks + z) * span, span, total) for h in range(2)]
-        weight = jnp.where(north, weights[1], weights[0])
-        stats = add_block(stats, [s_ref[z, i : i + 1, :] for i in range(8)], weight)
-    own_ref[...] = mine_ref[...] + offset
-    for i, stat in enumerate(stats):
-        half_ref[i : i + 1, :] = stat
-
-
-def finish_kernel(total, place_ref, own_ref, near_ref, far_ref, psi_ref, loss_ref):
-    _, samples, levels = psi_ref.shape
-    north = place_ref[0] // 128 == 1
-    near = near_ref[...]
-    far = far_ref[...]
-    south_half = jnp.where(north, far, near)
-    north_half = jnp.where(north, near, far)
-    weight = weight_of(total // 2, total // 2, total)
-    stats = add_block(
-        [south_half[i : i + 1] for i in range(8)], [north_half[i : i + 1] for i in range(8)], weight
-    )
+        stats = add_block(
+            stats, [s_ref[z, i : i + 1, :] for i in range(8)], weight_of(z * span, span, total)
+        )
     peak = jnp.max(jnp.maximum(jnp.abs(stats[1]), jnp.abs(stats[2])), axis=1, keepdims=True)
     scale = peak + EPSILON
-    psi = (own_ref[...] + jnp.where(north, far[0:1], 0.0)) / scale
+    psi = (mine_ref[...] + offset) / scale
     for b in range(samples):
         psi_ref[:, b, :] = psi[:, b * levels : (b + 1) * levels]
     a, b, c = (jnp.sum(stats[i], axis=1, keepdims=True) for i in (4, 6, 7))
@@ -410,12 +398,8 @@
     by_lon = swap(sums)
     got += [swap(x) for x in rest]
 
-    def both(g, after):
-        far = waves(half, table, own[g], got[g], after, True, BF16)
-        return far, waves(half, table, own[g], got[g], far, False, F32)
-
     peers = lax.axis_size(INNER)
-    outer = lax.axis_size("lev_0")
+    outer = lax.axis_size(OUTER)
     rows = small(
         lambda *refs: weigh_kernel(total, *refs),
         floats(peers, 16, width),
@@ -426,7 +410,8 @@
         desired,
     )
     near_bands = all_of(rows, INNER)
-    far0, near0 = both(0, rows)
+    far0, near0 = waves(half, table, own[0], got[0], rows, True, False)
+    far1, near1 = waves(half, table, own[1], got[1], near0, True, False)
     span = bands * peers
     mine, stats = small(
         lambda *refs: band_kernel(total, bands, levels, *refs),
@@ -434,27 +419,17 @@
         place,
         near_bands,
         scratch=[pltpu.VMEM((2 * span, width), F32)],
-        after=near0,
-    )
-    all_stats = all_of(stats, "lev_0")
-    far1, near1 = both(1, stats)
-    mine, near_half = small(
-        lambda *refs: half_kernel(total, span, *refs),
-        (floats(bands, width), floats(8, width)),
+        after=near1,
+    )
+    all_stats = all_of(stats, OUTER)
+    (far2,) = waves(half, table, own[2], got[2], stats, True)
+    (near2,) = waves(half, table, own[2], got[2], stats, False)
+    psi, loss = small(
+        lambda *refs: finish_kernel(total, span, *refs),
+        (floats(bands, samples, levels), floats(1, width)),
         place,
         mine,
         all_stats,
-        after=near1,
-    )
-    far_half = lax.ppermute(near_half, "lat", across)
-    far2, near2 = both(2, near_half)
-    psi, loss = small(
-        lambda *refs: finish_kernel(total, *refs),
-        (floats(bands, samples, levels), floats(1, width)),
-        place,
-        mine,
-        near_half,
-        far_half,
         after=near2,
     )
 

time: 87.3 us -> 89.3 us (1.023)
  waiting for transfers between devices: 33.4 us -> 35.7 us
  Pallas kernels: 23.5 us -> 25.1 us
  starting transfers between devices: 24.7 us -> 23.6 us
    all_to_all x2, waiting for transfers between devices: 2.48 us -> 6.1 us  [all_of(): return lax.all_to_all(x, axes, split_axis=0, concat_axis=0, tiled=True)]
    ppermute x1 -> x0, starting transfers between devices: 2.74 us -> none  [per_device(): far_half = lax.ppermute(near_half, 'lat', across)]
    all_to_all x2, starting transfers between devices: 15.4 us -> 18 us  [all_of(): return lax.all_to_all(x, axes, split_axis=0, concat_axis=0, tiled=True)]
    ppermute x1 -> x0, waiting for transfers between devices: 1.32 us -> none  [per_device(): far_half = lax.ppermute(near_half, 'lat', across)]
    ppermute x7, starting transfers between devices: 6.53 us -> 5.56 us  [swap(): return lax.ppermute(x, 'lon', across)]
    pallas_call x2, Pallas kernels: 3.09 us -> 4.05 us  [join(): pl.pallas_call(lambda *refs: join_kernel(rows[0], parts, *refs), out_shap...]
    pallas_call x4 -> x3, Pallas kernels: 3.39 us -> 4.31 us  [small(): pl.pallas_call(body, out_shape=out_shape, in_specs=specs, out_specs=(VMEM...]
    pallas_call x6 -> x4, Pallas kernels: 11.2 us -> 10.9 us  [waves(): pl.pallas_call(functools.partial(wave_kernel, flips=flips), out_shape=tup...]
  transfers between devices with their start and end apart: 10 -> 9, of which waited for: 4 -> 2; matrix products, arithmetic and copies ran while one was open for 0% -> 0% of each run, Pallas kernels for 19% -> 20%
where the time goes in v4:
time: 89.3 us; the launch traced here: 87.8 us
  waiting for transfers between devices  35.7 us (40%)
  Pallas kernels  25.1 us (28%)
  starting transfers between devices  23.6 us (26%)
  local copies, waits for them, and re-layouts  2.66 us (3%)
    ppermute x7, waiting for transfers between devices, swap(): return lax.ppermute(x, 'lon', across)  29.6 us
    all_to_all x2, starting transfers between devices, all_of(): return lax.all_to_all(x, axes, split_axis=0, concat_axis=0, tiled=True)  18 us
    pallas_call x4, Pallas kernels, waves(): pl.pallas_call(functools.partial(wave_kernel, flips=flips), out_shape=tup...  10.9 us
    all_to_all x2, waiting for transfers between devices, all_of(): return lax.all_to_all(x, axes, split_axis=0, concat_axis=0, tiled=True)  6.1 us
    ppermute x7, starting transfers between devices, swap(): return lax.ppermute(x, 'lon', across)  5.56 us
    pallas_call x3, Pallas kernels, small(): pl.pallas_call(body, out_shape=out_shape, in_specs=specs, out_specs=(VMEM...  4.31 us
    pallas_call x2, Pallas kernels, join(): pl.pallas_call(lambda *refs: join_kernel(rows[0], parts, *refs), out_shap...  4.05 us
    pallas_call x1, Pallas kernels, send(): pl.pallas_call(lambda *refs: send_kernel(groups, *refs), out_shape=(*pack...  4.02 us
  transfers between devices with their start and end apart: 9, of which 2 were waited for; matrix products, arithmetic and copies ran while one was open for 0% of the time, Pallas kernels for 20%

profile of v4, /device:TPU:1, one launch (start us, length us, event | category | flops | bytes accessed | tf_op | source)
XLA Modules:
  0.0 87.8 jit_solution(4841794365936855380)
XLA Ops:
  0.6 1.8 %pack.1.refs_5_ = bf16[1,192,720]{2,1,0:T(8,128)(2,1)} custom-call(s32[1]{0:T(128)} %bitcast.1.refs_0_.half_ref, bf16[5,4,32,720]{3,2,1,0:T(8,128)(2,1)} %refs_1_.3, bf16[5,4,32,720]{3,2,1,0:T(8,128)(2,1)} %refs_2_.3, bf16[5,4,32,720]{3,2,1,0:T(8,128)(2,1)} %refs_3_.3, s32[5,32,720]{2,1,0:T(8,128)} %refs_4_.4), custom_call_target="tpu_custom_call" | custom-call | tf_op jit(solution)/shard_map/pack/pallas_call | solution.py:75
  2.5 4.0 %send.1 = (bf16[2,192,720]{2,1,0:T(8,128)(2,1)}, bf16[2,192,720]{2,1,0:T(8,128)(2,1)}, bf16[1,192,720]{2,1,0:T(8,128)(2,1)}, bf16[2,192,720]{2,1,0:T(8,128)(2,1)...) custom-call(s32[1]{0:T(128)} %bitcast.1.refs_0_.half_ref, bf16[5,4,32,720]{3,2,1,0:T(8,128)(2,1)} %refs_1_.3, ...), custom_call_target="tpu_custom_call" | custom-call | tf_op jit(solution)/shard_map/send/pallas_call | solution.py:145
  6.6 2.1 %collective-permute-start.1 = (bf16[2,192,720]{2,1,0:T(8,128)(2,1)}, bf16[2,192,720]{2,1,0:T(8,128)(2,1)}, u32[]{:S(2)}, u32[]{:S(2)}) collective-permute-start(bf16[2,192,720]{2,1,0:T(8,128)(2,1)} %get-tuple-element.24), channel_id=1, source_target_pairs={{0,64},{64,0},{1,65},{65,1},{2,66},{66,2},{3,67},{67,3},{4,68},{68... | collective-permute-start | bytes 1658888 | tf_op jit(solution)/shard_map/ppermute | solution.py:392
  8.7 0.1 collective-permute-start.3
  8.8 1.4 %collective-permute-start.2 = (bf16[1,192,720]{2,1,0:T(8,128)(2,1)S(1)}, bf16[1,192,720]{2,1,0:T(8,128)(2,1)S(1)}, u32[]{:S(2)}, u32[]{:S(2)}) collective-permute-start(bf16[1,192,720]{2,1,0:T(8,128)(2,1)S(1)} %copy-done.9), channel_id=1, source_target_pairs={{0,64},{64,0},{1,65},{65,1},{2,66},{66,2},{3,67},{67,3},{4,68},{68... | collective-permute-start | bytes 829448 | tf_op jit(solution)/shard_map/ppermute | solution.py:392
  10.2 29.6 %collective-permute-done.refs_2_ = f32[10,128]{1,0:T(8,128)S(1)} collective-permute-done((f32[10,128]{1,0:T(8,128)}, f32[10,128]{1,0:T(8,128)S(1)}, u32[]{:S(2)}, u32[]{:S(2)}) %collective-permute-start) | collective-permute-done | bytes 5152 | tf_op jit(solution)/shard_map/ppermute | solution.py:392
  39.8 0.7 copy-done.7
  40.5 0.7 shard_map.102._
  41.2 7.2 %all-to-all-start = ((f32[8,16,128]{2,1,0:T(8,128)}), f32[8,16,128]{2,1,0:T(8,128)}, u32[]{:S(2)}, u32[]{:S(2)}) async-start(f32[8,16,128]{2,1,0:T(8,128)} %shard_map.102._), calls=%async_computation | async-start | bytes 131072 | tf_op jit(solution)/shard_map/all_to_all | solution.py:375
  48.5 1.0 %copy-done.5 = bf16[1,192,720]{2,1,0:T(8,128)(2,1)S(1)} copy-done((bf16[1,192,720]{2,1,0:T(8,128)(2,1)S(1)}, bf16[1,192,720]{2,1,0:T(8,128)(2,1)}, u32[]{:S(2)}) %copy-start.5) | copy-done | bytes 276504
  49.5 1.5 %waves.4 = (bf16[1,360,128]{2,1,0:T(8,128)(2,1)}, f32[1,360,128]{2,1,0:T(8,128)S(1)}) custom-call(s32[1]{0:T(128)} %bitcast.1.refs_0_.half_ref, bf16[2,720,720]{2,1,0:T(8,128)(2,1)S(1)} %copy-done, bf16[1,192,720]{2,1,0:T(8,128)(2,1)S(1)} %copy-done.5, bf16[1,192,720]{2,1,0:T(8,128)(2,1)S(1)} %collective-permute-done.2.got_ref, f32[8,16,128]{2,1,0:T(8,128)} %shard_map.102._), custom_call_target="tpu_custom_call" | custom-call | tf_op jit(solution)/shard_map/waves/pallas_call | solution.py:192
  51.0 3.9 %waves.5 = (bf16[2,360,128]{2,1,0:T(8,128)(2,1)}, f32[2,360,128]{2,1,0:T(8,128)S(1)}) custom-call(s32[1]{0:T(128)} %bitcast.1.refs_0_.half_ref, bf16[2,720,720]{2,1,0:T(8,128)(2,1)S(1)} %copy-done, bf16[2,192,720]{2,1,0:T(8,128)(2,1)S(1)} %copy-done.4, bf16[2,192,720]{2,1,0:T(8,128)(2,1)} %collective-permute-done.1.got_ref, ...), custom_call_target="tpu_custom_call" | custom-call | tf_op jit(solution)/shard_map/waves/pallas_call | solution.py:192
  54.9 1.2 %collective-permute-start.6 = (bf16[2,360,128]{2,1,0:T(8,128)(2,1)}, bf16[2,360,128]{2,1,0:T(8,128)(2,1)}, u32[]{:S(2)}, u32[]{:S(2)}) collective-permute-start(bf16[2,360,128]{2,1,0:T(8,128)(2,1)} %get-tuple-element.34), channel_id=1, source_target_pairs={{0,64},{64,0},{1,65},{65,1},{2,66},{66,2},{3,67},{67,3},{4,68},{68... | collective-permute-start | bytes 552968 | tf_op jit(solution)/shard_map/ppermute | solution.py:392
  56.1 2.0 %shard_map.103 = (f32[5,128]{1,0:T(8,128)S(1)}, f32[16,8,128]{2,1,0:T(8,128)}) custom-call(s32[1]{0:T(128)} %bitcast.refs_0_, f32[8,16,128]{2,1,0:T(8,128)} %all-to-all-done.refs_1_, f32[2,360,128]{2,1,0:T(8,128)S(1)} %get-tuple-element.27.refs_2_), custom_call_target="tpu_custom_call" | custom-call | tf_op jit(solution)/shard_map/pallas_call | solution.py:364
  58.1 3.1 %waves.7 = bf16[2,360,128]{2,1,0:T(8,128)(2,1)} custom-call(s32[1]{0:T(128)} %bitcast.1.refs_0_.half_ref, bf16[2,720,720]{2,1,0:T(8,128)(2,1)S(1)} %copy-done, bf16[2,192,720]{2,1,0:T(8,128)(2,1)S(1)} %copy-done.1, bf16[2,192,720]{2,1,0:T(8,128)(2,1)} %collective-permute-done.3.got_ref, f32[16,8,128]{2,1,0:T(8,128)} %get-tuple-element.29._), custom_call_target="tpu_custom_call" | custom-call | tf_op jit(solution)/shard_map/waves/pallas_call | solution.py:192
  61.2 0.2 collective-permute-start.4
  61.4 10.8 %all-to-all-start.1 = ((f32[16,8,128]{2,1,0:T(8,128)}), f32[16,8,128]{2,1,0:T(8,128)}, u32[]{:S(2)}, u32[]{:S(2)}) async-start(f32[16,8,128]{2,1,0:T(8,128)} %get-tuple-element.29._), calls=%async_computation.1 | async-start | bytes 131072 | tf_op jit(solution)/shard_map/all_to_all | solution.py:375
  72.2 0.4 collective-permute-start.5
  72.6 2.4 %waves.6.refs_3_.refs_1_ = f32[2,360,128]{2,1,0:T(8,128)S(1)} custom-call(s32[1]{0:T(128)} %bitcast.1.refs_0_.half_ref, bf16[2,720,720]{2,1,0:T(8,128)(2,1)S(1)} %copy-done, bf16[2,192,720]{2,1,0:T(8,128)(2,1)S(1)} %copy-done.1, bf16[2,192,720]{2,1,0:T(8,128)(2,1)} %collective-permute-done.3.got_ref, f32[16,8,128]{2,1,0:T(8,128)} %get-tuple-element.29._), custom_call_target="tpu_custom_call" | custom-call | tf_op jit(solution)/shard_map/waves/pallas_call | solution.py:192
  75.0 6.1 %all-to-all-done.1.refs_2_ = f32[16,8,128]{2,1,0:T(8,128)} async-done(((f32[16,8,128]{2,1,0:T(8,128)}), f32[16,8,128]{2,1,0:T(8,128)}, u32[]{:S(2)}, u32[]{:S(2)}) %all-to-all-start.1) | async-done | bytes 65568 | tf_op jit(solution)/shard_map/all_to_all | solution.py:375
  81.1 1.6 %shard_map.104 = (f32[5,4,32]{2,1,0:T(4,128)}, f32[1,128]{1,0:T(1,128)}) custom-call(s32[1]{0:T(128)} %bitcast.refs_0_, f32[5,128]{1,0:T(8,128)S(1)} %get-tuple-element.28.refs_1_, f32[16,8,128]{2,1,0:T(8,128)} %all-to-all-done.1.refs_2_, f32[2,360,128]{2,1,0:T(8,128)S(1)} %waves.6.refs_3_.refs_1_), custom_call_target="tpu_custom_call" | custom-call | tf_op jit(solution)/shard_map/pallas_call | solution.py:364
  82.8 0.9 %copy-done.3 = f32[1,360,128]{2,1,0:T(8,128)S(1)} copy-done((f32[1,360,128]{2,1,0:T(8,128)S(1)}, f32[1,360,128]{2,1,0:T(8,128)}, u32[]{:S(2)}) %copy-start.3) | copy-done | bytes 184344
  83.7 2.1 %join.2 = (f32[5,360,128]{2,1,0:T(8,128)}, f32[5,360,128]{2,1,0:T(8,128)}) custom-call(s32[1]{0:T(128)} %bitcast.1.refs_0_.half_ref, f32[1,360,128]{2,1,0:T(8,128)S(1)} %copy-done.3, f32[2,360,128]{2,1,0:T(8,128)S(1)} %get-tuple-element.27.refs_2_, bf16[1,360,128]{2,1,0:T(8,128)(2,1)} %collective-permute-done.5.refs_3_, ...), custom_call_target="tpu_custom_call" | custom-call | tf_op jit(solution)/shard_map/join/pallas_call | solution.py:238
  85.8 1.9 %join.3 = (f32[5,360,128]{2,1,0:T(8,128)}, f32[5,360,128]{2,1,0:T(8,128)}) custom-call(s32[1]{0:T(128)} %bitcast.1.refs_0_.half_ref, f32[2,360,128]{2,1,0:T(8,128)S(1)} %waves.6.refs_3_.refs_1_, bf16[2,360,128]{2,1,0:T(8,128)(2,1)} %collective-permute-done.4.refs_2_, ...), custom_call_target="tpu_custom_call", output_to_operand_aliasing={{0}: (3, {}), {1}: (4, {})} | custom-call | tf_op jit(solution)/shard_map/join/pallas_call | solution.py:238
  (25 shorter events, 0.2 us)
Async XLA Ops:
  2.5 6.3 %copy-start.9 = (bf16[1,192,720]{2,1,0:T(8,128)(2,1)S(1)}, bf16[1,192,720]{2,1,0:T(8,128)(2,1)}, u32[]{:S(2)}) copy-start(bf16[1,192,720]{2,1,0:T(8,128)(2,1)} %pack.1.refs_5_) | copy-start | bytes 829444
  2.5 37.3 %copy-start.6 = (f32[5,4,32]{2,1,0:T(4,128)S(1)}, f32[5,4,32]{2,1,0:T(4,128)}, u32[]{:S(2)}) copy-start(f32[5,4,32]{2,1,0:T(4,128)} %refs_4_.5) | copy-start | bytes 7684
  2.5 37.3 %copy-start.8 = (f32[32]{0:T(128)S(1)}, f32[32]{0:T(128)}, u32[]{:S(2)}) copy-start(f32[32]{0:T(128)} %param.11) | copy-start | bytes 388
  2.5 45.9 %copy-start = (bf16[2,720,720]{2,1,0:T(8,128)(2,1)S(1)}, bf16[2,720,720]{2,1,0:T(8,128)(2,1)}, u32[]{:S(2)}) copy-start(bf16[2,720,720]{2,1,0:T(8,128)(2,1)} %constant.29.clone.table_ref) | copy-start | bytes 6220804
  6.6 44.5 %collective-permute-start.1 = (bf16[2,192,720]{2,1,0:T(8,128)(2,1)}, bf16[2,192,720]{2,1,0:T(8,128)(2,1)}, u32[]{:S(2)}, u32[]{:S(2)}) collective-permute-start(bf16[2,192,720]{2,1,0:T(8,128)(2,1)} %get-tuple-element.24), channel_id=1, source_target_pairs={{0,64},{64,0},{1,65},{65,1},{2,66},{66,2},{3,67},{67,3},{4,68},{68... | collective-permute-start | bytes 1658888 | tf_op jit(solution)/shard_map/ppermute | solution.py:392
  8.7 49.4 %collective-permute-start.3 = (bf16[2,192,720]{2,1,0:T(8,128)(2,1)}, bf16[2,192,720]{2,1,0:T(8,128)(2,1)}, u32[]{:S(2)}, u32[]{:S(2)}) collective-permute-start(bf16[2,192,720]{2,1,0:T(8,128)(2,1)} %get-tuple-element.31), channel_id=1, source_target_pairs={{0,64},{64,0},{1,65},{65,1},{2,66},{66,2},{3,67},{67,3},{4,68},{68... | collective-permute-start | bytes 1658888 | tf_op jit(solution)/shard_map/ppermute | solution.py:392
  8.8 39.7 %collective-permute-start.2 = (bf16[1,192,720]{2,1,0:T(8,128)(2,1)S(1)}, bf16[1,192,720]{2,1,0:T(8,128)(2,1)S(1)}, u32[]{:S(2)}, u32[]{:S(2)}) collective-permute-start(bf16[1,192,720]{2,1,0:T(8,128)(2,1)S(1)} %copy-done.9), channel_id=1, source_target_pairs={{0,64},{64,0},{1,65},{65,1},{2,66},{66,2},{3,67},{67,3},{4,68},{68... | collective-permute-start | bytes 829448 | tf_op jit(solution)/shard_map/ppermute | solution.py:392
  10.1 29.7 %collective-permute-start = (f32[10,128]{1,0:T(8,128)}, f32[10,128]{1,0:T(8,128)S(1)}, u32[]{:S(2)}, u32[]{:S(2)}) collective-permute-start(f32[10,128]{1,0:T(8,128)} %get-tuple-element.22.refs_1_), channel_id=1, source_target_pairs={{0,64},{64,0},{1,65},{65,1},{2,66},{66,2},{3,67},{67,3},{4,68},{68... | collective-permute-start | bytes 15368 | tf_op jit(solution)/shard_map/ppermute | solution.py:392
  39.8 0.7 copy-start.7
  41.2 14.9 %all-to-all-start = ((f32[8,16,128]{2,1,0:T(8,128)}), f32[8,16,128]{2,1,0:T(8,128)}, u32[]{:S(2)}, u32[]{:S(2)}) async-start(f32[8,16,128]{2,1,0:T(8,128)} %shard_map.102._), calls=%async_computation | async-start | bytes 131072 | tf_op jit(solution)/shard_map/all_to_all | solution.py:375
  48.4 2.6 %copy-start.4 = (bf16[2,192,720]{2,1,0:T(8,128)(2,1)S(1)}, bf16[2,192,720]{2,1,0:T(8,128)(2,1)}, u32[]{:S(2)}) copy-start(bf16[2,192,720]{2,1,0:T(8,128)(2,1)} %get-tuple-element.23.own_ref) | copy-start | bytes 1658884
  48.5 1.0 %copy-start.5 = (bf16[1,192,720]{2,1,0:T(8,128)(2,1)S(1)}, bf16[1,192,720]{2,1,0:T(8,128)(2,1)}, u32[]{:S(2)}) copy-start(bf16[1,192,720]{2,1,0:T(8,128)(2,1)} %get-tuple-element.25.own_ref) | copy-start | bytes 829444
  51.0 10.2 %copy-start.2 = (f32[1,360,128]{2,1,0:T(8,128)}, f32[1,360,128]{2,1,0:T(8,128)S(1)}, u32[]{:S(2)}) copy-start(f32[1,360,128]{2,1,0:T(8,128)S(1)} %get-tuple-element.26._.refs_1_) | copy-start | bytes 552964
  51.0 7.1 %copy-start.1 = (bf16[2,192,720]{2,1,0:T(8,128)(2,1)S(1)}, bf16[2,192,720]{2,1,0:T(8,128)(2,1)}, u32[]{:S(2)}) copy-start(bf16[2,192,720]{2,1,0:T(8,128)(2,1)} %get-tuple-element.30.own_ref) | copy-start | bytes 1658884
  54.9 27.9 %collective-permute-start.6 = (bf16[2,360,128]{2,1,0:T(8,128)(2,1)}, bf16[2,360,128]{2,1,0:T(8,128)(2,1)}, u32[]{:S(2)}, u32[]{:S(2)}) collective-permute-start(bf16[2,360,128]{2,1,0:T(8,128)(2,1)} %get-tuple-element.34), channel_id=1, source_target_pairs={{0,64},{64,0},{1,65},{65,1},{2,66},{66,2},{3,67},{67,3},{4,68},{68... | collective-permute-start | bytes 552968 | tf_op jit(solution)/shard_map/ppermute | solution.py:392
  61.2 24.7 %collective-permute-start.4 = (bf16[2,360,128]{2,1,0:T(8,128)(2,1)}, bf16[2,360,128]{2,1,0:T(8,128)(2,1)}, u32[]{:S(2)}, u32[]{:S(2)}) collective-permute-start(bf16[2,360,128]{2,1,0:T(8,128)(2,1)} %waves.7), channel_id=1, source_target_pairs={{0,64},{64,0},{1,65},{65,1},{2,66},{66,2},{3,67},{67,3},{4,68},{68... | collective-permute-start | bytes 552968 | tf_op jit(solution)/shard_map/ppermute | solution.py:392
  61.4 19.7 %all-to-all-start.1 = ((f32[16,8,128]{2,1,0:T(8,128)}), f32[16,8,128]{2,1,0:T(8,128)}, u32[]{:S(2)}, u32[]{:S(2)}) async-start(f32[16,8,128]{2,1,0:T(8,128)} %get-tuple-element.29._), calls=%async_computation.1 | async-start | bytes 131072 | tf_op jit(solution)/shard_map/all_to_all | solution.py:375
  72.2 10.6 %collective-permute-start.5 = (bf16[1,360,128]{2,1,0:T(8,128)(2,1)}, bf16[1,360,128]{2,1,0:T(8,128)(2,1)}, u32[]{:S(2)}, u32[]{:S(2)}) collective-permute-start(bf16[1,360,128]{2,1,0:T(8,128)(2,1)} %get-tuple-element.33), channel_id=1, source_target_pairs={{0,64},{64,0},{1,65},{65,1},{2,66},{66,2},{3,67},{67,3},{4,68},{68... | collective-permute-start | bytes 276488 | tf_op jit(solution)/shard_map/ppermute | solution.py:392
  82.8 0.9 %copy-start.3 = (f32[1,360,128]{2,1,0:T(8,128)S(1)}, f32[1,360,128]{2,1,0:T(8,128)}, u32[]{:S(2)}) copy-start(f32[1,360,128]{2,1,0:T(8,128)} %copy-done.2) | copy-start | bytes 552964

commit v5 on v4

--- a/solution.py
+++ b/solution.py
@@ -15,7 +15,7 @@
 ORDERS = 720
 LAT_LEV = ("lat", "lev_0", "lev_1", "lev_2")
 INNER = ("lev_1", "lev_2")
-OUTER = ("lat", "lev_0")
+OUTER = "lev_0"
 EPSILON = 1e-06
 GROUPS = ((0,), (1, 2), (3, 4))
 F32 = jnp.float32
@@ -331,21 +331,37 @@
     )
 
 
-def finish_kernel(total, span, place_ref, mine_ref, s_ref, psi_ref, loss_ref):
-    _, samples, levels = psi_ref.shape
+def half_kernel(total, span, place_ref, mine_ref, s_ref, own_ref, half_ref):
     blocks = s_ref.shape[0]
-    here = place_ref[0] // 128 * (blocks // 2) + place_ref[0] % 64 // 8
+    here = place_ref[0] % 64 // 8
+    north = place_ref[0] // 128 == 1
     stats = None
     offset = jnp.zeros((1, s_ref.shape[2]), F32)
     for z in range(blocks):
         if z:
             offset = jnp.where(here == z, stats[0], offset)
-        stats = add_block(
-            stats, [s_ref[z, i : i + 1, :] for i in range(8)], weight_of(z * span, span, total)
-        )
+        weights = [weight_of((h * blocks + z) * span, span, total) for h in range(2)]
+        weight = jnp.where(north, weights[1], weights[0])
+        stats = add_block(stats, [s_ref[z, i : i + 1, :] for i in range(8)], weight)
+    own_ref[...] = mine_ref[...] + offset
+    for i, stat in enumerate(stats):
+        half_ref[i : i + 1, :] = stat
+
+
+def finish_kernel(total, place_ref, own_ref, near_ref, far_ref, psi_ref, loss_ref):
+    _, samples, levels = psi_ref.shape
+    north = place_ref[0] // 128 == 1
+    near = near_ref[...]
+    far = far_ref[...]
+    south_half = jnp.where(north, far, near)
+    north_half = jnp.where(north, near, far)
+    weight = weight_of(total // 2, total // 2, total)
+    stats = add_block(
+        [south_half[i : i + 1] for i in range(8)], [north_half[i : i + 1] for i in range(8)], weight
+    )
     peak = jnp.max(jnp.maximum(jnp.abs(stats[1]), jnp.abs(stats[2])), axis=1, keepdims=True)
     scale = peak + EPSILON
-    psi = (mine_ref[...] + offset) / scale
+    psi = (own_ref[...] + jnp.where(north, far[0:1], 0.0)) / scale
     for b in range(samples):
         psi_ref[:, b, :] = psi[:, b * levels : (b + 1) * levels]
     a, b, c = (jnp.sum(stats[i], axis=1, keepdims=True) for i in (4, 6, 7))
@@ -411,7 +427,6 @@
     )
     near_bands = all_of(rows, INNER)
     far0, near0 = waves(half, table, own[0], got[0], rows, True, False)
-    far1, near1 = waves(half, table, own[1], got[1], near0, True, False)
     span = bands * peers
     mine, stats = small(
         lambda *refs: band_kernel(total, bands, levels, *refs),
@@ -419,17 +434,26 @@
         place,
         near_bands,
         scratch=[pltpu.VMEM((2 * span, width), F32)],
-        after=near1,
     )
     all_stats = all_of(stats, OUTER)
-    (far2,) = waves(half, table, own[2], got[2], stats, True)
-    (near2,) = waves(half, table, own[2], got[2], stats, False)
+    mine, near_half = small(
+        lambda *refs: half_kernel(total, span, *refs),
+        (floats(bands, width), floats(8, width)),
+        place,
+        mine,
+        all_stats,
+    )
+    far_half = lax.ppermute(near_half, "lat", across)
+    far1, near1 = waves(half, table, own[1], got[1], near_half, True, False)
+    (far2,) = waves(half, table, own[2], got[2], near1, True)
+    (near2,) = waves(half, table, own[2], got[2], near1, False)
     psi, loss = small(
-        lambda *refs: finish_kernel(total, span, *refs),
+        lambda *refs: finish_kernel(total, *refs),
         (floats(bands, samples, levels), floats(1, width)),
         place,
         mine,
-        all_stats,
+        near_half,
+        far_half,
         after=near2,
     )
 

time: 89.3 us -> 88.9 us (level)
  blocking collectives: 0 us -> 26.7 us
  starting transfers between devices: 23.6 us -> 9.07 us
  Pallas kernels: 25.1 us -> 18 us
  waiting for transfers between devices: 35.7 us -> 31.2 us
    all_to_all x0 -> x2, blocking collectives: none -> 26.7 us  [all_of(): return lax.all_to_all(x, axes, split_axis=0, concat_axis=0, tiled=True)]
    all_to_all x2 -> x0, starting transfers between devices: 18 us -> none  [all_of(): return lax.all_to_all(x, axes, split_axis=0, concat_axis=0, tiled=True)]
    all_to_all x2 -> x0, waiting for transfers between devices: 6.1 us -> none  [all_of(): return lax.all_to_all(x, axes, split_axis=0, concat_axis=0, tiled=True)]
    pallas_call x3 -> x4, Pallas kernels: 4.31 us -> 1.41 us  [small(): pl.pallas_call(body, out_shape=out_shape, in_specs=specs, out_specs=(VMEM...]
    ppermute x0 -> x1, starting transfers between devices: none -> 2.44 us  [per_device(): far_half = lax.ppermute(near_half, 'lat', across)]
    pallas_call x4, Pallas kernels: 10.9 us -> 8.55 us  [waves(): pl.pallas_call(functools.partial(wave_kernel, flips=flips), out_shape=tup...]
    pallas_call x2, Pallas kernels: 4.05 us -> 2.18 us  [join(): pl.pallas_call(lambda *refs: join_kernel(rows[0], parts, *refs), out_shap...]
    ppermute x0 -> x1, waiting for transfers between devices: none -> 1.66 us  [per_device(): far_half = lax.ppermute(near_half, 'lat', across)]
  transfers between devices with their start and end apart: 9 -> 8, of which waited for: 2 -> 2; matrix products, arithmetic and copies ran while one was open for 0% -> 0% of each run, Pallas kernels for 20% -> 13%
where the time goes in v5:
time: 88.9 us; the launch traced here: 87.6 us
  waiting for transfers between devices  31.2 us (35%)
  blocking collectives  26.7 us (30%)
  Pallas kernels  18 us (20%)
  starting transfers between devices  9.07 us (10%)
  local copies, waits for them, and re-layouts  1.78 us (2%)
    ppermute x7, waiting for transfers between devices, swap(): return lax.ppermute(x, 'lon', across)  29.6 us
    all_to_all x2, blocking collectives, all_of(): return lax.all_to_all(x, axes, split_axis=0, concat_axis=0, tiled=True)  26.7 us
    pallas_call x4, Pallas kernels, waves(): pl.pallas_call(functools.partial(wave_kernel, flips=flips), out_shape=tup...  8.55 us
    ppermute x7, starting transfers between devices, swap(): return lax.ppermute(x, 'lon', across)  6.63 us
    pallas_call x1, Pallas kernels, send(): pl.pallas_call(lambda *refs: send_kernel(groups, *refs), out_shape=(*pack...  4 us
    ppermute x1, starting transfers between devices, per_device(): far_half = lax.ppermute(near_half, 'lat', across)  2.44 us
    pallas_call x2, Pallas kernels, join(): pl.pallas_call(lambda *refs: join_kernel(rows[0], parts, *refs), out_shap...  2.18 us
    pallas_call x1, Pallas kernels, pack(): pl.pallas_call(lambda *refs: pack_kernel(rows, flip, *refs), out_shape=ja...  1.84 us
  transfers between devices with their start and end apart: 8, of which 2 were waited for; matrix products, arithmetic and copies ran while one was open for 0% of the time, Pallas kernels for 13%

profile of v5, /device:TPU:1, one launch (start us, length us, event | category | flops | bytes accessed | tf_op | source)
XLA Modules:
  0.0 87.6 jit_solution(3258168579139813230)
XLA Ops:
  0.6 1.8 %pack.1.refs_5_ = bf16[1,192,720]{2,1,0:T(8,128)(2,1)} custom-call(s32[1]{0:T(128)} %bitcast.1.refs_0_.half_ref, bf16[5,4,32,720]{3,2,1,0:T(8,128)(2,1)} %refs_1_.3, bf16[5,4,32,720]{3,2,1,0:T(8,128)(2,1)} %refs_2_.3, bf16[5,4,32,720]{3,2,1,0:T(8,128)(2,1)} %refs_3_.3, s32[5,32,720]{2,1,0:T(8,128)} %refs_4_.4), custom_call_target="tpu_custom_call" | custom-call | tf_op jit(solution)/shard_map/pack/pallas_call | solution.py:75
  2.5 4.0 %send.1 = (bf16[2,192,720]{2,1,0:T(8,128)(2,1)}, bf16[2,192,720]{2,1,0:T(8,128)(2,1)}, bf16[1,192,720]{2,1,0:T(8,128)(2,1)}, bf16[2,192,720]{2,1,0:T(8,128)(2,1)...) custom-call(s32[1]{0:T(128)} %bitcast.1.refs_0_.half_ref, bf16[5,4,32,720]{3,2,1,0:T(8,128)(2,1)} %refs_1_.3, ...), custom_call_target="tpu_custom_call" | custom-call | tf_op jit(solution)/shard_map/send/pallas_call | solution.py:145
  6.5 2.1 %collective-permute-start.3 = (bf16[2,192,720]{2,1,0:T(8,128)(2,1)}, bf16[2,192,720]{2,1,0:T(8,128)(2,1)}, u32[]{:S(2)}, u32[]{:S(2)}) collective-permute-start(bf16[2,192,720]{2,1,0:T(8,128)(2,1)} %get-tuple-element.32), channel_id=1, source_target_pairs={{0,64},{64,0},{1,65},{65,1},{2,66},{66,2},{3,67},{67,3},{4,68},{68... | collective-permute-start | bytes 1658888 | tf_op jit(solution)/shard_map/ppermute | solution.py:408
  8.6 0.1 collective-permute-start.2
  8.7 1.4 %collective-permute-start.5 = (bf16[1,192,720]{2,1,0:T(8,128)(2,1)}, bf16[1,192,720]{2,1,0:T(8,128)(2,1)}, u32[]{:S(2)}, u32[]{:S(2)}) collective-permute-start(bf16[1,192,720]{2,1,0:T(8,128)(2,1)} %pack.1.refs_5_), channel_id=1, source_target_pairs={{0,64},{64,0},{1,65},{65,1},{2,66},{66,2},{3,67},{67,3},{4,68},{68... | collective-permute-start | bytes 829448 | tf_op jit(solution)/shard_map/ppermute | solution.py:408
  10.1 0.1 collective-permute-start
  10.2 29.6 %collective-permute-done.refs_2_ = f32[10,128]{1,0:T(8,128)S(1)} collective-permute-done((f32[10,128]{1,0:T(8,128)}, f32[10,128]{1,0:T(8,128)S(1)}, u32[]{:S(2)}, u32[]{:S(2)}) %collective-permute-start) | collective-permute-done | bytes 5152 | tf_op jit(solution)/shard_map/ppermute | solution.py:408
  39.8 0.7 copy-done.5
  40.6 11.9 %all_to_all.10.refs_1_ = f32[8,16,128]{2,1,0:T(8,128)S(1)} all-to-all(f32[8,16,128]{2,1,0:T(8,128)S(1)} %shard_map.102._), channel_id=1, replica_groups=mesh['lat'=2,'lon'=2,'lev_0'=8,'lev_1'=4,'lev_2'=2] {'lev_1','lev_2'}, dimensions={0} | all-to-all | bytes 131072 | tf_op jit(solution)/shard_map/all_to_all | solution.py:391
  52.5 0.5 shard_map.103
  53.0 14.9 %all_to_all.11.refs_2_ = f32[8,8,128]{2,1,0:T(8,128)S(1)} all-to-all(f32[8,8,128]{2,1,0:T(8,128)S(1)} %get-tuple-element.26), channel_id=1, replica_groups=mesh['lat'=2,'lon'=2,'lev_0'=8,'lev_1'=4,'lev_2'=2] {'lev_0'}, dimensions={0} | all-to-all | bytes 65536 | tf_op jit(solution)/shard_map/all_to_all | solution.py:391
  67.9 1.1 %copy-done.2 = bf16[2,192,720]{2,1,0:T(8,128)(2,1)S(1)} copy-done((bf16[2,192,720]{2,1,0:T(8,128)(2,1)S(1)}, bf16[2,192,720]{2,1,0:T(8,128)(2,1)}, u32[]{:S(2)}) %copy-start.2) | copy-done | bytes 552984
  68.9 3.6 %waves.4 = (bf16[2,360,128]{2,1,0:T(8,128)(2,1)S(1)}, f32[2,360,128]{2,1,0:T(8,128)S(1)}) custom-call(s32[1]{0:T(128)} %bitcast.1.refs_0_.half_ref, bf16[2,720,720]{2,1,0:T(8,128)(2,1)S(1)} %copy-done, bf16[2,192,720]{2,1,0:T(8,128)(2,1)S(1)} %copy-done.2, bf16[2,192,720]{2,1,0:T(8,128)(2,1)} %collective-permute-done.3.got_ref, ...), custom_call_target="tpu_custom_call" | custom-call | tf_op jit(solution)/shard_map/waves/pallas_call | solution.py:192
  72.5 1.3 %collective-permute-start.7 = (bf16[2,360,128]{2,1,0:T(8,128)(2,1)S(1)}, bf16[2,360,128]{2,1,0:T(8,128)(2,1)S(1)}, u32[]{:S(2)}, u32[]{:S(2)}) collective-permute-start(bf16[2,360,128]{2,1,0:T(8,128)(2,1)S(1)} %get-tuple-element.38), channel_id=1, source_target_pairs={{0,64},{64,0},{1,65},{65,1},{2,66},{66,2},{3,67},{67,3},{4,68},{68... | collective-permute-start | bytes 552968 | tf_op jit(solution)/shard_map/ppermute | solution.py:408
  73.8 1.3 %waves.6 = bf16[2,360,128]{2,1,0:T(8,128)(2,1)S(1)} custom-call(s32[1]{0:T(128)} %bitcast.1.refs_0_.half_ref, bf16[2,720,720]{2,1,0:T(8,128)(2,1)S(1)} %copy-done, bf16[2,192,720]{2,1,0:T(8,128)(2,1)S(1)} %copy-done.1, bf16[2,192,720]{2,1,0:T(8,128)(2,1)S(1)} %collective-permute-done.2.got_ref, f32[2,360,128]{2,1,0:T(8,128)S(1)} %get-tuple-element.33._.refs_2_), custom_call_target="tpu_custom_call" | custom-call | tf_op jit(solution)/shard_map/waves/pallas_call | solution.py:192
  75.2 0.3 collective-permute-start.4
  75.5 2.3 %waves.7 = (bf16[1,360,128]{2,1,0:T(8,128)(2,1)S(1)}, f32[1,360,128]{2,1,0:T(8,128)S(1)}) custom-call(s32[1]{0:T(128)} %bitcast.1.refs_0_.half_ref, bf16[2,720,720]{2,1,0:T(8,128)(2,1)S(1)} %copy-done, bf16[1,192,720]{2,1,0:T(8,128)(2,1)S(1)} %copy-done.3, bf16[1,192,720]{2,1,0:T(8,128)(2,1)} %collective-permute-done.5.got_ref, f32[8,16,128]{2,1,0:T(8,128)S(1)} %shard_map.102._), custom_call_target="tpu_custom_call" | custom-call | tf_op jit(solution)/shard_map/waves/pallas_call | solution.py:192
  77.8 1.3 %collective-permute-start.6 = (bf16[1,360,128]{2,1,0:T(8,128)(2,1)S(1)}, bf16[1,360,128]{2,1,0:T(8,128)(2,1)S(1)}, u32[]{:S(2)}, u32[]{:S(2)}) collective-permute-start(bf16[1,360,128]{2,1,0:T(8,128)(2,1)S(1)} %get-tuple-element.37), channel_id=1, source_target_pairs={{0,64},{64,0},{1,65},{65,1},{2,66},{66,2},{3,67},{67,3},{4,68},{68... | collective-permute-start | bytes 276488 | tf_op jit(solution)/shard_map/ppermute | solution.py:408
  79.1 2.4 %collective-permute-start.1 = (f32[8,128]{1,0:T(8,128)S(1)}, f32[8,128]{1,0:T(8,128)S(1)}, u32[]{:S(2)}, u32[]{:S(2)}) collective-permute-start(f32[8,128]{1,0:T(8,128)S(1)} %get-tuple-element.28._.refs_2_), channel_id=1, source_target_pairs={{0,128},{128,0},{1,129},{129,1},{2,130},{130,2},{3,131},{131,3},{4... | collective-permute-start | bytes 12296 | tf_op jit(solution)/shard_map/ppermute | solution.py:446
  81.6 1.3 %waves.5.refs_4_.refs_1_ = f32[2,360,128]{2,1,0:T(8,128)S(1)} custom-call(s32[1]{0:T(128)} %bitcast.1.refs_0_.half_ref, bf16[2,720,720]{2,1,0:T(8,128)(2,1)S(1)} %copy-done, bf16[2,192,720]{2,1,0:T(8,128)(2,1)S(1)} %copy-done.1, bf16[2,192,720]{2,1,0:T(8,128)(2,1)S(1)} %collective-permute-done.2.got_ref, f32[2,360,128]{2,1,0:T(8,128)S(1)} %get-tuple-element.33._.refs_2_), custom_call_target="tpu_custom_call" | custom-call | tf_op jit(solution)/shard_map/waves/pallas_call | solution.py:192
  82.9 1.7 %collective-permute-done.1.refs_3_ = f32[8,128]{1,0:T(8,128)S(1)} collective-permute-done((f32[8,128]{1,0:T(8,128)S(1)}, f32[8,128]{1,0:T(8,128)S(1)}, u32[]{:S(2)}, u32[]{:S(2)}) %collective-permute-start.1) | collective-permute-done | bytes 4128 | tf_op jit(solution)/shard_map/ppermute | solution.py:446
  84.6 0.8 shard_map.105
  85.4 1.2 %join.2 = (f32[5,360,128]{2,1,0:T(8,128)}, f32[5,360,128]{2,1,0:T(8,128)}) custom-call(s32[1]{0:T(128)} %bitcast.1.refs_0_.half_ref, f32[1,360,128]{2,1,0:T(8,128)S(1)} %get-tuple-element.36.refs_1_, f32[2,360,128]{2,1,0:T(8,128)S(1)} %get-tuple-element.33._.refs_2_, bf16[1,360,128]{2,1,0:T(8,128)(2,1)S(1)} %collective-permute-done.6.refs_3_, ...), custom_call_target="tpu_custom_call" | custom-call | tf_op jit(solution)/shard_map/join/pallas_call | solution.py:238
  86.6 1.0 %join.3 = (f32[5,360,128]{2,1,0:T(8,128)}, f32[5,360,128]{2,1,0:T(8,128)}) custom-call(s32[1]{0:T(128)} %bitcast.1.refs_0_.half_ref, f32[2,360,128]{2,1,0:T(8,128)S(1)} %waves.5.refs_4_.refs_1_, bf16[2,360,128]{2,1,0:T(8,128)(2,1)S(1)} %collective-permute-done.4.refs_2_, ...), custom_call_target="tpu_custom_call", output_to_operand_aliasing={{0}: (3, {}), {1}: (4, {})} | custom-call | tf_op jit(solution)/shard_map/join/pallas_call | solution.py:238
  (20 shorter events, 0.2 us)
Async XLA Ops:
  2.5 37.3 %copy-start.4 = (f32[5,4,32]{2,1,0:T(4,128)S(1)}, f32[5,4,32]{2,1,0:T(4,128)}, u32[]{:S(2)}) copy-start(f32[5,4,32]{2,1,0:T(4,128)} %refs_4_.5) | copy-start | bytes 7684
  2.5 37.3 %copy-start.6 = (f32[32]{0:T(128)S(1)}, f32[32]{0:T(128)}, u32[]{:S(2)}) copy-start(f32[32]{0:T(128)} %param.11) | copy-start | bytes 388
  2.5 65.4 %copy-start = (bf16[2,720,720]{2,1,0:T(8,128)(2,1)S(1)}, bf16[2,720,720]{2,1,0:T(8,128)(2,1)}, u32[]{:S(2)}) copy-start(bf16[2,720,720]{2,1,0:T(8,128)(2,1)} %constant.29.clone.table_ref) | copy-start | bytes 6220804
  6.5 67.3 %copy-start.1 = (bf16[2,192,720]{2,1,0:T(8,128)(2,1)S(1)}, bf16[2,192,720]{2,1,0:T(8,128)(2,1)}, u32[]{:S(2)}) copy-start(bf16[2,192,720]{2,1,0:T(8,128)(2,1)} %get-tuple-element.29.own_ref) | copy-start | bytes 1658884
  6.5 61.3 %collective-permute-start.3 = (bf16[2,192,720]{2,1,0:T(8,128)(2,1)}, bf16[2,192,720]{2,1,0:T(8,128)(2,1)}, u32[]{:S(2)}, u32[]{:S(2)}) collective-permute-start(bf16[2,192,720]{2,1,0:T(8,128)(2,1)} %get-tuple-element.32), channel_id=1, source_target_pairs={{0,64},{64,0},{1,65},{65,1},{2,66},{66,2},{3,67},{67,3},{4,68},{68... | collective-permute-start | bytes 1658888 | tf_op jit(solution)/shard_map/ppermute | solution.py:408
  8.6 65.2 %collective-permute-start.2 = (bf16[2,192,720]{2,1,0:T(8,128)(2,1)}, bf16[2,192,720]{2,1,0:T(8,128)(2,1)S(1)}, u32[]{:S(2)}, u32[]{:S(2)}) collective-permute-start(bf16[2,192,720]{2,1,0:T(8,128)(2,1)} %get-tuple-element.30), channel_id=1, source_target_pairs={{0,64},{64,0},{1,65},{65,1},{2,66},{66,2},{3,67},{67,3},{4,68},{68... | collective-permute-start | bytes 1658888 | tf_op jit(solution)/shard_map/ppermute | solution.py:408
  8.7 66.8 %collective-permute-start.5 = (bf16[1,192,720]{2,1,0:T(8,128)(2,1)}, bf16[1,192,720]{2,1,0:T(8,128)(2,1)}, u32[]{:S(2)}, u32[]{:S(2)}) collective-permute-start(bf16[1,192,720]{2,1,0:T(8,128)(2,1)} %pack.1.refs_5_), channel_id=1, source_target_pairs={{0,64},{64,0},{1,65},{65,1},{2,66},{66,2},{3,67},{67,3},{4,68},{68... | collective-permute-start | bytes 829448 | tf_op jit(solution)/shard_map/ppermute | solution.py:408
  10.1 29.7 %collective-permute-start = (f32[10,128]{1,0:T(8,128)}, f32[10,128]{1,0:T(8,128)S(1)}, u32[]{:S(2)}, u32[]{:S(2)}) collective-permute-start(f32[10,128]{1,0:T(8,128)} %get-tuple-element.24.refs_1_), channel_id=1, source_target_pairs={{0,64},{64,0},{1,65},{65,1},{2,66},{66,2},{3,67},{67,3},{4,68},{68... | collective-permute-start | bytes 15368 | tf_op jit(solution)/shard_map/ppermute | solution.py:408
  39.8 0.7 copy-start.5
  67.9 1.1 %copy-start.2 = (bf16[2,192,720]{2,1,0:T(8,128)(2,1)S(1)}, bf16[2,192,720]{2,1,0:T(8,128)(2,1)}, u32[]{:S(2)}) copy-start(bf16[2,192,720]{2,1,0:T(8,128)(2,1)} %get-tuple-element.31.own_ref) | copy-start | bytes 1658884
  72.5 3.0 %copy-start.3 = (bf16[1,192,720]{2,1,0:T(8,128)(2,1)S(1)}, bf16[1,192,720]{2,1,0:T(8,128)(2,1)}, u32[]{:S(2)}) copy-start(bf16[1,192,720]{2,1,0:T(8,128)(2,1)} %get-tuple-element.35.own_ref) | copy-start | bytes 829444
  72.5 12.9 %collective-permute-start.7 = (bf16[2,360,128]{2,1,0:T(8,128)(2,1)S(1)}, bf16[2,360,128]{2,1,0:T(8,128)(2,1)S(1)}, u32[]{:S(2)}, u32[]{:S(2)}) collective-permute-start(bf16[2,360,128]{2,1,0:T(8,128)(2,1)S(1)} %get-tuple-element.38), channel_id=1, source_target_pairs={{0,64},{64,0},{1,65},{65,1},{2,66},{66,2},{3,67},{67,3},{4,68},{68... | collective-permute-start | bytes 552968 | tf_op jit(solution)/shard_map/ppermute | solution.py:408
  75.2 11.4 %collective-permute-start.4 = (bf16[2,360,128]{2,1,0:T(8,128)(2,1)S(1)}, bf16[2,360,128]{2,1,0:T(8,128)(2,1)S(1)}, u32[]{:S(2)}, u32[]{:S(2)}) collective-permute-start(bf16[2,360,128]{2,1,0:T(8,128)(2,1)S(1)} %waves.6), channel_id=1, source_target_pairs={{0,64},{64,0},{1,65},{65,1},{2,66},{66,2},{3,67},{67,3},{4,68},{68... | collective-permute-start | bytes 552968 | tf_op jit(solution)/shard_map/ppermute | solution.py:408
  77.8 7.6 %collective-permute-start.6 = (bf16[1,360,128]{2,1,0:T(8,128)(2,1)S(1)}, bf16[1,360,128]{2,1,0:T(8,128)(2,1)S(1)}, u32[]{:S(2)}, u32[]{:S(2)}) collective-permute-start(bf16[1,360,128]{2,1,0:T(8,128)(2,1)S(1)} %get-tuple-element.37), channel_id=1, source_target_pairs={{0,64},{64,0},{1,65},{65,1},{2,66},{66,2},{3,67},{67,3},{4,68},{68... | collective-permute-start | bytes 276488 | tf_op jit(solution)/shard_map/ppermute | solution.py:408
  79.1 5.5 %collective-permute-start.1 = (f32[8,128]{1,0:T(8,128)S(1)}, f32[8,128]{1,0:T(8,128)S(1)}, u32[]{:S(2)}, u32[]{:S(2)}) collective-permute-start(f32[8,128]{1,0:T(8,128)S(1)} %get-tuple-element.28._.refs_2_), channel_id=1, source_target_pairs={{0,128},{128,0},{1,129},{129,1},{2,130},{130,2},{3,131},{131,3},{4... | collective-permute-start | bytes 12296 | tf_op jit(solution)/shard_map/ppermute | solution.py:446
